TPU v7x, 32 devices: a whole 2x2x4 slice. The times are simulated.
32 devices in a mesh: fsdp: 4 (over x, core), expert: 8 (over z, y).
Axes of the slice: x: 2, y: 2, z: 4, core: 2. Of those that a mesh axis runs over, the one named last changes fastest.
Arguments:
- hidden_in: bfloat16 [4096, 1536], P(('fsdp', 'expert')), may hold values from -6 to 6
- doc_ids: int32 [32, 128], P(('fsdp', 'expert')), may hold values from 0 to 1, never falling along the last dimension, each value on 1 to 80 neighbouring positions
- routes: int32 [4096, 8], P(('fsdp', 'expert')), may hold values from 0 to 39, all different within a row; in each aligned block of 128 rows (0 to 127, 128 to 255, ...) at most 48 rows name the same one
- gain_attn: float32 [1536], replicated, may hold values from 0.5 to 1.5
- w_query: bfloat16 [1536, 1536], P('fsdp'), may hold values from -0.15625 to 0.15625
- key_matrix: bfloat16 [1536, 512], P('fsdp'), may hold values from -0.15625 to 0.15625
- value_matrix: bfloat16 [1536, 512], P('fsdp'), may hold values from -0.15625 to 0.15625
- w_output: bfloat16 [1536, 1536], P('fsdp'), may hold values from -0.625 to 0.625
- gain_ffn: float32 [1536], replicated, may hold values from 0.5 to 1.5
- w_router: bfloat16 [1536, 40], P('fsdp'), may hold values from -0.046875 to 0.046875
- w_gateup: bfloat16 [80, 1536, 512], P('expert'), may hold values from -0.15625 to 0.15625
- w_down: bfloat16 [80, 256, 1536], P('expert'), may hold values from -2 to 2
- cotangent: bfloat16 [4096, 1536], P(('fsdp', 'expert')), may hold values from -6 to 6
Outputs:
- block_out: bfloat16 [4096, 1536], P(('fsdp', 'expert'))
- grad_input: float32 [4096, 1536], P(('fsdp', 'expert'))
- grad_query: float32 [1536, 1536], P('fsdp')
- grad_key: float32 [1536, 512], P('fsdp')
- grad_value: float32 [1536, 512], P('fsdp')
- grad_output: float32 [1536, 1536], P('fsdp')
- grad_router: float32 [1536, 40], P('fsdp')
- grad_gain_attn: float32 [1536], P('fsdp')
- grad_gain_ffn: float32 [1536], P('fsdp')
- grad_gateup: float32 [80, 1536, 512], P('expert', 'fsdp')
- grad_down: float32 [80, 256, 1536], P('expert', 'fsdp')
Inputs may be any that keep to these rules, and one draw needn't show every extreme that they name: `doc_ids`: along each device's row the document numbers never fall; each document has 1 to 80 tokens. `routes`: A token names 8 different experts; among the 128 tokens of one device no expert is named by more than 48 slots.
All inputs are finite; a program needn't handle non-finite values.
Results may differ from a plain program's by a relative error of at most 0.015.
Values may be sent and summed in bfloat16 or wider, within the bound.
A program may use at most 320 MiB of HBM per device.

v0:
```python
import math

import jax
import jax.numpy as jnp
from jax import lax
from jax.sharding import PartitionSpec as P

MODEL_WIDTH = 1536
QUERY_HEADS = 24
KEY_VALUE_HEADS = 8
HEAD_SIZE = 64
TOP = 8
CAP = 48


EPS = 1e-05
BASE = 10000.0
SCORE_SCALE = 0.015625
MASKED = -1e30


def rope_tables(doc_row):
    document_length = doc_row.shape[0]
    places = jnp.arange(document_length, dtype=jnp.int32)
    same_doc = doc_row[:, None] == doc_row[None, :]
    starts = jnp.min(jnp.where(same_doc, places[None, :], document_length), axis=1)
    position = (places - starts).astype(jnp.float32)
    half_width = HEAD_SIZE // 2
    inverse = jnp.exp(
        -math.log(BASE) * (2.0 * jnp.arange(half_width, dtype=jnp.float32) / HEAD_SIZE)
    )
    angle = position[:, None] * inverse[None, :]
    allowed = same_doc & (places[None, :] <= places[:, None])
    return (jnp.cos(angle), jnp.sin(angle), allowed)


def rotate(tensor, cosine_table, sine_table):
    half_width = HEAD_SIZE // 2
    first_half = tensor[..., :half_width]
    second = tensor[..., half_width:]
    cos_part = cosine_table[:, None, :]
    sin_part = sine_table[:, None, :]
    return jnp.concatenate(
        [first_half * cos_part - second * sin_part, second * cos_part + first_half * sin_part],
        axis=-1,
    )


def inverse_rotation(tensor, cosine_table, sine_table):
    half_width = HEAD_SIZE // 2
    first_half = tensor[..., :half_width]
    second = tensor[..., half_width:]
    cos_part = cosine_table[:, None, :]
    sin_part = sine_table[:, None, :]
    return jnp.concatenate(
        [first_half * cos_part + second * sin_part, second * cos_part - first_half * sin_part],
        axis=-1,
    )


def norm_forward(value_rows, gain):
    scale_inv = lax.rsqrt(jnp.mean(value_rows * value_rows, axis=-1, keepdims=True) + EPS)
    normed = value_rows * scale_inv
    return ((normed * gain).astype(jnp.bfloat16), normed, scale_inv)


def norm_backward(grad_out, normed, scale_inv, gain):
    grad_normed = grad_out * gain
    grad_gain = jnp.sum(grad_out * normed, axis=0)
    value_gradients = scale_inv * (
        grad_normed - normed * jnp.mean(grad_normed * normed, axis=-1, keepdims=True)
    )
    return (value_gradients, grad_gain)


def scores_of(query_rows, key_rows, allowed):
    document_length = query_rows.shape[0]
    group_rows = query_rows.reshape(
        document_length, KEY_VALUE_HEADS, QUERY_HEADS // KEY_VALUE_HEADS, HEAD_SIZE
    )
    scores = (
        jnp.einsum("qgrd,kgd->grqk", group_rows, key_rows, preferred_element_type=jnp.float32)
        * SCORE_SCALE
    )
    return jnp.where(allowed[None, None], scores, MASKED)


def forward_local(
    hidden_rows,
    doc_row,
    route_rows,
    gain_attn,
    w_query,
    key_matrix,
    value_matrix,
    w_output,
    gain_ffn,
    w_router,
):
    document_length = hidden_rows.shape[0]
    hidden_f = hidden_rows.astype(jnp.float32)
    attention_input, normed_attn, scale_attn = norm_forward(hidden_f, gain_attn)
    cosine_table, sine_table, allowed = rope_tables(doc_row)
    query_rows = jnp.dot(attention_input, w_query, preferred_element_type=jnp.float32).reshape(
        document_length, QUERY_HEADS, HEAD_SIZE
    )
    key_rows = jnp.dot(attention_input, key_matrix, preferred_element_type=jnp.float32).reshape(
        document_length, KEY_VALUE_HEADS, HEAD_SIZE
    )
    value_rows = (
        jnp.dot(attention_input, value_matrix, preferred_element_type=jnp.float32)
        .astype(jnp.bfloat16)
        .reshape(document_length, KEY_VALUE_HEADS, HEAD_SIZE)
    )
    query_rows = rotate(query_rows, cosine_table, sine_table).astype(jnp.bfloat16)
    key_rows = rotate(key_rows, cosine_table, sine_table).astype(jnp.bfloat16)
    scores = scores_of(query_rows, key_rows, allowed)
    top_score = jnp.max(scores, axis=-1, keepdims=True)
    log_total = top_score + jnp.log(jnp.sum(jnp.exp(scores - top_score), axis=-1, keepdims=True))
    weights = jnp.exp(scores - log_total).astype(jnp.bfloat16)
    attention_mixed = jnp.einsum(
        "grqk,kgd->qgrd", weights, value_rows, preferred_element_type=jnp.float32
    )
    attention_mixed = attention_mixed.reshape(document_length, QUERY_HEADS * HEAD_SIZE).astype(
        jnp.bfloat16
    )
    resid = hidden_f + jnp.dot(attention_mixed, w_output, preferred_element_type=jnp.float32)
    ffn_in, normed_ffn, scale_ffn = norm_forward(resid, gain_ffn)
    logits = jnp.dot(ffn_in, w_router, preferred_element_type=jnp.float32)
    probs = jax.nn.softmax(logits, axis=-1)
    picks = route_rows[:, :, None] == jnp.arange(probs.shape[1], dtype=jnp.int32)[None, None, :]
    gates = jnp.sum(jnp.where(picks, probs[:, None, :], 0.0), axis=-1)
    return (
        normed_attn,
        scale_attn,
        attention_input,
        cosine_table,
        sine_table,
        allowed,
        query_rows,
        key_rows,
        value_rows,
        attention_mixed,
        log_total,
        resid,
        ffn_in,
        normed_ffn,
        scale_ffn,
        probs,
        gates,
    )


def backward_local(
    state,
    route_rows,
    cot_rows,
    grad_ffn_in,
    grad_gates,
    gain_attn,
    w_query,
    key_matrix,
    value_matrix,
    w_output,
    gain_ffn,
    w_router,
):
    (
        normed_attn,
        scale_attn,
        attention_input,
        cosine_table,
        sine_table,
        allowed,
        query_rows,
        key_rows,
        value_rows,
        attention_mixed,
        log_total,
        resid,
        ffn_in,
        normed_ffn,
        scale_ffn,
        probs,
        gates,
    ) = state
    document_length = attention_input.shape[0]
    query_group = QUERY_HEADS // KEY_VALUE_HEADS
    picks = route_rows[:, :, None] == jnp.arange(probs.shape[1], dtype=jnp.int32)[None, None, :]
    grad_probs = jnp.sum(jnp.where(picks, grad_gates[:, :, None], 0.0), axis=1)
    grad_logits = (
        probs * (grad_probs - jnp.sum(probs * grad_probs, axis=-1, keepdims=True))
    ).astype(jnp.bfloat16)
    grad_router = jnp.dot(ffn_in.T, grad_logits, preferred_element_type=jnp.float32)
    grad_ffn_in = grad_ffn_in + jnp.dot(grad_logits, w_router.T, preferred_element_type=jnp.float32)
    grad_resid_part, grad_gain_ffn = norm_backward(grad_ffn_in, normed_ffn, scale_ffn, gain_ffn)
    grad_resid = cot_rows.astype(jnp.float32) + grad_resid_part
    grad_attn = grad_resid.astype(jnp.bfloat16)
    grad_output = jnp.dot(attention_mixed.T, grad_attn, preferred_element_type=jnp.float32)
    mixed_gradient = jnp.dot(grad_attn, w_output.T, preferred_element_type=jnp.float32).astype(
        jnp.bfloat16
    )
    scores = scores_of(query_rows, key_rows, allowed)
    weights = jnp.exp(scores - log_total)
    weights_low = weights.astype(jnp.bfloat16)
    gradient_by_group = mixed_gradient.reshape(
        document_length, KEY_VALUE_HEADS, query_group, HEAD_SIZE
    )
    mixed_by_group = attention_mixed.reshape(
        document_length, KEY_VALUE_HEADS, query_group, HEAD_SIZE
    )
    value_gradients = jnp.einsum(
        "grqk,qgrd->kgd", weights_low, gradient_by_group, preferred_element_type=jnp.float32
    )
    grad_weights = jnp.einsum(
        "qgrd,kgd->grqk", gradient_by_group, value_rows, preferred_element_type=jnp.float32
    )
    delta = jnp.transpose(
        jnp.sum(
            gradient_by_group.astype(jnp.float32) * mixed_by_group.astype(jnp.float32), axis=-1
        ),
        (1, 2, 0),
    )
    grad_scores = (weights * (grad_weights - delta[..., None]) * SCORE_SCALE).astype(jnp.bfloat16)
    query_by_group = query_rows.reshape(document_length, KEY_VALUE_HEADS, query_group, HEAD_SIZE)
    grad_query_rows = jnp.einsum(
        "grqk,kgd->qgrd", grad_scores, key_rows, preferred_element_type=jnp.float32
    ).reshape(document_length, QUERY_HEADS, HEAD_SIZE)
    key_row_gradient = jnp.einsum(
        "grqk,qgrd->kgd", grad_scores, query_by_group, preferred_element_type=jnp.float32
    )
    grad_query_rows = (
        inverse_rotation(grad_query_rows, cosine_table, sine_table)
        .reshape(document_length, QUERY_HEADS * HEAD_SIZE)
        .astype(jnp.bfloat16)
    )
    key_row_gradient = (
        inverse_rotation(key_row_gradient, cosine_table, sine_table)
        .reshape(document_length, KEY_VALUE_HEADS * HEAD_SIZE)
        .astype(jnp.bfloat16)
    )
    value_row_gradient = value_gradients.reshape(
        document_length, KEY_VALUE_HEADS * HEAD_SIZE
    ).astype(jnp.bfloat16)
    grad_query = jnp.dot(attention_input.T, grad_query_rows, preferred_element_type=jnp.float32)
    grad_key = jnp.dot(attention_input.T, key_row_gradient, preferred_element_type=jnp.float32)
    grad_value = jnp.dot(attention_input.T, value_row_gradient, preferred_element_type=jnp.float32)
    grad_attn_in = jnp.dot(grad_query_rows, w_query.T, preferred_element_type=jnp.float32)
    grad_attn_in = grad_attn_in + jnp.dot(
        key_row_gradient, key_matrix.T, preferred_element_type=jnp.float32
    )
    grad_attn_in = grad_attn_in + jnp.dot(
        value_row_gradient, value_matrix.T, preferred_element_type=jnp.float32
    )
    grad_hidden_part, grad_gain_attn = norm_backward(
        grad_attn_in, normed_attn, scale_attn, gain_attn
    )
    grad_in = grad_resid + grad_hidden_part
    return (
        grad_in,
        (grad_query, grad_key, grad_value, grad_output, grad_router, grad_gain_attn, grad_gain_ffn),
    )


def local(
    hidden_in,
    doc_ids,
    routes,
    gain_attn,
    w_query,
    key_matrix,
    value_matrix,
    w_output,
    gain_ffn,
    w_router,
    w_gateup,
    w_down,
    cotangent,
):
    full_query, full_key, full_value, full_output, full_router = (
        lax.all_gather(w_query, "fsdp", axis=0, tiled=True),
        lax.all_gather(key_matrix, "fsdp", axis=0, tiled=True),
        lax.all_gather(value_matrix, "fsdp", axis=0, tiled=True),
        lax.all_gather(w_output, "fsdp", axis=0, tiled=True),
        lax.all_gather(w_router, "fsdp", axis=0, tiled=True),
    )
    weights_attn = (gain_attn, full_query, full_key, full_value, full_output, gain_ffn, full_router)
    document_length = hidden_in.shape[0]
    experts = full_router.shape[1]
    owners = lax.axis_size("expert")
    held = w_gateup.shape[0]
    half_units = w_down.shape[1]
    hidden_units = w_gateup.shape[2]
    pairing = 2 if held % 2 == 0 else 1
    copies = 2 // pairing
    groups = held // pairing
    w_pairs = w_gateup.reshape(groups, pairing, MODEL_WIDTH, hidden_units)
    down_pairs = w_down.reshape(groups, pairing, half_units, MODEL_WIDTH)
    state = forward_local(hidden_in, doc_ids[0], routes, *weights_attn)
    resid = state[11]
    ffn_in = state[12]
    gates = state[16]
    slot_total = document_length * TOP
    slot_expert = routes.reshape(slot_total)
    onehot_slots = (slot_expert[:, None] == jnp.arange(experts, dtype=jnp.int32)[None, :]).astype(
        jnp.int32
    )
    ranks = jnp.sum((jnp.cumsum(onehot_slots, axis=0) - 1) * onehot_slots, axis=1)
    flat_pos = slot_expert * CAP + ranks
    slot_of = (
        jnp.full((experts * CAP,), slot_total, jnp.int32)
        .at[flat_pos]
        .set(jnp.arange(slot_total, dtype=jnp.int32))
    )
    token_of = slot_of // TOP
    padded_rows = jnp.concatenate([ffn_in, jnp.zeros((1, MODEL_WIDTH), jnp.bfloat16)], axis=0)
    expert_rows = padded_rows[token_of].reshape(experts, CAP, MODEL_WIDTH)
    sent_rows = jnp.repeat(expert_rows, copies, axis=0).reshape(owners, groups, CAP, MODEL_WIDTH)
    got_rows = lax.all_to_all(sent_rows, "expert", split_axis=0, concat_axis=0, tiled=True)
    gate_up = jnp.einsum("secd,emdf->semcf", got_rows, w_pairs, preferred_element_type=jnp.float32)
    gate_part = gate_up[..., :half_units]
    up_part = gate_up[..., half_units:]
    acted = (jax.nn.silu(gate_part) * up_part).astype(jnp.bfloat16)
    made_parts = jnp.einsum(
        "semcf,emfd->semcd", acted, down_pairs, preferred_element_type=jnp.float32
    ).astype(jnp.bfloat16)
    made = jnp.sum(made_parts.astype(jnp.float32), axis=2).astype(jnp.bfloat16)
    returned = lax.all_to_all(made, "expert", split_axis=0, concat_axis=0, tiled=True)
    joined_out = jnp.sum(
        returned.reshape(experts, copies, CAP, MODEL_WIDTH).astype(jnp.float32), axis=1
    )
    joined_out = lax.optimization_barrier(joined_out.astype(jnp.bfloat16)).astype(jnp.float32)
    slot_out = joined_out.reshape(experts * CAP, MODEL_WIDTH)[flat_pos].reshape(
        document_length, TOP, MODEL_WIDTH
    )
    combined = jnp.einsum("tk,tkd->td", gates, slot_out)
    block_out = (resid + combined).astype(jnp.bfloat16)
    cot_f = cotangent.astype(jnp.float32)
    grad_gates = jnp.einsum("td,tkd->tk", cot_f, slot_out)
    grad_slots = (
        (gates[:, :, None] * cot_f[:, None, :])
        .astype(jnp.bfloat16)
        .reshape(slot_total, MODEL_WIDTH)
    )
    padded_grads = jnp.concatenate([grad_slots, jnp.zeros((1, MODEL_WIDTH), jnp.bfloat16)], axis=0)
    expert_grads_rows = padded_grads[slot_of].reshape(experts, CAP, MODEL_WIDTH)
    sent_grads = jnp.repeat(expert_grads_rows, copies, axis=0).reshape(
        owners, groups, CAP, MODEL_WIDTH
    )
    owner_rows, owner_grads = (
        lax.all_to_all(sent_rows, "expert", split_axis=0, concat_axis=0, tiled=True),
        lax.all_to_all(sent_grads, "expert", split_axis=0, concat_axis=0, tiled=True),
    )
    gate_up_again = jnp.einsum(
        "secd,emdf->semcf", owner_rows, w_pairs, preferred_element_type=jnp.float32
    )
    gate_again = gate_up_again[..., :half_units]
    up_again = gate_up_again[..., half_units:]
    acted_again = (jax.nn.silu(gate_again) * up_again).astype(jnp.bfloat16)
    grad_acted = jnp.einsum(
        "secd,emfd->semcf", owner_grads, down_pairs, preferred_element_type=jnp.float32
    )
    grad_down_local = jnp.einsum(
        "semcf,secd->emfd", acted_again, owner_grads, preferred_element_type=jnp.float32
    ).reshape(held, half_units, MODEL_WIDTH)
    sigma = jax.nn.sigmoid(gate_again)
    grad_gate = grad_acted * up_again * sigma * (1.0 + gate_again * (1.0 - sigma))
    grad_up = grad_acted * gate_again * sigma
    grad_joined = jnp.concatenate([grad_gate, grad_up], axis=-1).astype(jnp.bfloat16)
    grad_gateup_local = jnp.einsum(
        "secd,semcf->emdf", owner_rows, grad_joined, preferred_element_type=jnp.float32
    ).reshape(held, MODEL_WIDTH, hidden_units)
    grad_parts = jnp.einsum(
        "semcf,emdf->semcd", grad_joined, w_pairs, preferred_element_type=jnp.float32
    ).astype(jnp.bfloat16)
    grad_rows = jnp.sum(grad_parts.astype(jnp.float32), axis=2).astype(jnp.bfloat16)
    grad_back = lax.all_to_all(grad_rows, "expert", split_axis=0, concat_axis=0, tiled=True)
    grad_joined_back = jnp.sum(
        grad_back.reshape(experts, copies, CAP, MODEL_WIDTH).astype(jnp.float32), axis=1
    )
    grad_joined_back = lax.optimization_barrier(grad_joined_back.astype(jnp.bfloat16)).astype(
        jnp.float32
    )
    grad_ffn = jnp.sum(
        grad_joined_back.reshape(experts * CAP, MODEL_WIDTH)[flat_pos].reshape(
            document_length, TOP, MODEL_WIDTH
        ),
        axis=1,
    )
    grad_gateup, grad_down = (
        lax.psum_scatter(grad_gateup_local, "fsdp", scatter_dimension=1, tiled=True),
        lax.psum_scatter(grad_down_local, "fsdp", scatter_dimension=1, tiled=True),
    )
    grad_input, grads = backward_local(
        state, routes, cotangent, grad_ffn, grad_gates, *weights_attn
    )
    (
        local_query,
        local_key,
        local_value,
        local_output,
        local_router,
        local_gain_attn,
        local_gain_ffn,
    ) = grads
    (
        share_query,
        share_key,
        share_value,
        share_output,
        share_router,
        share_gain_attn,
        share_gain_ffn,
    ) = (
        lax.psum_scatter(local_query, "fsdp", scatter_dimension=0, tiled=True),
        lax.psum_scatter(local_key, "fsdp", scatter_dimension=0, tiled=True),
        lax.psum_scatter(local_value, "fsdp", scatter_dimension=0, tiled=True),
        lax.psum_scatter(local_output, "fsdp", scatter_dimension=0, tiled=True),
        lax.psum_scatter(local_router, "fsdp", scatter_dimension=0, tiled=True),
        lax.psum_scatter(local_gain_attn, "fsdp", scatter_dimension=0, tiled=True),
        lax.psum_scatter(local_gain_ffn, "fsdp", scatter_dimension=0, tiled=True),
    )
    (
        total_query,
        total_key,
        total_value,
        total_output,
        total_router,
        total_gain_attn,
        total_gain_ffn,
    ) = lax.psum(
        (
            share_query,
            share_key,
            share_value,
            share_output,
            share_router,
            share_gain_attn,
            share_gain_ffn,
        ),
        "expert",
    )
    return (
        block_out,
        grad_input,
        total_query,
        total_key,
        total_value,
        total_output,
        total_router,
        total_gain_attn,
        total_gain_ffn,
        grad_gateup,
        grad_down,
    )


def solution(mesh):
    in_specs = (
        P(("fsdp", "expert"), None),
        P(("fsdp", "expert"), None),
        P(("fsdp", "expert"), None),
        P(),
        P("fsdp", None),
        P("fsdp", None),
        P("fsdp", None),
        P("fsdp", None),
        P(),
        P("fsdp", None),
        P("expert", None, None),
        P("expert", None, None),
        P(("fsdp", "expert"), None),
    )
    out_specs = (
        P(("fsdp", "expert"), None),
        P(("fsdp", "expert"), None),
        P("fsdp", None),
        P("fsdp", None),
        P("fsdp", None),
        P("fsdp", None),
        P("fsdp", None),
        P("fsdp"),
        P("fsdp"),
        P("expert", "fsdp", None),
        P("expert", "fsdp", None),
    )
    return jax.shard_map(local, mesh=mesh, in_specs=in_specs, out_specs=out_specs, check_vma=False)
```

profile of v0, /device:TPU:0, one launch (start us, length us, event | category | flops | bytes accessed | tf_op | source)
XLA Modules:
  0.0 1629.3 jit_solution(8194340336029407756)
XLA Ops:
  11.9 11.3 reduce-window.6
  23.7 4.3 scatter_custom_fusion
  29.3 2.7 all-gather.5.cloned.1.call-done
  32.0 1.8 convolution_convert_fusion.4
  33.9 19.3 %all-gather.7.cloned.1.call-done = bf16[1536,512]{1,0:T(8,128)(2,1)} async-done(((bf16[384,512]{1,0:T(8,128)(2,1)}), bf16[1536,512]{1,0:T(8,128)(2,1)}) %all-gather.7.cloned.1.call-update) | async-done | bytes 1572880 | tf_op jit(solution)/shard_map/all_gather | solution.py:282
  53.3 2.2 fusion.74
  55.5 36.8 %all-gather.9.cloned.1.call-done = bf16[1536,1536]{1,0:T(8,128)(2,1)} async-done(((bf16[384,1536]{1,0:T(8,128)(2,1)}), bf16[1536,1536]{1,0:T(8,128)(2,1)}) %all-gather.9.cloned.1.call-update) | async-done | bytes 4718608 | tf_op jit(solution)/shard_map/all_gather | solution.py:281
  92.3 4.3 fusion.72
  98.8 32.3 %all-gather.11.cloned.1.call-done = bf16[1536,1536]{1,0:T(8,128)(2,1)} async-done(((bf16[384,1536]{1,0:T(8,128)(2,1)}), bf16[1536,1536]{1,0:T(8,128)(2,1)}) %all-gather.11.cloned.1.call-update) | async-done | bytes 4718608 | tf_op jit(solution)/shard_map/all_gather | solution.py:284
  131.2 3.2 multiply_reduce_fusion.3
  135.5 7.7 gather_fusion
  143.2 136.5 %all_to_all.21 = bf16[8,5,48,1536]{3,2,1,0:T(8,128)(2,1)} all-to-all(bf16[8,5,48,1536]{3,2,1,0:T(8,128)(2,1)} %bitcast.198), channel_id=1, replica_groups=mesh['fsdp'=4,'expert'=8] {'expert'}, dimensions={0} | all-to-all | bytes 11796480 | tf_op jit(solution)/shard_map/all_to_all | solution.py:319
  279.7 11.4 fusion.25
  291.1 1.2 multiply_convert_fusion
  292.3 2.0 copy-done.8
  294.3 10.5 fusion.17
  304.8 5.6 copy.155
  310.5 4.8 all-to-all-start.1
  315.3 1.0 convert_element_type.131
  316.3 5.4 all_gather.19
  323.2 120.9 %all-to-all-done.1 = bf16[8,5,48,1536]{3,2,1,0:T(8,128)(2,1)} async-done(((bf16[8,5,48,1536]{3,2,1,0:T(8,128)(2,1)}), bf16[8,5,48,1536]{3,2,1,0:T(8,128)(2,1)}, u32[]{:S(2)}, u32[]{:S(2)}) %all-to-all-start.1) | async-done | bytes 5898272 | tf_op jit(solution)/shard_map/all_to_all | solution.py:328
  444.2 10.2 gather_fusion.1
  454.4 2.4 fusion.21
  456.8 0.9 copy.183
  458.7 1.6 fusion
  460.9 7.7 gather_fusion.2
  468.7 134.1 %all_to_all.22 = bf16[8,5,48,1536]{3,2,1,0:T(8,128)(2,1)} all-to-all(bf16[8,5,48,1536]{3,2,1,0:T(8,128)(2,1)} %bitcast.199), channel_id=1, replica_groups=mesh['fsdp'=4,'expert'=8] {'expert'}, dimensions={0} | all-to-all | bytes 11796480 | tf_op jit(solution)/shard_map/all_to_all | solution.py:352
  602.8 12.5 fusion.13
  615.3 14.0 fusion.18
  629.2 5.6 copy.159
  634.9 5.0 all-to-all-start.3
  640.4 1.8 fusion.23
  642.2 125.5 %all-to-all-done.3 = bf16[8,5,48,1536]{3,2,1,0:T(8,128)(2,1)} async-done(((bf16[8,5,48,1536]{3,2,1,0:T(8,128)(2,1)}), bf16[8,5,48,1536]{3,2,1,0:T(8,128)(2,1)}, u32[]{:S(2)}, u32[]{:S(2)}) %all-to-all-start.3) | async-done | bytes 5898272 | tf_op jit(solution)/shard_map/all_to_all | solution.py:377
  767.7 8.7 bitcast_convert_fusion
  776.4 12.0 gather_fusion.3
  788.4 4.6 bitcast_reduce_fusion
  793.1 1.0 multiply_reduce_fusion
  794.1 1.1 multiply_add_fusion
  795.1 4.1 convolution_convert_fusion.2
  799.5 1.2 fusion.37
  801.4 2.3 fusion.66
  803.9 1.4 fusion.31
  806.2 1.5 convolution_bitcast_fusion.1
  807.9 2.5 fusion.68
  810.4 5.0 fusion.49
  815.6 1.0 copy-done.12
  817.1 5.2 fusion.70
  824.2 13.0 fusion.1
  837.3 2.6 reduce-scatter.12.cloned.1.call-done
  839.9 40.9 %reduce-scatter.10.cloned.1.call-done = f32[384,512]{1,0:T(8,128)} async-done(((f32[1536,512]{1,0:T(8,128)}), f32[384,512]{1,0:T(8,128)}) %reduce-scatter.10.cloned.1.call-update) | async-done | bytes 786448 | tf_op jit(solution)/shard_map/reduce_scatter | solution.py:416
  880.7 80.6 %reduce-scatter.14.cloned.1.call-done = f32[384,1536]{1,0:T(8,128)} async-done(((f32[1536,1536]{1,0:T(8,128)}), f32[384,1536]{1,0:T(8,128)}) %reduce-scatter.14.cloned.1.call-update) | async-done | bytes 2359312 | tf_op jit(solution)/shard_map/reduce_scatter | solution.py:418
  961.3 80.6 %reduce-scatter.8.cloned.1.call-done = f32[384,1536]{1,0:T(8,128)} async-done(((f32[1536,1536]{1,0:T(8,128)}), f32[384,1536]{1,0:T(8,128)}) %reduce-scatter.8.cloned.1.call-update) | async-done | bytes 2359312 | tf_op jit(solution)/shard_map/reduce_scatter | solution.py:415
  1041.9 17.7 %fusion.3 = f32[5,2,512,1536,1]{3,2,1,4,0:T(8,128)} fusion(bf16[8,5,2,48,256]{4,3,2,0,1:T(8,128)(2,1)} %get-tuple-element.27, bf16[8,5,2,48,256]{4,3,2,0,1:T(8,128)(2,1)} %copy-done.64, bf16[8,5,48,1536]{3,2,1,0:T(8,128)(2,1)} %all_to_all.21), kind=kOutput, calls=%fused_computation.12 | convolution fusion | flops 6047662080 | bytes 41287680 | tf_op jit(solution)/shard_map/secd,semcf->emdf/dot_general | solution.py:370
  1059.7 32.3 %copy.166 = f32[10,1536,512]{2,1,0:T(8,128)} copy(f32[10,1536,512]{1,2,0:T(8,128)} %bitcast.197) | data formatting | bytes 62914560 | tf_op jit(solution)/shard_map/reshape | solution.py:372
  1093.9 4.3 fusion.79
  1099.7 11.8 all-reduce.6
  1111.6 38.5 %all-reduce.4 = (f32[384,40]{0,1:T(8,128)}, f32[384]{0:T(512)}, f32[384]{0:T(512)}) all-reduce(f32[384,40]{0,1:T(8,128)} %reduce-scatter.16.cloned.1.call-done, f32[384]{0:T(512)S(1)} %dynamic-slice.1, f32[384]{0:T(512)S(1)} %dynamic-slice.3), channel_id=1, replica_groups=mesh['fsdp'=4,'expert'=8] {'expert'}, use_global_device_ids=true, to_apply=%region_29.30 | all-reduce | flops 16128 | bytes 129024 | tf_op jit(solution)/shard_map/psum | solution.py:431
  1150.1 1.2 fusion.42
  1151.3 33.5 %reduce-scatter.20.cloned.1.call-done = f32[10,64,1536]{2,1,0:T(8,128)} async-done(((f32[10,256,1536]{2,1,0:T(8,128)}), f32[10,64,1536]{2,1,0:T(8,128)}) %reduce-scatter.20.cloned.1.call-update) | async-done | bytes 3932176 | tf_op jit(solution)/shard_map/reduce_scatter | solution.py:392
  1184.8 214.9 %all-reduce.9.cloned.1.call-done = (f32[384,1536]{1,0:T(8,128)}, f32[384,512]{1,0:T(8,128)}, f32[384,512]{1,0:T(8,128)}, f32[384,1536]{1,0:T(8,128)}) async-done(((f32[384,1536]{1,0:T(8,128)}, f32[384,512]{1,0:T(8,128)}, f32[384,512]{1,0:T(8,128)}, f32[384,1536]{1,0:T(8,128)}), (f32[384,1536]{1,0:T(8,128)}, f32[384,512]{1,0:T(8,128)}, f32[384,512]{1,0:T(8,128)}, ...) | async-done | bytes 6291472 | tf_op jit(solution)/shard_map/psum | solution.py:431
  1399.7 215.8 %reduce-scatter.18.cloned.1.call-done = f32[10,384,512]{2,1,0:T(8,128)} async-done(((f32[10,1536,512]{2,1,0:T(8,128)}), f32[10,384,512]{2,1,0:T(8,128)}) %reduce-scatter.18.cloned.1.call-update) | async-done | bytes 7864336 | tf_op jit(solution)/shard_map/reduce_scatter | solution.py:391
  1615.5 3.4 copy.232
  1619.8 0.9 copy.234
  1620.7 1.4 copy.235
  (215 shorter events, 21.6 us)
Async XLA Ops:
  7.2 21.5 %copy-start.62 = (s32[1,128]{1,0:T(1,128)S(1)}, s32[1,128]{1,0:T(1,128)}, u32[]{:S(2)}) copy-start(s32[1,128]{1,0:T(1,128)} %param.14) | copy-start | bytes 1540
  7.2 21.6 %copy-start = (bf16[128,1536]{1,0:T(8,128)(2,1)S(1)}, bf16[128,1536]{1,0:T(8,128)(2,1)}, u32[]{:S(2)}) copy-start(bf16[128,1536]{1,0:T(8,128)(2,1)} %param.13) | copy-start | bytes 1179652
  7.2 24.8 %copy-start.31 = (f32[1536]{0:T(1024)S(1)}, f32[1536]{0:T(1024)}, u32[]{:S(2)}) copy-start(f32[1536]{0:T(1024)} %param.16) | copy-start | bytes 18436
  7.2 24.8 %all-gather.5.cloned.1.call-start = ((), (), s32[]{:S(2)}) async-start(), calls=%async_computation.11 | async-start | bytes 1966080 | tf_op jit(solution)/shard_map/all_gather | solution.py:283
  7.9 45.3 %all-gather.7.cloned.1.call-start = ((), (), s32[]{:S(2)}) async-start(), calls=%async_computation.12 | async-start | bytes 1966080 | tf_op jit(solution)/shard_map/all_gather | solution.py:282
  8.7 83.6 %all-gather.9.cloned.1.call-start = ((), (), s32[]{:S(2)}) async-start(), calls=%async_computation.13 | async-start | bytes 5898240 | tf_op jit(solution)/shard_map/all_gather | solution.py:281
  9.4 121.8 %all-gather.11.cloned.1.call-start = ((), (), s32[]{:S(2)}) async-start(), calls=%async_computation.14 | async-start | bytes 5898240 | tf_op jit(solution)/shard_map/all_gather | solution.py:284
  23.7 4.3 copy-start.54
  29.0 67.6 %copy-start.50 = (f32[128]{0:T(128)}, f32[128]{0:T(128)S(1)}, u32[]{:S(2)}) copy-start(f32[128]{0:T(128)S(1)} %add_rsqrt_fusion.1) | copy-start | bytes 1540
  29.2 67.4 %copy-start.34 = (f32[128,32]{0,1:T(8,128)}, f32[128,32]{0,1:T(8,128)S(1)}, u32[]{:S(2)}) copy-start(f32[128,32]{0,1:T(8,128)S(1)} %get-tuple-element.40) | copy-start | bytes 49156
  29.2 67.4 %copy-start.37 = (f32[128,32]{0,1:T(8,128)}, f32[128,32]{0,1:T(8,128)S(1)}, u32[]{:S(2)}) copy-start(f32[128,32]{0,1:T(8,128)S(1)} %get-tuple-element.41) | copy-start | bytes 49156
  33.9 63.7 %copy-start.24 = (bf16[128,512]{0,1:T(8,128)(2,1)}, bf16[128,512]{0,1:T(8,128)(2,1)S(1)}, u32[]{:S(2)}) copy-start(bf16[128,512]{0,1:T(8,128)(2,1)S(1)} %copy.144) | copy-start | bytes 393220
  55.5 41.7 %copy-start.41 = (bf16[128,8,32]{0,2,1:T(8,128)(2,1)}, bf16[128,8,32]{0,2,1:T(8,128)(2,1)S(1)}, u32[]{:S(2)}) copy-start(bf16[128,8,32]{0,2,1:T(8,128)(2,1)S(1)} %get-tuple-element.36) | copy-start | bytes 196612
  55.5 41.7 %copy-start.43 = (bf16[128,8,32]{0,2,1:T(8,128)(2,1)}, bf16[128,8,32]{0,2,1:T(8,128)(2,1)S(1)}, u32[]{:S(2)}) copy-start(bf16[128,8,32]{0,2,1:T(8,128)(2,1)S(1)} %get-tuple-element.37) | copy-start | bytes 196612
  98.4 36.9 %copy-start.47 = (f32[1536]{0:T(1024)S(1)}, f32[1536]{0:T(1024)}, u32[]{:S(2)}) copy-start(f32[1536]{0:T(1024)} %param.21) | copy-start | bytes 18436
  98.8 35.6 %copy-start.9 = (bf16[8,64,3,128]{3,1,2,0:T(8,128)(2,1)}, bf16[8,64,3,128]{3,1,2,0:T(8,128)(2,1)S(1)}, u32[]{:S(2)}) copy-start(bf16[8,64,3,128]{3,1,2,0:T(8,128)(2,1)S(1)} %convolution_convert_fusion.3) | copy-start | bytes 1179652
  134.4 8.7 copy-start.60
  135.4 186.9 %copy-start.14 = (bf16[128,1536]{1,0:T(8,128)(2,1)}, bf16[128,1536]{1,0:T(8,128)(2,1)S(1)}, u32[]{:S(2)}) copy-start(bf16[128,1536]{1,0:T(8,128)(2,1)S(1)} %multiply_convert_fusion.1) | copy-start | bytes 1179652
  291.1 3.2 copy-start.8
  294.3 10.5 copy-start.18
  310.5 4.8 copy-start.20
  310.5 5.8 copy-start.53
  310.5 11.2 copy-start.55
  310.5 133.7 %all-to-all-start.1 = ((bf16[8,5,48,1536]{3,2,1,0:T(8,128)(2,1)}), bf16[8,5,48,1536]{3,2,1,0:T(8,128)(2,1)}, u32[]{:S(2)}, u32[]{:S(2)}) async-start(bf16[8,5,48,1536]{3,2,1,0:T(8,128)(2,1)} %copy.155), calls=%async_computation.1 | async-start | bytes 11796480 | tf_op jit(solution)/shard_map/all_to_all | solution.py:328
  321.7 122.5 %copy-start.25 = (bf16[1536,40]{0,1:T(8,128)(2,1)}, bf16[1536,40]{0,1:T(8,128)(2,1)S(1)}, u32[]{:S(2)}) copy-start(bf16[1536,40]{0,1:T(8,128)(2,1)S(1)} %all_gather.19) | copy-start | bytes 368644
  322.6 121.6 %copy-start.32 = (f32[128,40]{0,1:T(8,128)}, f32[128,40]{0,1:T(8,128)S(1)}, u32[]{:S(2)}) copy-start(f32[128,40]{0,1:T(8,128)S(1)} %get-tuple-element.47) | copy-start | bytes 61444
  322.6 121.6 %copy-start.56 = (f32[128]{0:T(128)}, f32[128]{0:T(128)S(1)}, u32[]{:S(2)}) copy-start(f32[128]{0:T(128)S(1)} %get-tuple-element.46) | copy-start | bytes 1540
  322.6 121.6 %copy-start.58 = (f32[128]{0:T(128)}, f32[128]{0:T(128)S(1)}, u32[]{:S(2)}) copy-start(f32[128]{0:T(128)S(1)} %fusion.58) | copy-start | bytes 1540
  454.4 4.3 copy-start.6
  615.3 14.0 copy-start.64
  634.9 5.4 copy-start.33
  634.9 5.4 copy-start.57
  634.9 5.4 copy-start.59
  634.9 5.5 copy-start.7
  634.9 132.8 %all-to-all-start.3 = ((bf16[8,5,48,1536]{3,2,1,0:T(8,128)(2,1)}), bf16[8,5,48,1536]{3,2,1,0:T(8,128)(2,1)}, u32[]{:S(2)}, u32[]{:S(2)}) async-start(bf16[8,5,48,1536]{3,2,1,0:T(8,128)(2,1)} %copy.159), calls=%async_computation.3 | async-start | bytes 11796480 | tf_op jit(solution)/shard_map/all_to_all | solution.py:377
  639.9 200.0 %reduce-scatter.12.cloned.1.call-start = ((), (), s32[]{:S(2)}) async-start(), calls=%async_computation.17 | async-start | bytes 3932160 | tf_op jit(solution)/shard_map/reduce_scatter | solution.py:417
  640.4 152.6 %copy-start.45 = (bf16[128,40]{0,1:T(8,128)(2,1)}, bf16[128,40]{0,1:T(8,128)(2,1)S(1)}, u32[]{:S(2)}) copy-start(bf16[128,40]{0,1:T(8,128)(2,1)S(1)} %multiply_convert_fusion.2) | copy-start | bytes 30724
  767.7 8.7 copy-start.48
  788.4 4.6 copy-start.5
  788.4 4.6 copy-start.26
  788.4 4.7 copy-start.61
  788.4 5.7 copy-start.16
  788.4 5.7 copy-start.21
  795.1 4.4 copy-start.3
  795.1 6.2 copy-start.1
  795.1 6.2 copy-start.51
  800.7 3.0 copy-start.10
  803.7 77.0 %reduce-scatter.10.cloned.1.call-start = ((), (), s32[]{:S(2)}) async-start(), calls=%async_computation.16 | async-start | bytes 3932160 | tf_op jit(solution)/shard_map/reduce_scatter | solution.py:416
  803.8 4.0 copy-start.35
  803.8 4.0 copy-start.38
  810.4 150.9 %reduce-scatter.14.cloned.1.call-start = ((), (), s32[]{:S(2)}) async-start(), calls=%async_computation.18 | async-start | bytes 11796480 | tf_op jit(solution)/shard_map/reduce_scatter | solution.py:418
  815.5 1.4 copy-start.39
  815.5 226.4 %reduce-scatter.8.cloned.1.call-start = ((), (), s32[]{:S(2)}) async-start(), calls=%async_computation.15 | async-start | bytes 11796480 | tf_op jit(solution)/shard_map/reduce_scatter | solution.py:415
  822.2 289.4 %reduce-scatter.16.cloned.1.call-start = ((), (), s32[]{:S(2)}) async-start(), calls=%async_computation.19 | async-start | bytes 307200 | tf_op jit(solution)/shard_map/reduce_scatter | solution.py:419
  824.1 360.7 %reduce-scatter.20.cloned.1.call-start = ((), (), s32[]{:S(2)}) async-start(), calls=%async_computation.21 | async-start | bytes 19660800 | tf_op jit(solution)/shard_map/reduce_scatter | solution.py:392
  837.2 562.5 %all-reduce.9.cloned.1.call-start = ((), (), s32[]{:S(2)}) async-start(), calls=%async_computation.22 | async-start | bytes 12582912 | tf_op jit(solution)/shard_map/psum | solution.py:431
  1041.9 573.6 %reduce-scatter.18.cloned.1.call-start = ((), (), s32[]{:S(2)}) async-start(), calls=%async_computation.20 | async-start | bytes 39321600 | tf_op jit(solution)/shard_map/reduce_scatter | solution.py:391
  1092.0 6.2 copy-start.13
  1093.9 5.0 copy-start.19
  1093.9 5.0 copy-start.23
  1098.2 1.5 copy-start.49
  1399.7 219.2 %copy-start.28 = (f32[384,512]{1,0:T(8,128)S(1)}, f32[384,512]{1,0:T(8,128)}, u32[]{:S(2)}) copy-start(f32[384,512]{1,0:T(8,128)} %get-tuple-element.55) | copy-start | bytes 2359300
  1399.7 220.1 %copy-start.27 = (f32[384,512]{1,0:T(8,128)S(1)}, f32[384,512]{1,0:T(8,128)}, u32[]{:S(2)}) copy-start(f32[384,512]{1,0:T(8,128)} %get-tuple-element.56) | copy-start | bytes 2359300
  1615.5 5.1 copy-start.17
  (15 other events, 14.2 us)
Sparse Core Ops, SparseCore 0:
  9.6 22.3 all-gather.4
  33.5 19.7 all-gather.6
  54.8 37.4 all-gather.8
  93.7 37.4 all-gather.10
  803.8 35.9 reduce-scatter.11
  842.8 37.8 reduce-scatter.9
  883.3 77.9 reduce-scatter.13
  963.9 77.9 reduce-scatter.7
  1044.9 19.9 reduce-scatter.15
  1068.0 116.8 reduce-scatter.19
  1189.3 210.3 all-reduce.8
  1402.7 212.7 reduce-scatter.17
where the time goes:
time: 1640 us; the launch traced here: 1630 us
  waiting for transfers between devices  1010 us (62%)
  blocking collectives  326 us (20%)
  matrix products  127 us (8%)
  local copies, waits for them, and re-layouts  104 us (6%)
  other arithmetic  35.6 us (2%)
    reduce_scatter x1, waiting for transfers between devices, local(): lax.psum_scatter(grad_gateup_local, 'fsdp', scatter_dimension=1, tiled=True)  216 us
    psum x1, waiting for transfers between devices, local(): lax.psum((share_query, share_key, share_value, share_output, share_router...  215 us
    all_to_all x1, blocking collectives, local(): lax.all_to_all(sent_rows, 'expert', split_axis=0, concat_axis=0, tiled=True)  137 us
    all_to_all x1, blocking collectives, local(): lax.all_to_all(sent_grads, 'expert', split_axis=0, concat_axis=0, tiled=T...  134 us
    all_to_all x1, waiting for transfers between devices, local(): lax.all_to_all(grad_rows, 'expert', split_axis=0, concat_axis=0, tiled=True)  125 us
    all_to_all x1, waiting for transfers between devices, local(): lax.all_to_all(made, 'expert', split_axis=0, concat_axis=0, tiled=True)  121 us
    reduce_scatter x1, waiting for transfers between devices, local(): lax.psum_scatter(local_output, 'fsdp', scatter_dimension=0, tiled=True)  80.6 us
    reduce_scatter x1, waiting for transfers between devices, local(): lax.psum_scatter(local_query, 'fsdp', scatter_dimension=0, tiled=True)  80.6 us
  transfers between devices with their start and end apart: 14, of which 13 were waited for; matrix products, arithmetic and copies ran while one was open for 7% of the time, Pallas kernels for 0%

commit v1 on v0

--- a/solution.py
+++ b/solution.py
@@ -1,8 +1,11 @@
+import functools
 import math
 
 import jax
 import jax.numpy as jnp
 from jax import lax
+from jax.experimental import pallas as pl
+from jax.experimental.pallas import tpu as pltpu
 from jax.sharding import PartitionSpec as P
 
 MODEL_WIDTH = 1536
@@ -186,8 +189,7 @@
     ) = state
     document_length = attention_input.shape[0]
     query_group = QUERY_HEADS // KEY_VALUE_HEADS
-    picks = route_rows[:, :, None] == jnp.arange(probs.shape[1], dtype=jnp.int32)[None, None, :]
-    grad_probs = jnp.sum(jnp.where(picks, grad_gates[:, :, None], 0.0), axis=1)
+    grad_probs = jnp.where(route_rows, grad_gates, 0.0)
     grad_logits = (
         probs * (grad_probs - jnp.sum(probs * grad_probs, axis=-1, keepdims=True))
     ).astype(jnp.bfloat16)
@@ -262,7 +264,593 @@
     )
 
 
-def local(
+MESH = pl.DeviceIdType.MESH
+F32, BF16 = jnp.float32, jnp.bfloat16
+
+
+def dot(a, b, da=1, db=0):
+    return lax.dot_general(a, b, (((da,), (db,)), ((), ())), preferred_element_type=F32)
+
+
+class Place:
+    def __init__(self, shards, owners):
+        self.shards, self.owners = shards, owners
+        self.line = 4 if owners % 4 == 0 else 1
+        self.side = owners // self.line
+        self.chips = shards // 2
+        self.f = lax.axis_index("fsdp")
+        self.e = lax.axis_index("expert")
+        self.a, self.b = self.e // self.side, self.e % self.side
+        self.x, self.c = self.f // 2, self.f % 2
+
+    def others(self):
+        out = [((self.f, self.e + self.side), self.a < self.line - 1)]
+        out.append(((self.f, self.e - self.side), self.a > 0))
+        for i in range(1, self.side):
+            out.append(((self.f, self.a * self.side + (self.b + i) % self.side), None))
+        out.append(((self.x * 2 + 1 - self.c, self.e), None))
+        for i in range(1, self.chips):
+            out.append((((self.x + i) % self.chips * 2 + self.c, self.e), None))
+        return out
+
+    def meet(self):
+        bar = pltpu.get_barrier_semaphore()
+        for dev, cond in self.others():
+
+            def signal(dev=dev):
+                pl.semaphore_signal(bar, inc=1, device_id=dev, device_id_type=MESH)
+
+            if cond is None:
+                signal()
+            else:
+                pl.when(cond)(signal)
+        count = self.side - 1 + 1 + self.chips - 1
+        pl.semaphore_wait(
+            bar,
+            count
+            + jnp.where(self.a < self.line - 1, 1, 0)
+            + jnp.where(self.a > 0, 1, 0),
+        )
+
+
+def remote(src, dst, send, recv, dev):
+    return pltpu.make_async_remote_copy(
+        src_ref=src, dst_ref=dst, send_sem=send, recv_sem=recv, device_id=dev, device_id_type=MESH
+    )
+
+
+class LineGather:
+    def __init__(self, at, buf, send, recv):
+        self.at, self.buf, self.send, self.recv = at, buf, send, recv
+
+    def up(self, k):
+        at = self.at
+        return remote(
+            self.buf.at[k], self.buf.at[k], self.send.at[0, k], self.recv.at[k], (at.f, at.e + at.side)
+        )
+
+    def down(self, k):
+        at = self.at
+        return remote(
+            self.buf.at[k], self.buf.at[k], self.send.at[1, k], self.recv.at[k], (at.f, at.e - at.side)
+        )
+
+    def across(self, k, i):
+        at = self.at
+        dev = (at.f, at.a * at.side + (at.b + i) % at.side)
+        return remote(
+            self.buf.at[k], self.buf.at[k], self.send.at[1 + i, k], self.recv.at[k], dev
+        )
+
+    def begin(self):
+        at = self.at
+
+        @pl.when(at.a < at.line - 1)
+        def _():
+            self.up(at.e).start()
+
+        @pl.when(at.a > 0)
+        def _():
+            self.down(at.e).start()
+
+        for i in range(1, at.side):
+            self.across(at.e, i).start()
+
+    def relay(self):
+        at = self.at
+        for s in range(1, at.line):
+
+            @pl.when(at.a - s >= 0)
+            def _(s=s):
+                k = at.e - s * at.side
+                self.down(k).wait_recv()
+
+                @pl.when(at.a < at.line - 1)
+                def _():
+                    self.up(k).start()
+
+                for i in range(1, at.side):
+                    self.across(k, i).start()
+
+            @pl.when(at.a + s < at.line)
+            def _(s=s):
+                k = at.e + s * at.side
+                self.up(k).wait_recv()
+
+                @pl.when(at.a > 0)
+                def _():
+                    self.down(k).start()
+
+                for i in range(1, at.side):
+                    self.across(k, i).start()
+
+    def each(self, use):
+        at = self.at
+
+        def step(i, carry):
+            k = (at.a + i) % at.line * at.side + (at.b + i // at.line) % at.side
+
+            @pl.when(i >= at.line)
+            def _():
+                self.across(k, 1).wait_recv()
+
+            use(k)
+            return carry
+
+        lax.fori_loop(0, at.owners, step, 0)
+
+    def finish(self):
+        at = self.at
+        for s in range(at.line):
+            k = s * at.side + at.b
+
+            @pl.when((at.a < at.line - 1) & (at.a >= s))
+            def _():
+                self.up(k).wait_send()
+
+            @pl.when((at.a > 0) & (at.a <= s))
+            def _():
+                self.down(k).wait_send()
+
+            for i in range(1, at.side):
+                self.across(k, i).wait_send()
+
+
+class LineScatter:
+    def __init__(self, at, part, side_in, line_in, own, sems):
+        self.at, self.part, self.side_in, self.line_in, self.own = at, part, side_in, line_in, own
+        self.ssend, self.srecv, self.lsend, self.lrecv = sems
+
+    def across(self, s, i):
+        at = self.at
+        b = (at.b + i) % at.side
+        j = at.side - 1 - i
+        return remote(
+            self.part.at[s * at.side + b],
+            self.side_in.at[s, j],
+            self.ssend.at[s, i - 1],
+            self.srecv.at[s, j],
+            (at.f, at.a * at.side + b),
+        )
+
+    def along(self, s, dev, slot):
+        at = self.at
+        return remote(
+            self.part.at[s * at.side + at.b],
+            self.line_in.at[slot],
+            self.lsend.at[s],
+            self.lrecv.at[slot],
+            (at.f, dev),
+        )
+
+    def up(self, s):
+        return self.along(s, self.at.e + self.at.side, s)
+
+    def down(self, s):
+        at = self.at
+        return self.along(s, at.e - at.side, jnp.where(s == at.a - 1, at.line, s))
+
+    def place(self, i):
+        at = self.at
+        return jnp.where(at.a < at.line // 2, at.line - 1 - i, i)
+
+    def begin(self, make):
+        at = self.at
+
+        def step(n, carry):
+            s, i = self.place(n % at.line), n // at.line + 1
+            make(s * at.side + (at.b + i) % at.side)
+
+            @pl.when(i < at.side)
+            def _():
+                self.across(s, i).start()
+
+            return carry
+
+        lax.fori_loop(0, at.owners, step, 0)
+
+    def sum(self):
+        at = self.at
+
+        def step(n, carry):
+            s = self.place(n)
+            k = s * at.side + at.b
+            for i in range(1, at.side):
+                self.across(s, i).wait_recv()
+            total = self.part[k].astype(F32)
+            for j in range(at.side - 1):
+                total = total + self.side_in[s, j].astype(F32)
+            self.own[...] = total
+
+            @pl.when(((s > at.a) & (at.a > 0)) | ((s < at.a) & (at.a < at.line - 1)))
+            def _():
+                self.along(s, at.e, s).wait_recv()
+                self.own[...] += self.line_in[s].astype(F32)
+
+            self.part[k] = self.own[...].astype(BF16)
+
+            @pl.when(s > at.a)
+            def _():
+                self.up(s).start()
+
+            @pl.when(s < at.a)
+            def _():
+                self.down(s).start()
+
+            return carry
+
+        lax.fori_loop(0, at.line, step, 0)
+        total = self.part[at.e].astype(F32)
+        self.own[...] = total
+
+        @pl.when(at.a > 0)
+        def _():
+            self.along(at.a, at.e, at.a).wait_recv()
+            self.own[...] += self.line_in[at.a].astype(F32)
+
+        @pl.when(at.a < at.line - 1)
+        def _():
+            self.along(at.a, at.e, at.line).wait_recv()
+            self.own[...] += self.line_in[at.line].astype(F32)
+
+    def finish(self):
+        at = self.at
+        for s in range(at.line):
+            for i in range(1, at.side):
+                self.across(s, i).wait_send()
+
+            @pl.when(at.a < s)
+            def _(s=s):
+                self.up(s).wait_send()
+
+            @pl.when(at.a > s)
+            def _(s=s):
+                self.down(s).wait_send()
+
+
+def moe_kernel(sizes, sent, cot, wgu, wd, comb_out, back_out, sums, far, *scratch):
+    shards, owners, tokens, experts, held, pairing = sizes
+    (rows_all, cot_all, taken, cots, slot_gate, place, wg_buf, wd_buf, gg, gd, from_core, to_far,
+     own_sum, z_acc, dx_acc, dg_acc, side1, line1, side2, line2, own2,
+     rs, rr, cs, cr, wsem, coresend, corerecv, farsend, farrecv, osem, free, s1, s2, s3, s4, t1, t2, t3, t4,
+     ) = scratch
+    at = Place(shards, owners)
+    groups = held // pairing
+    slots = groups * CAP
+    half = wd.shape[1]
+    rg, rd = MODEL_WIDTH // shards, half // shards
+    width = MODEL_WIDTH + 128
+
+    def weights(h, slot):
+        return (
+            pltpu.make_async_copy(wgu.at[h], wg_buf.at[slot], wsem.at[0, slot]),
+            pltpu.make_async_copy(wd.at[h], wd_buf.at[slot], wsem.at[1, slot]),
+        )
+
+    for c in weights(0, 0):
+        c.start()
+    at.meet()
+    rows = LineGather(at, rows_all, rs, rr)
+    cotg = LineGather(at, cot_all, cs, cr)
+    c1 = pltpu.make_async_copy(sent, rows_all.at[at.e], osem.at[0, 0])
+    c2 = pltpu.make_async_copy(cot, cot_all.at[at.e], osem.at[0, 1])
+    c1.start()
+    c2.start()
+    c1.wait()
+    rows.begin()
+    rows.relay()
+    c2.wait()
+    cotg.begin()
+
+    lane = lax.broadcasted_iota(jnp.int32, (128, slots), 1)
+    row = lax.broadcasted_iota(jnp.int32, (128, slots), 0)
+
+    def expert_of(j):
+        return (at.e * held + j // CAP * pairing) // 2
+
+    e_lane = expert_of(lane)
+    find_rank = (row == e_lane).astype(F32).astype(BF16)
+    slot_rank = (lane % CAP).astype(F32)
+    e_row = expert_of(lax.broadcasted_iota(jnp.int32, (slots, 128), 0))
+    col = lax.broadcasted_iota(jnp.int32, (slots, 128), 1)
+    pick_gate = (col == e_row + experts) | (col == e_row + 2 * experts)
+
+    def dispatch_rows(k):
+        rank_at = dot(rows_all[k, :, MODEL_WIDTH:], find_rank)
+        pt = jnp.where(rank_at == slot_rank, 1.0, 0.0).astype(BF16)
+        place[k] = pt
+        got = dot(pt, rows_all[k], 0, 0)
+        gate = jnp.sum(jnp.where(pick_gate, got[:, MODEL_WIDTH:], 0.0), axis=1, keepdims=True)
+        gate = jnp.broadcast_to(gate, (slots, 128))
+        to = pl.ds(k * CAP, CAP)
+        for g in range(groups):
+            taken[g, to, :] = got[g * CAP : (g + 1) * CAP, :MODEL_WIDTH].astype(BF16)
+            slot_gate[g, to, :] = gate[g * CAP : (g + 1) * CAP]
+
+    def dispatch_cot(k):
+        got = dot(place[k], cot_all[k], 0, 0).astype(BF16)
+        to = pl.ds(k * CAP, CAP)
+        for g in range(groups):
+            cots[g, to, :] = got[g * CAP : (g + 1) * CAP]
+
+    rows.each(dispatch_rows)
+    cotg.relay()
+    cotg.each(dispatch_cot)
+
+    def to_core(h, slot):
+        out = []
+        for i in range(at.chips):
+            f = 2 * i + 1 - at.c
+            for n, (buf, r, o) in enumerate(((gg, rg, 0), (gd, rd, 1))):
+                out.append(
+                    remote(
+                        buf.at[slot, pl.ds(pl.multiple_of(f * r, r), r)],
+                        from_core[o].at[slot, i],
+                        coresend.at[slot, n, i],
+                        corerecv.at[slot, n, i],
+                        (at.x * 2 + 1 - at.c, at.e),
+                    )
+                )
+        return out
+
+    def to_chips(h):
+        out = []
+        for i in range(1, at.chips):
+            j = at.chips - 1 - i
+            dev = ((at.x + i) % at.chips * 2 + at.c, at.e)
+            for n in range(2):
+                out.append(
+                    remote(
+                        to_far[n].at[h, i - 1],
+                        far[n].at[j, h],
+                        farsend.at[n, i - 1, h],
+                        farrecv.at[n, j, h],
+                        dev,
+                    )
+                )
+        return out
+
+    def own_copy(h, slot):
+        return [
+            pltpu.make_async_copy(own_sum[n].at[slot], sums[n].at[h], osem.at[n, slot])
+            for n in range(2)
+        ]
+
+    def add(h, slot):
+        for c in to_core(h, slot):
+            c.wait()
+
+        @pl.when(h >= 2)
+        def _():
+            for c in own_copy(h, slot):
+                c.wait()
+
+        for i in range(at.chips):
+            x = (at.x + i) % at.chips
+            f = 2 * x + at.c
+            for n, (buf, r) in enumerate(((gg, rg), (gd, rd))):
+                mine = buf[slot, pl.ds(pl.multiple_of(f * r, r), r)].astype(F32)
+                total = (mine + from_core[n][slot, x].astype(F32)).astype(BF16)
+                if i == 0:
+                    own_sum[n][slot] = total
+                else:
+                    to_far[n][h, i - 1] = total
+        for c in to_chips(h):
+            c.start()
+        for c in own_copy(h, slot):
+            c.start()
+
+        @pl.when(h < held - 2)
+        def _():
+            pl.semaphore_signal(
+                free, inc=1, device_id=(at.x * 2 + 1 - at.c, at.e), device_id_type=MESH
+            )
+
+    def step(h, carry):
+        slot = h % 2
+        g, m = h // pairing, h % pairing
+        for c in weights(h, slot):
+            c.wait()
+
+        @pl.when(h + 1 < held)
+        def _():
+            for c in weights(h + 1, 1 - slot):
+                c.start()
+
+        @pl.when(m == 0)
+        def _():
+            z_acc[...] = jnp.zeros_like(z_acc)
+            dx_acc[...] = jnp.zeros_like(dx_acc)
+            dg_acc[...] = jnp.zeros_like(dg_acc)
+
+        gu = dot(taken[g], wg_buf[slot])
+        a, b = gu[:, :half], gu[:, half:]
+        gate = slot_gate[g][:, :1]
+        sig = 1.0 / (1.0 + jnp.exp(-a))
+        s = a * sig
+        act = s * b
+        actg = (act * gate).astype(BF16)
+        dp = dot(cots[g], wd_buf[slot], 1, 1)
+        dg_acc[...] += jnp.broadcast_to(
+            jnp.sum(act * dp, axis=1, keepdims=True), dg_acc.shape
+        )
+        dact = dp * gate
+        da = dact * b * sig * (1.0 + a * (1.0 - sig))
+        db = dact * s
+        du = jnp.concatenate([da, db], axis=1).astype(BF16)
+        z_acc[...] += dot(actg, wd_buf[slot])
+        dx_acc[...] += dot(du, wg_buf[slot], 1, 1)
+        for i in range(3):
+            n = MODEL_WIDTH // 3
+            gg[slot, i * n : (i + 1) * n, :] = dot(
+                taken[g, :, i * n : (i + 1) * n], du, 0, 0
+            ).astype(BF16)
+        gd[slot] = dot(actg, cots[g], 0, 0).astype(BF16)
+
+        @pl.when(h >= 2)
+        def _():
+            pl.semaphore_wait(free, 1)
+
+        for c in to_core(h, slot):
+            c.start()
+
+        @pl.when(h > 0)
+        def _():
+            add(h - 1, 1 - slot)
+
+        @pl.when(m == pairing - 1)
+        def _():
+            taken[g] = z_acc[...].astype(BF16)
+            cots[g] = dx_acc[...].astype(BF16)
+            slot_gate[g] = dg_acc[...]
+
+        return carry
+
+    lax.fori_loop(0, held, step, 0)
+    add(held - 1, (held - 1) % 2)
+
+    rows.finish()
+    cotg.finish()
+
+    home = (col == e_row).astype(F32).astype(BF16)
+    home_low = (col == e_row + experts).astype(F32).astype(BF16)
+
+    def make_back(k):
+        to = pl.ds(k * CAP, CAP)
+        dx = jnp.concatenate([cots[g, to, :] for g in range(groups)], axis=0)
+        dg = jnp.concatenate([slot_gate[g, to, :] for g in range(groups)], axis=0)
+        high = dg.astype(BF16)
+        low = (dg - high.astype(F32)).astype(BF16)
+        dgm = high * home + low * home_low
+        pt = place[k]
+        rows_all[k, :, :MODEL_WIDTH] = dot(pt, dx).astype(BF16)
+        rows_all[k, :, MODEL_WIDTH:] = dot(pt, dgm).astype(BF16)
+
+    def make_comb(k):
+        to = pl.ds(k * CAP, CAP)
+        y = jnp.concatenate([taken[g, to, :] for g in range(groups)], axis=0)
+        cot_all[k] = dot(place[k], y).astype(BF16)
+
+    back = LineScatter(at, rows_all, side1, line1, back_out, (s1, s2, s3, s4))
+    comb = LineScatter(at, cot_all, side2, line2, own2, (t1, t2, t3, t4))
+    back.begin(make_back)
+    comb.begin(make_comb)
+    back.sum()
+    comb.sum()
+    comb_out[...] = own2[...]
+    back.finish()
+    comb.finish()
+    for h in range(held - 2, held):
+        for c in own_copy(h, h % 2):
+            c.wait()
+
+    def drain(h, carry):
+        for c in to_chips(h):
+            c.wait()
+        return carry
+
+    lax.fori_loop(0, held, drain, 0)
+
+
+def moe(sizes, sent, cot, wgu, wd):
+    shards, owners, tokens, experts, held, pairing = sizes
+    groups = held // pairing
+    slots, rows = groups * CAP, owners * CAP
+    hidden, half = wgu.shape[2], wd.shape[1]
+    rg, rd = MODEL_WIDTH // shards, half // shards
+    chips = shards // 2
+    line = 4 if owners % 4 == 0 else 1
+    side = owners // line
+    width = MODEL_WIDTH + 128
+    vm, dma = pltpu.VMEM, pltpu.SemaphoreType.DMA
+    any_, vmem = pl.BlockSpec(memory_space=pl.ANY), pl.BlockSpec(memory_space=pltpu.VMEM)
+
+    def pair(lead, dtype=BF16):
+        return (vm((*lead, rg, hidden), dtype), vm((*lead, rd, MODEL_WIDTH), dtype))
+
+    def outs(lead):
+        return (
+            jax.ShapeDtypeStruct((*lead, rg, hidden), BF16),
+            jax.ShapeDtypeStruct((*lead, rd, MODEL_WIDTH), BF16),
+        )
+
+    def scatter_sems():
+        return [dma((line, side)), dma((line, side)), dma((line,)), dma((line + 1,))]
+
+    return pl.pallas_call(
+        functools.partial(moe_kernel, sizes),
+        name="moe",
+        out_shape=(
+            jax.ShapeDtypeStruct((tokens, MODEL_WIDTH), F32),
+            jax.ShapeDtypeStruct((tokens, width), F32),
+            outs((held,)),
+            outs((chips - 1, held)),
+        ),
+        in_specs=[any_] * 4,
+        out_specs=(vmem, vmem, (any_, any_), (any_, any_)),
+        scratch_shapes=[
+            vm((owners, tokens, width), BF16),
+            vm((owners, tokens, MODEL_WIDTH), BF16),
+            vm((groups, rows, MODEL_WIDTH), BF16),
+            vm((groups, rows, MODEL_WIDTH), BF16),
+            vm((groups, rows, 128), F32),
+            vm((owners, tokens, slots), BF16),
+            vm((2, MODEL_WIDTH, hidden), BF16),
+            vm((2, half, MODEL_WIDTH), BF16),
+            vm((2, MODEL_WIDTH, hidden), BF16),
+            vm((2, half, MODEL_WIDTH), BF16),
+            pair((2, chips)),
+            pair((held, chips - 1)),
+            pair((2,)),
+            vm((rows, MODEL_WIDTH), F32),
+            vm((rows, MODEL_WIDTH), F32),
+            vm((rows, 128), F32),
+            vm((line, side - 1, tokens, width), BF16),
+            vm((line + 1, tokens, width), BF16),
+            vm((line, side - 1, tokens, MODEL_WIDTH), BF16),
+            vm((line + 1, tokens, MODEL_WIDTH), BF16),
+            vm((tokens, MODEL_WIDTH), F32),
+            dma((side + 1, owners)),
+            dma((owners,)),
+            dma((side + 1, owners)),
+            dma((owners,)),
+            dma((2, 2)),
+            dma((2, 2, chips)),
+            dma((2, 2, chips)),
+            dma((2, chips - 1, held)),
+            dma((2, chips - 1, held)),
+            dma((2, 2)),
+            pltpu.SemaphoreType.REGULAR,
+            *scatter_sems(),
+            *scatter_sems(),
+        ],
+        compiler_params=pltpu.CompilerParams(
+            collective_id=1, has_side_effects=True, vmem_limit_bytes=63 * 2**20
+        ),
+    )(sent, cot, wgu, wd)
+
+
+def plain_local(
     hidden_in,
     doc_ids,
     routes,
@@ -277,182 +865,214 @@
     w_down,
     cotangent,
 ):
-    full_query, full_key, full_value, full_output, full_router = (
-        lax.all_gather(w_query, "fsdp", axis=0, tiled=True),
-        lax.all_gather(key_matrix, "fsdp", axis=0, tiled=True),
-        lax.all_gather(value_matrix, "fsdp", axis=0, tiled=True),
-        lax.all_gather(w_output, "fsdp", axis=0, tiled=True),
-        lax.all_gather(w_router, "fsdp", axis=0, tiled=True),
-    )
-    weights_attn = (gain_attn, full_query, full_key, full_value, full_output, gain_ffn, full_router)
-    document_length = hidden_in.shape[0]
-    experts = full_router.shape[1]
+    tokens = hidden_in.shape[0]
+    experts = w_router.shape[1]
+    shards = lax.axis_size("fsdp")
     owners = lax.axis_size("expert")
     held = w_gateup.shape[0]
-    half_units = w_down.shape[1]
+    half = w_down.shape[1]
     hidden_units = w_gateup.shape[2]
     pairing = 2 if held % 2 == 0 else 1
-    copies = 2 // pairing
     groups = held // pairing
+    slots = groups * CAP
+    mine = lax.axis_index("expert")
+    f32, bf16 = jnp.float32, jnp.bfloat16
+
+    first = lax.all_gather(
+        jnp.concatenate([w_query, key_matrix, value_matrix, w_router], axis=1),
+        "fsdp",
+        axis=0,
+        tiled=True,
+    )
+    full_query, full_key, full_value, full_router = jnp.split(first, (1536, 2048, 2560), axis=1)
+    full_output = lax.all_gather(w_output, "fsdp", axis=0, tiled=True)
+    cot_all = lax.all_gather(cotangent, "expert", axis=0)
+    weights_attn = (gain_attn, full_query, full_key, full_value, full_output, gain_ffn, full_router)
+    state = forward_local(hidden_in, doc_ids[0], routes, *weights_attn)
+    resid, ffn_in, probs = state[11], state[12], state[15]
+
+    chosen = jnp.any(
+        routes[:, :, None] == jnp.arange(experts, dtype=jnp.int32)[None, None, :], axis=1
+    )
+    below = jnp.tril(jnp.ones((tokens, tokens), bf16), -1)
+    rank = jnp.dot(below, chosen.astype(bf16), preferred_element_type=f32)
+    rank = jnp.where(chosen, rank, -1.0)
+    gate = jnp.where(chosen, probs, 0.0)
+    gate_high = gate.astype(bf16)
+    gate_low = (gate - gate_high.astype(f32)).astype(bf16)
+    meta = jnp.concatenate([rank.astype(bf16), gate_high, gate_low], axis=1)
+    sent = jnp.concatenate(
+        [ffn_in, meta, jnp.zeros((tokens, 128 - 3 * experts), bf16)], axis=1
+    )
+    got = lax.all_gather(sent, "expert", axis=0)
+    rows_all = got[:, :, :MODEL_WIDTH]
+    meta_all = got[:, :, MODEL_WIDTH:]
+    lane = jnp.arange(slots, dtype=jnp.int32)
+    slot_expert = (mine * held + (lane // CAP) * pairing) // 2
+    spread = (jnp.arange(experts, dtype=jnp.int32)[:, None] == slot_expert[None, :]).astype(bf16)
+    rank_at = jnp.dot(meta_all[:, :, :experts], spread, preferred_element_type=f32)
+    gate_at = jnp.dot(
+        meta_all[:, :, experts : 2 * experts], spread, preferred_element_type=f32
+    ) + jnp.dot(meta_all[:, :, 2 * experts : 3 * experts], spread, preferred_element_type=f32)
+    place = rank_at == (lane % CAP).astype(f32)[None, None, :]
+    onehot = place.astype(bf16)
+    gated = jnp.where(place, gate_at, 0.0)
+    slot_gate = jnp.sum(gated, axis=1)
+
+    def dispatch(rows):
+        out = jnp.einsum("stj,std->sjd", onehot, rows, preferred_element_type=f32)
+        return out.reshape(owners, groups, CAP, MODEL_WIDTH)
+
+    taken = dispatch(rows_all).astype(bf16)
+    cot_rows = dispatch(cot_all)
+    slot_gate_4 = slot_gate.reshape(owners, groups, CAP, 1)
+    grads_in = (cot_rows * slot_gate_4).astype(bf16)
     w_pairs = w_gateup.reshape(groups, pairing, MODEL_WIDTH, hidden_units)
-    down_pairs = w_down.reshape(groups, pairing, half_units, MODEL_WIDTH)
+    down_pairs = w_down.reshape(groups, pairing, half, MODEL_WIDTH)
+    gate_up = jnp.einsum("secd,emdf->emscf", taken, w_pairs, preferred_element_type=f32)
+    a, b = gate_up[..., :half], gate_up[..., half:]
+    sigma = jax.nn.sigmoid(a)
+    acted = (a * sigma * b).astype(bf16)
+    made = jnp.einsum("emscf,emfd->secd", acted, down_pairs, preferred_element_type=f32)
+    made = made.astype(bf16)
+    grad_slot = jnp.sum(made.astype(f32) * cot_rows, axis=-1).reshape(owners, slots)
+    grad_gate_back = jnp.where(place, grad_slot[:, None, :], 0.0).reshape(
+        owners, tokens, groups, CAP
+    )
+    grad_gate_back = jnp.sum(grad_gate_back, axis=-1)
+    onto = (
+        (mine * held + jnp.arange(groups) * pairing)[:, None] // 2
+        == jnp.arange(128, dtype=jnp.int32)[None, :]
+    ).astype(bf16)
+    grad_gate_back = jnp.dot(
+        grad_gate_back.astype(bf16), onto, preferred_element_type=f32
+    ).astype(bf16)
+    weighted = (made.astype(f32) * slot_gate_4).astype(bf16).reshape(owners, slots, MODEL_WIDTH)
+    combined = jnp.einsum("stj,sjd->std", onehot, weighted, preferred_element_type=f32)
+    grad_acted = jnp.einsum("secd,emfd->emscf", grads_in, down_pairs, preferred_element_type=f32)
+    grad_down = jnp.einsum("emscf,secd->emfd", acted, grads_in, preferred_element_type=f32)
+    grad_a = grad_acted * b * sigma * (1.0 + a * (1.0 - sigma))
+    grad_b = grad_acted * a * sigma
+    joined = jnp.concatenate([grad_a, grad_b], axis=-1).astype(bf16)
+    grad_gateup = jnp.einsum("secd,emscf->emdf", taken, joined, preferred_element_type=f32)
+    grad_rows = jnp.einsum("emscf,emdf->secd", joined, w_pairs, preferred_element_type=f32)
+    grad_rows = grad_rows.astype(bf16).reshape(owners, slots, MODEL_WIDTH)
+    grad_ffn = jnp.einsum("stj,sjd->std", onehot, grad_rows, preferred_element_type=f32)
+    back = jnp.concatenate([grad_ffn.astype(bf16), grad_gate_back], axis=-1)
+    back = lax.psum_scatter(
+        back.reshape(owners * tokens, -1), "expert", scatter_dimension=0, tiled=True
+    ).astype(f32)
+    grad_ffn, grad_gate_dense = back[:, :MODEL_WIDTH], back[:, MODEL_WIDTH : MODEL_WIDTH + experts]
+    combined = lax.psum_scatter(
+        combined.astype(bf16).reshape(owners * tokens, -1),
+        "expert",
+        scatter_dimension=0,
+        tiled=True,
+    )
+    block_out = (resid + combined.astype(f32)).astype(bf16)
+    grad_gateup, grad_down = (
+        lax.psum_scatter(
+            grad_gateup.reshape(held, MODEL_WIDTH, hidden_units).astype(bf16),
+            "fsdp",
+            scatter_dimension=1,
+            tiled=True,
+        ).astype(f32),
+        lax.psum_scatter(
+            grad_down.reshape(held, half, MODEL_WIDTH).astype(bf16),
+            "fsdp",
+            scatter_dimension=1,
+            tiled=True,
+        ).astype(f32),
+    )
+    grad_input, grads = backward_local(
+        state, chosen, cotangent, grad_ffn, grad_gate_dense, *weights_attn
+    )
+    widths = [g.shape[1] if g.ndim == 2 else 1 for g in grads]
+    flat = jnp.concatenate([g if g.ndim == 2 else g[:, None] for g in grads], axis=1)
+    share = lax.psum_scatter(flat.astype(bf16), "fsdp", scatter_dimension=0, tiled=True)
+    total = lax.psum(share, "expert").astype(f32)
+    pieces = jnp.split(total, [sum(widths[: i + 1]) for i in range(len(widths) - 1)], axis=1)
+    pieces = [p if g.ndim == 2 else p[:, 0] for p, g in zip(pieces, grads)]
+    return (block_out, grad_input, *pieces, grad_gateup, grad_down)
+
+
+def kernel_local(
+    hidden_in,
+    doc_ids,
+    routes,
+    gain_attn,
+    w_query,
+    key_matrix,
+    value_matrix,
+    w_output,
+    gain_ffn,
+    w_router,
+    w_gateup,
+    w_down,
+    cotangent,
+):
+    tokens = hidden_in.shape[0]
+    experts = w_router.shape[1]
+    shards = lax.axis_size("fsdp")
+    owners = lax.axis_size("expert")
+    held = w_gateup.shape[0]
+    pairing = 2 if held % 2 == 0 else 1
+    f32, bf16 = jnp.float32, jnp.bfloat16
+
+    first = lax.all_gather(
+        jnp.concatenate([w_query, key_matrix, value_matrix, w_router], axis=1),
+        "fsdp",
+        axis=0,
+        tiled=True,
+    )
+    full_query, full_key, full_value, full_router = jnp.split(first, (1536, 2048, 2560), axis=1)
+    full_output = lax.all_gather(w_output, "fsdp", axis=0, tiled=True)
+    weights_attn = (gain_attn, full_query, full_key, full_value, full_output, gain_ffn, full_router)
     state = forward_local(hidden_in, doc_ids[0], routes, *weights_attn)
-    resid = state[11]
-    ffn_in = state[12]
-    gates = state[16]
-    slot_total = document_length * TOP
-    slot_expert = routes.reshape(slot_total)
-    onehot_slots = (slot_expert[:, None] == jnp.arange(experts, dtype=jnp.int32)[None, :]).astype(
-        jnp.int32
-    )
-    ranks = jnp.sum((jnp.cumsum(onehot_slots, axis=0) - 1) * onehot_slots, axis=1)
-    flat_pos = slot_expert * CAP + ranks
-    slot_of = (
-        jnp.full((experts * CAP,), slot_total, jnp.int32)
-        .at[flat_pos]
-        .set(jnp.arange(slot_total, dtype=jnp.int32))
-    )
-    token_of = slot_of // TOP
-    padded_rows = jnp.concatenate([ffn_in, jnp.zeros((1, MODEL_WIDTH), jnp.bfloat16)], axis=0)
-    expert_rows = padded_rows[token_of].reshape(experts, CAP, MODEL_WIDTH)
-    sent_rows = jnp.repeat(expert_rows, copies, axis=0).reshape(owners, groups, CAP, MODEL_WIDTH)
-    got_rows = lax.all_to_all(sent_rows, "expert", split_axis=0, concat_axis=0, tiled=True)
-    gate_up = jnp.einsum("secd,emdf->semcf", got_rows, w_pairs, preferred_element_type=jnp.float32)
-    gate_part = gate_up[..., :half_units]
-    up_part = gate_up[..., half_units:]
-    acted = (jax.nn.silu(gate_part) * up_part).astype(jnp.bfloat16)
-    made_parts = jnp.einsum(
-        "semcf,emfd->semcd", acted, down_pairs, preferred_element_type=jnp.float32
-    ).astype(jnp.bfloat16)
-    made = jnp.sum(made_parts.astype(jnp.float32), axis=2).astype(jnp.bfloat16)
-    returned = lax.all_to_all(made, "expert", split_axis=0, concat_axis=0, tiled=True)
-    joined_out = jnp.sum(
-        returned.reshape(experts, copies, CAP, MODEL_WIDTH).astype(jnp.float32), axis=1
-    )
-    joined_out = lax.optimization_barrier(joined_out.astype(jnp.bfloat16)).astype(jnp.float32)
-    slot_out = joined_out.reshape(experts * CAP, MODEL_WIDTH)[flat_pos].reshape(
-        document_length, TOP, MODEL_WIDTH
-    )
-    combined = jnp.einsum("tk,tkd->td", gates, slot_out)
-    block_out = (resid + combined).astype(jnp.bfloat16)
-    cot_f = cotangent.astype(jnp.float32)
-    grad_gates = jnp.einsum("td,tkd->tk", cot_f, slot_out)
-    grad_slots = (
-        (gates[:, :, None] * cot_f[:, None, :])
-        .astype(jnp.bfloat16)
-        .reshape(slot_total, MODEL_WIDTH)
-    )
-    padded_grads = jnp.concatenate([grad_slots, jnp.zeros((1, MODEL_WIDTH), jnp.bfloat16)], axis=0)
-    expert_grads_rows = padded_grads[slot_of].reshape(experts, CAP, MODEL_WIDTH)
-    sent_grads = jnp.repeat(expert_grads_rows, copies, axis=0).reshape(
-        owners, groups, CAP, MODEL_WIDTH
-    )
-    owner_rows, owner_grads = (
-        lax.all_to_all(sent_rows, "expert", split_axis=0, concat_axis=0, tiled=True),
-        lax.all_to_all(sent_grads, "expert", split_axis=0, concat_axis=0, tiled=True),
-    )
-    gate_up_again = jnp.einsum(
-        "secd,emdf->semcf", owner_rows, w_pairs, preferred_element_type=jnp.float32
-    )
-    gate_again = gate_up_again[..., :half_units]
-    up_again = gate_up_again[..., half_units:]
-    acted_again = (jax.nn.silu(gate_again) * up_again).astype(jnp.bfloat16)
-    grad_acted = jnp.einsum(
-        "secd,emfd->semcf", owner_grads, down_pairs, preferred_element_type=jnp.float32
-    )
-    grad_down_local = jnp.einsum(
-        "semcf,secd->emfd", acted_again, owner_grads, preferred_element_type=jnp.float32
-    ).reshape(held, half_units, MODEL_WIDTH)
-    sigma = jax.nn.sigmoid(gate_again)
-    grad_gate = grad_acted * up_again * sigma * (1.0 + gate_again * (1.0 - sigma))
-    grad_up = grad_acted * gate_again * sigma
-    grad_joined = jnp.concatenate([grad_gate, grad_up], axis=-1).astype(jnp.bfloat16)
-    grad_gateup_local = jnp.einsum(
-        "secd,semcf->emdf", owner_rows, grad_joined, preferred_element_type=jnp.float32
-    ).reshape(held, MODEL_WIDTH, hidden_units)
-    grad_parts = jnp.einsum(
-        "semcf,emdf->semcd", grad_joined, w_pairs, preferred_element_type=jnp.float32
-    ).astype(jnp.bfloat16)
-    grad_rows = jnp.sum(grad_parts.astype(jnp.float32), axis=2).astype(jnp.bfloat16)
-    grad_back = lax.all_to_all(grad_rows, "expert", split_axis=0, concat_axis=0, tiled=True)
-    grad_joined_back = jnp.sum(
-        grad_back.reshape(experts, copies, CAP, MODEL_WIDTH).astype(jnp.float32), axis=1
-    )
-    grad_joined_back = lax.optimization_barrier(grad_joined_back.astype(jnp.bfloat16)).astype(
-        jnp.float32
-    )
-    grad_ffn = jnp.sum(
-        grad_joined_back.reshape(experts * CAP, MODEL_WIDTH)[flat_pos].reshape(
-            document_length, TOP, MODEL_WIDTH
-        ),
-        axis=1,
+    resid, ffn_in, probs = state[11], state[12], state[15]
+
+    chosen = jnp.any(
+        routes[:, :, None] == jnp.arange(experts, dtype=jnp.int32)[None, None, :], axis=1
+    )
+    below = jnp.tril(jnp.ones((tokens, tokens), bf16), -1)
+    rank = jnp.dot(below, chosen.astype(bf16), preferred_element_type=f32)
+    rank = jnp.where(chosen, rank, -1.0)
+    gate = jnp.where(chosen, probs, 0.0)
+    gate_high = gate.astype(bf16)
+    gate_low = (gate - gate_high.astype(f32)).astype(bf16)
+    meta = jnp.concatenate([rank.astype(bf16), gate_high, gate_low], axis=1)
+    sent = jnp.concatenate(
+        [ffn_in, meta, jnp.zeros((tokens, 128 - 3 * experts), bf16)], axis=1
+    )
+    sizes = (shards, owners, tokens, experts, held, pairing)
+    combined, back, sums, far = moe(sizes, sent, cotangent, w_gateup, w_down)
+    block_out = (resid + combined).astype(bf16)
+    grad_ffn = back[:, :MODEL_WIDTH]
+    grad_gate_dense = (
+        back[:, MODEL_WIDTH : MODEL_WIDTH + experts]
+        + back[:, MODEL_WIDTH + experts : MODEL_WIDTH + 2 * experts]
     )
     grad_gateup, grad_down = (
-        lax.psum_scatter(grad_gateup_local, "fsdp", scatter_dimension=1, tiled=True),
-        lax.psum_scatter(grad_down_local, "fsdp", scatter_dimension=1, tiled=True),
+        s.astype(f32) + jnp.sum(r.astype(f32), axis=0) for s, r in zip(sums, far)
     )
     grad_input, grads = backward_local(
-        state, routes, cotangent, grad_ffn, grad_gates, *weights_attn
-    )
-    (
-        local_query,
-        local_key,
-        local_value,
-        local_output,
-        local_router,
-        local_gain_attn,
-        local_gain_ffn,
-    ) = grads
-    (
-        share_query,
-        share_key,
-        share_value,
-        share_output,
-        share_router,
-        share_gain_attn,
-        share_gain_ffn,
-    ) = (
-        lax.psum_scatter(local_query, "fsdp", scatter_dimension=0, tiled=True),
-        lax.psum_scatter(local_key, "fsdp", scatter_dimension=0, tiled=True),
-        lax.psum_scatter(local_value, "fsdp", scatter_dimension=0, tiled=True),
-        lax.psum_scatter(local_output, "fsdp", scatter_dimension=0, tiled=True),
-        lax.psum_scatter(local_router, "fsdp", scatter_dimension=0, tiled=True),
-        lax.psum_scatter(local_gain_attn, "fsdp", scatter_dimension=0, tiled=True),
-        lax.psum_scatter(local_gain_ffn, "fsdp", scatter_dimension=0, tiled=True),
-    )
-    (
-        total_query,
-        total_key,
-        total_value,
-        total_output,
-        total_router,
-        total_gain_attn,
-        total_gain_ffn,
-    ) = lax.psum(
-        (
-            share_query,
-            share_key,
-            share_value,
-            share_output,
-            share_router,
-            share_gain_attn,
-            share_gain_ffn,
-        ),
-        "expert",
-    )
-    return (
-        block_out,
-        grad_input,
-        total_query,
-        total_key,
-        total_value,
-        total_output,
-        total_router,
-        total_gain_attn,
-        total_gain_ffn,
-        grad_gateup,
-        grad_down,
-    )
+        state, chosen, cotangent, grad_ffn, grad_gate_dense, *weights_attn
+    )
+    widths = [g.shape[1] if g.ndim == 2 else 1 for g in grads]
+    flat = jnp.concatenate([g if g.ndim == 2 else g[:, None] for g in grads], axis=1)
+    share = lax.psum_scatter(flat.astype(bf16), "fsdp", scatter_dimension=0, tiled=True)
+    total = lax.psum(share, "expert").astype(f32)
+    pieces = jnp.split(total, [sum(widths[: i + 1]) for i in range(len(widths) - 1)], axis=1)
+    pieces = [p if g.ndim == 2 else p[:, 0] for p, g in zip(pieces, grads)]
+    return (block_out, grad_input, *pieces, grad_gateup, grad_down)
+
+
+def local(*args):
+    owners, held = lax.axis_size("expert"), args[10].shape[0]
+    groups = held // (2 if held % 2 == 0 else 1)
+    if owners * groups * CAP <= 2048 and owners % 4 == 0:
+        return kernel_local(*args)
+    return plain_local(*args)
 
 
 def solution(mesh):

time: 1640 us -> 700 us (0.43)
  waiting for transfers between devices: 1010 us -> 306 us
  blocking collectives: 326 us -> 0 us
  Pallas kernels: 0 us -> 216 us
  matrix products: 127 us -> 39.2 us
    reduce_scatter x7 -> x0, waiting for transfers between devices: 454 us -> none  [the longest x1 216 us: local(): lax.psum_scatter(grad_gateup_local, 'fsdp', scatter_dimension=1, tiled=True)]
    all_to_all x2 -> x0, blocking collectives: 271 us -> none  [the longest x1 137 us: local(): lax.all_to_all(sent_rows, 'expert', split_axis=0, concat_axis=0, tiled=True)]
    all_to_all x2 -> x0, waiting for transfers between devices: 246 us -> none  [the longest x1 125 us: local(): lax.all_to_all(grad_rows, 'expert', split_axis=0, concat_axis=0, tiled=True)]
    pallas_call x0 -> x1, Pallas kernels: none -> 216 us  [moe(): pl.pallas_call(functools.partial(moe_kernel, sizes), name='moe', out_shap...]
    unnamed x12 -> x5, waiting for transfers between devices: 2.71 us -> 102 us
    psum x1, waiting for transfers between devices: 215 us -> 117 us  [kernel_local(): total = lax.psum(share, 'expert').astype(f32)]
    dot_general x8 -> x1, matrix products: 83.3 us -> 0.2 us  [kernel_local(): rank = jnp.dot(below, chosen.astype(bf16), preferred_element_type=f32)]
    concatenate x2, local copies, waits for them, and re-layouts: 0.24 us -> 54.1 us  [the longest x1 53.2 us: kernel_local(): jnp.concatenate([g if g.ndim == 2 else g[:, None] for g in grads], axis=1)]
  transfers between devices with their start and end apart: 14 -> 4, of which waited for: 13 -> 4; matrix products, arithmetic and copies ran while one was open for 7% -> 3% of each run, Pallas kernels for 0% -> 0%
where the time goes in v1:
time: 700 us; the launch traced here: 697 us
  waiting for transfers between devices  306 us (44%)
  Pallas kernels  216 us (31%)
  local copies, waits for them, and re-layouts  99.5 us (14%)
  matrix products  39.2 us (6%)
  other arithmetic  21.4 us (3%)
  between operations  14.6 us (2%)
    pallas_call x1, Pallas kernels, moe(): pl.pallas_call(functools.partial(moe_kernel, sizes), name='moe', out_shap...  216 us
    psum x1, waiting for transfers between devices, kernel_local(): total = lax.psum(share, 'expert').astype(f32)  117 us
    unnamed x5, waiting for transfers between devices  102 us
    all_gather x1, waiting for transfers between devices, kernel_local(): lax.all_gather(jnp.concatenate([w_query, key_matrix, value_matrix, w_rout...  58.6 us
    concatenate x1, local copies, waits for them, and re-layouts, kernel_local(): jnp.concatenate([g if g.ndim == 2 else g[:, None] for g in grads], axis=1)  53.2 us
    unnamed x93, local copies, waits for them, and re-layouts  36.9 us
    all_gather x1, waiting for transfers between devices, kernel_local(): full_output = lax.all_gather(w_output, 'fsdp', axis=0, tiled=True)  28.2 us
  transfers between devices with their start and end apart: 4, of which 4 were waited for; matrix products, arithmetic and copies ran while one was open for 3% of the time, Pallas kernels for 0%

profile of v1, /device:TPU:0, one launch (start us, length us, event | category | flops | bytes accessed | tf_op | source)
XLA Modules:
  0.0 697.3 jit_solution(17186469083673853320)
XLA Ops:
  7.2 0.9 copy.97
  8.1 3.0 pad_maximum_fusion
  11.2 0.7 all-gather.5.cloned.1.call-update
  12.3 0.2 fusion.29
  12.6 0.1 multiply_cosine_fusion
  12.7 0.2 fusion.22
  12.9 58.6 %all-gather.3.cloned.1.call-done = bf16[1536,2600]{1,0:T(8,128)(2,1)} async-done(((bf16[384,2600]{1,0:T(8,128)(2,1)}), bf16[1536,2600]{1,0:T(8,128)(2,1)}) %all-gather.3.cloned.1.call-update) | async-done | bytes 7987216 | tf_op jit(solution)/shard_map/all_gather | solution.py:1022
  71.6 1.8 fusion.19
  73.4 0.1 copy.98
  73.5 2.2 fusion.9
  75.8 4.4 fusion.2
  80.2 0.1 subtract_convert_fusion.1
  80.4 0.4 fusion.60
  80.8 0.3 exponential_reduce_fusion
  81.2 0.8 copy-done.1
  82.0 0.4 convolution_convert_fusion.6
  82.4 28.2 %all-gather.5.cloned.1.call-done = bf16[1536,1536]{1,0:T(8,128)(2,1)} async-done(((bf16[384,1536]{1,0:T(8,128)(2,1)}), bf16[1536,1536]{1,0:T(8,128)(2,1)}) %all-gather.5.cloned.1.call-update) | async-done | bytes 4718608 | tf_op jit(solution)/shard_map/all_gather | solution.py:1029
  110.6 3.2 multiply_reduce_fusion.3
  113.9 0.8 copy-done.4
  114.7 0.1 multiply_convert_fusion
  114.9 1.4 fusion.61
  116.4 0.2 fusion.42
  116.8 0.3 copy-done.36
  117.1 0.9 concatenate.36.sent
  118.0 216.0 %moe.1 = (f32[128,1536]{1,0:T(8,128)}, f32[128,1664]{1,0:T(8,128)}, bf16[10,384,512]{2,1,0:T(8,128)(2,1)}, bf16[10,64,1536]{2,1,0:T(8,128)(2,1)}, bf16[1,10,384,...) custom-call(bf16[128,1664]{1,0:T(8,128)(2,1)} %concatenate.36.sent, bf16[128,1536]{1,0:T(8,128)(2,1)} %cot.1, ...), custom_call_target="tpu_custom_call" | custom-call | tf_op jit(solution)/shard_map/moe/pallas_call | solution.py:800
  334.1 1.2 multiply_reduce_fusion.4
  335.4 1.1 multiply_convert_fusion.1
  336.4 1.9 convolution_convert_fusion.5
  338.3 2.0 multiply_reduce_fusion
  340.3 1.0 multiply_add_fusion
  341.4 4.8 convolution_convert_fusion.4
  346.2 1.9 copy.107
  348.2 1.2 multiply_reduce_fusion.1
  349.4 1.5 fusion.18
  350.9 0.5 fusion.6
  351.5 0.5 convolution_bitcast_fusion.1
  352.0 0.3 fusion.38
  352.3 3.6 convolution_convert_fusion.1
  356.0 0.1 add_convert_fusion.1
  356.1 0.6 convolution_convert_fusion.2
  356.8 1.8 convolution_convert_fusion.3
  358.7 3.7 convolution_convert_fusion
  362.3 1.7 fusion
  364.0 0.6 convolution_add_fusion.1
  364.7 1.6 fusion.28
  366.3 53.2 %concatenate.39 = bf16[1536,4138]{0,1:T(8,128)(2,1)} concatenate(bf16[1536,1536]{0,1:T(8,128)(2,1)} %convolution_convert_fusion, bf16[1536,512]{0,1:T(8,128)(2,1)} %convolution_convert_fusion.3, bf16[1536,512]{0,1:T(8,128)(2,1)S(1)} %convolution_convert_fusion.2, bf16[1536,1536]{0,1:T(8,128)(2,1)} %convolution_convert_fusion.1, bf16[1536,40]{0,1:T(8,128)(2,1)S(1)} %copy-done.17, ...), dimensions={1} | concatenate | bytes 25423872 | tf_op jit(solution)/shard_map/concatenate | solution.py:1062
  419.5 16.4 %copy.126 = bf16[1536,4138]{1,0:T(8,128)(2,1)} copy(bf16[1536,4138]{0,1:T(8,128)(2,1)} %concatenate.39) | data formatting | bytes 25423872
  436.0 0.3 all-reduce.2.cloned.1.call-start
  436.3 101.2 %reduce-scatter.4.cloned.1.call-done = bf16[384,4138]{1,0:T(8,128)(2,1)} async-done(((bf16[1536,4138]{1,0:T(8,128)(2,1)}), bf16[384,4138]{1,0:T(8,128)(2,1)}) %reduce-scatter.4.cloned.1.call-update) | async-done | bytes 3178000
  537.5 5.6 copy.127
  543.1 1.1 copy-done.8
  544.2 1.2 fusion.27
  545.4 8.1 %convert_add_fusion = f32[10,384,512]{2,1,0:T(8,128)} fusion(bf16[10,384,512]{2,1,0:T(8,128)(2,1)} %get-tuple-element.19, bf16[1,10,384,512]{3,2,1,0:T(8,128)(2,1)} %get-tuple-element.20), kind=kLoop, calls=%fused_computation | loop fusion | flops 5898240 | bytes 15728640 | tf_op jit(solution)/shard_map/add | solution.py:1056
  553.5 2.5 convert_add_fusion.1
  556.0 117.4 %all-reduce.2.cloned.1.call-done = bf16[384,4138]{0,1:T(8,128)(2,1)} async-done(((bf16[384,4138]{0,1:T(8,128)(2,1)}), bf16[384,4138]{0,1:T(8,128)(2,1)}) %all-reduce.2.cloned.1.call-update) | async-done | bytes 3178000 | tf_op jit(solution)/shard_map/psum | solution.py:1064
  673.4 2.5 fusion.59
  675.9 2.3 copy.113
  678.2 2.3 copy.112
  680.5 2.5 fusion.58
  683.0 3.0 copy.114
  686.0 3.0 copy.111
  689.1 0.4 convert_element_type.130
  689.5 0.6 slice_reduce_fusion
  690.1 0.6 split.52
  (110 shorter events, 1.2 us)
Async XLA Ops:
  7.2 64.4 %all-gather.3.cloned.1.call-start = ((), (), s32[]{:S(2)}) async-start(), calls=%async_computation.1 | async-start | bytes 10321920 | tf_op jit(solution)/shard_map/all_gather | solution.py:1022
  8.1 3.9 copy-start.39
  8.1 4.1 copy-start.40
  8.1 4.2 copy-start.3
  8.1 63.4 %copy-start.29 = (f32[1536]{0:T(1024)S(1)}, f32[1536]{0:T(1024)}, u32[]{:S(2)}) copy-start(f32[1536]{0:T(1024)} %param.16) | copy-start | bytes 18436
  11.2 99.4 %all-gather.5.cloned.1.call-start = ((), (), s32[]{:S(2)}) async-start(), calls=%async_computation.2 | async-start | bytes 5898240 | tf_op jit(solution)/shard_map/all_gather | solution.py:1029
  11.9 525.5 %reduce-scatter.4.cloned.1.call-start = ((), (), s32[]{:S(2)}) async-start(), calls=%async_computation.4 | async-start | bytes 16220160
  12.1 104.5 %copy-start.24 = (pred[128,40]{1,0:T(32,128)(4,1)}, pred[128,40]{1,0:T(32,128)(4,1)S(1)}, u32[]{:S(2)}) copy-start(pred[128,40]{1,0:T(32,128)(4,1)S(1)} %copy.102) | copy-start | bytes 15364
  12.5 63.3 %copy-start.34 = (f32[128]{0:T(128)}, f32[128]{0:T(128)S(1)}, u32[]{:S(2)}) copy-start(f32[128]{0:T(128)S(1)} %add_rsqrt_fusion.1) | copy-start | bytes 1540
  12.7 67.5 %copy-start.18 = (f32[128,32]{0,1:T(8,128)}, f32[128,32]{0,1:T(8,128)S(1)}, u32[]{:S(2)}) copy-start(f32[128,32]{0,1:T(8,128)S(1)} %get-tuple-element.100) | copy-start | bytes 49156
  12.7 67.5 %copy-start.20 = (f32[128,32]{0,1:T(8,128)}, f32[128,32]{0,1:T(8,128)S(1)}, u32[]{:S(2)}) copy-start(f32[128,32]{0,1:T(8,128)S(1)} %get-tuple-element.101) | copy-start | bytes 49156
  75.8 4.6 copy-start.25
  75.8 4.6 copy-start.27
  80.3 0.8 copy-start.13
  80.3 0.8 copy-start.15
  80.8 1.1 copy-start.1
  81.1 32.7 %copy-start.22 = (f32[8,3,128]{2,1,0:T(4,128)}, f32[8,3,128]{2,1,0:T(4,128)S(1)}, u32[]{:S(2)}) copy-start(f32[8,3,128]{2,1,0:T(4,128)S(1)} %log_add_fusion) | copy-start | bytes 36868
  82.3 32.4 %copy-start.31 = (f32[1536]{0:T(1024)S(1)}, f32[1536]{0:T(1024)}, u32[]{:S(2)}) copy-start(f32[1536]{0:T(1024)} %param.21) | copy-start | bytes 18436
  113.8 0.9 copy-start.4
  113.9 2.4 copy-start.37
  114.9 2.3 copy-start.7
  116.3 0.5 copy-start.33
  116.6 0.5 copy-start.36
  334.1 6.2 copy-start.5
  334.1 6.2 copy-start.11
  334.1 6.2 copy-start.12
  334.1 6.2 copy-start.32
  334.1 6.2 copy-start.38
  341.4 8.0 %copy-start.2 = (f32[8,3,128,128]{2,3,1,0:T(8,128)S(1)}, f32[8,3,128,128]{2,3,1,0:T(8,128)}, u32[]{:S(2)}) copy-start(f32[8,3,128,128]{2,3,1,0:T(8,128)} %copy-done.1) | copy-start | bytes 4718596
  341.4 8.0 %copy-start.23 = (f32[8,3,128]{2,1,0:T(4,128)S(1)}, f32[8,3,128]{2,1,0:T(4,128)}, u32[]{:S(2)}) copy-start(f32[8,3,128]{2,1,0:T(4,128)} %copy-done.22) | copy-start | bytes 36868
  348.2 2.8 copy-start.6
  348.2 3.3 copy-start.14
  348.2 3.3 copy-start.16
  349.4 2.6 copy-start.26
  349.4 2.6 copy-start.28
  352.3 3.7 copy-start.19
  352.3 3.7 copy-start.21
  352.3 3.8 copy-start.30
  352.3 3.8 copy-start.35
  356.0 6.3 slice-start
  358.6 3.7 slice-start.1
  364.0 2.3 copy-start.17
  436.0 237.4 %all-reduce.2.cloned.1.call-start = ((), (), s32[]{:S(2)}) async-start(), calls=%async_computation.3 | async-start | bytes 6365184 | tf_op jit(solution)/shard_map/psum | solution.py:1064
  543.1 1.1 copy-start.8
  545.4 8.1 %copy-start.9 = (bf16[10,64,1536]{2,1,0:T(8,128)(2,1)S(1)}, bf16[10,64,1536]{2,1,0:T(8,128)(2,1)}, u32[]{:S(2)}) copy-start(bf16[10,64,1536]{2,1,0:T(8,128)(2,1)} %get-tuple-element.21) | copy-start | bytes 5898244
  545.4 8.1 %copy-start.10 = (bf16[1,10,64,1536]{3,2,1,0:T(8,128)(2,1)S(1)}, bf16[1,10,64,1536]{3,2,1,0:T(8,128)(2,1)}, u32[]{:S(2)}) copy-start(bf16[1,10,64,1536]{3,2,1,0:T(8,128)(2,1)} %get-tuple-element.22) | copy-start | bytes 5898244
  673.4 7.1 %copy-start = (bf16[384,4138]{0,1:T(8,128)(2,1)S(1)}, bf16[384,4138]{0,1:T(8,128)(2,1)}, u32[]{:S(2)}) copy-start(bf16[384,4138]{0,1:T(8,128)(2,1)} %all-reduce.2.cloned.1.call-done) | copy-start | bytes 9533956
Sparse Core Ops, SparseCore 0:
  11.3 60.2 all-gather.2
  73.1 37.4 all-gather.4
  436.1 101.3 reduce-scatter.3
  543.2 130.1 all-reduce.1

commit v2 on v1

--- a/solution.py
+++ b/solution.py
@@ -283,19 +283,23 @@
         self.a, self.b = self.e // self.side, self.e % self.side
         self.x, self.c = self.f // 2, self.f % 2
 
-    def others(self):
+    def others(self, all_fsdp):
         out = [((self.f, self.e + self.side), self.a < self.line - 1)]
         out.append(((self.f, self.e - self.side), self.a > 0))
         for i in range(1, self.side):
             out.append(((self.f, self.a * self.side + (self.b + i) % self.side), None))
+        if all_fsdp:
+            out += [(((self.f + i) % self.shards, self.e), None) for i in range(1, self.shards)]
+            return out
         out.append(((self.x * 2 + 1 - self.c, self.e), None))
         for i in range(1, self.chips):
             out.append((((self.x + i) % self.chips * 2 + self.c, self.e), None))
         return out
 
-    def meet(self):
+    def meet(self, all_fsdp=False):
         bar = pltpu.get_barrier_semaphore()
-        for dev, cond in self.others():
+        others = self.others(all_fsdp)
+        for dev, cond in others:
 
             def signal(dev=dev):
                 pl.semaphore_signal(bar, inc=1, device_id=dev, device_id_type=MESH)
@@ -304,10 +308,10 @@
                 signal()
             else:
                 pl.when(cond)(signal)
-        count = self.side - 1 + 1 + self.chips - 1
         pl.semaphore_wait(
             bar,
-            count
+            len(others)
+            - 2
             + jnp.where(self.a < self.line - 1, 1, 0)
             + jnp.where(self.a > 0, 1, 0),
         )
@@ -357,32 +361,35 @@
             self.across(at.e, i).start()
 
     def relay(self):
+        for s in range(1, self.at.line):
+            self.relay_step(s)
+
+    def relay_step(self, s):
         at = self.at
-        for s in range(1, at.line):
-
-            @pl.when(at.a - s >= 0)
-            def _(s=s):
-                k = at.e - s * at.side
-                self.down(k).wait_recv()
-
-                @pl.when(at.a < at.line - 1)
-                def _():
-                    self.up(k).start()
-
-                for i in range(1, at.side):
-                    self.across(k, i).start()
-
-            @pl.when(at.a + s < at.line)
-            def _(s=s):
-                k = at.e + s * at.side
-                self.up(k).wait_recv()
-
-                @pl.when(at.a > 0)
-                def _():
-                    self.down(k).start()
-
-                for i in range(1, at.side):
-                    self.across(k, i).start()
+
+        @pl.when(at.a - s >= 0)
+        def _():
+            k = at.e - s * at.side
+            self.down(k).wait_recv()
+
+            @pl.when(at.a < at.line - 1)
+            def _():
+                self.up(k).start()
+
+            for i in range(1, at.side):
+                self.across(k, i).start()
+
+        @pl.when(at.a + s < at.line)
+        def _():
+            k = at.e + s * at.side
+            self.up(k).wait_recv()
+
+            @pl.when(at.a > 0)
+            def _():
+                self.down(k).start()
+
+            for i in range(1, at.side):
+                self.across(k, i).start()
 
     def each(self, use):
         at = self.at
@@ -528,11 +535,294 @@
                 self.down(s).wait_send()
 
 
+def rope_of(allowed, tokens):
+    lane = lax.broadcasted_iota(jnp.int32, (tokens, 128), 1)
+    position = jnp.sum(allowed.astype(F32), axis=1, keepdims=True) - 1.0
+    half = HEAD_SIZE // 2
+    inverse = jnp.exp(-math.log(BASE) * (2.0 * (lane % half).astype(F32) / HEAD_SIZE))
+    angle = position * inverse
+    return jnp.cos(angle), jnp.sin(angle), lane % HEAD_SIZE < half
+
+
+def turn(x, cos, sin, first):
+    half = HEAD_SIZE // 2
+    other = jnp.where(first, -pltpu.roll(x, 128 - half, 1), pltpu.roll(x, half, 1))
+    return x * cos + other * sin
+
+
+def visible(doc, tokens):
+    row = lax.broadcasted_iota(jnp.int32, (tokens, tokens), 0)
+    col = lax.broadcasted_iota(jnp.int32, (tokens, tokens), 1)
+    key_doc = jnp.broadcast_to(doc.astype(F32), (tokens, tokens))
+    own = jnp.sum(jnp.where(row == col, key_doc, 0.0), axis=1, keepdims=True)
+    return (own == key_doc) & (col <= row)
+
+
+def attend_kernel(sizes, hidden, doc, routes, gain_a, gain_f, *refs):
+    shards, owners, tokens, experts = sizes
+    shares, cot = refs[:5], refs[5]
+    h1, q, k, v, mixed, lse, resid, sent, probs_out = refs[6:15]
+    fulls, cot_out = refs[15:20], refs[20]
+    (bufs, cot_all, acc, lsem, xs, xr, ys, yr, zs, zr, ss, sr, cs, cr) = refs[21:]
+    at = Place(shards, owners)
+    rg = MODEL_WIDTH // shards
+    half, quarter = rg // 2, rg // 4
+    f = at.f
+    sib = (at.x * 2 + 1 - at.c, at.e)
+    over = ((at.x + 1) % at.chips * 2 + at.c, at.e)
+    far = over[0]
+    mine = (at.a + at.b) % 2
+    beside = (f, at.a * at.side + (at.b + 1) % at.side)
+    step = jnp.where(at.a % 2 == 0, at.side, -at.side)
+    along = (f, at.e + step)
+    count = len(shares)
+
+    own = [pltpu.make_async_copy(shares[n], bufs[n].at[f], lsem.at[n]) for n in range(count)]
+    own.append(pltpu.make_async_copy(cot, cot_all.at[at.e], lsem.at[count]))
+    for c in own:
+        c.start()
+
+    def piece(n, g, start, size, send, recv, dev):
+        ref = bufs[n].at[g, pl.ds(pl.multiple_of(start, quarter), size)]
+        return remote(ref, ref, send, recv, dev)
+
+    def out_x(n):
+        start = pl.multiple_of(mine * half, half)
+        return remote(
+            shares[n].at[pl.ds(start, half)], bufs[n].at[f, pl.ds(start, half)],
+            xs.at[n], xr.at[n], over,
+        )
+
+    def in_x(n):
+        return piece(n, far, mine * half, half, xs.at[n], xr.at[n], over)
+
+    def out_y(n):
+        return piece(n, far, mine * half, quarter, ys.at[n], yr.at[n], beside)
+
+    def in_y(n):
+        return piece(n, far, (1 - mine) * half, quarter, ys.at[n], yr.at[n], beside)
+
+    def out_z(n):
+        return piece(n, far, mine * half + quarter, quarter, zs.at[n], zr.at[n], along)
+
+    def in_z(n):
+        return piece(n, far, (1 - mine) * half + quarter, quarter, zs.at[n], zr.at[n], along)
+
+    def to_sib(n, i, g):
+        start = (0, mine * half, (1 - mine) * half, (1 - mine) * half + quarter)[i]
+        size = (rg, half, quarter, quarter)[i]
+        return piece(n, g, start, size, ss.at[n, i], sr.at[n, i], sib)
+
+    def own_sib(n):
+        return remote(shares[n], bufs[n].at[f], ss.at[n, 0], sr.at[n, 0], sib)
+
+    at.meet()
+    for n in range(count):
+        out_x(n).start()
+        own_sib(n).start()
+    cotg = LineGather(at, cot_all, cs, cr)
+    own[count].wait()
+    cotg.begin()
+
+    x = hidden[...].astype(F32)
+    scale = lax.rsqrt(jnp.mean(x * x, axis=1, keepdims=True) + EPS)
+    h1[...] = (x * scale * gain_a[...]).astype(BF16)
+    allowed = visible(doc[...], tokens)
+    cos, sin, first = rope_of(allowed, tokens)
+
+    ends = (0, 1536, 2048, 2560)
+
+    def project(g):
+        part = h1[:, pl.ds(pl.multiple_of(g * rg, 128), rg)]
+        return [dot(part, bufs[n][g]) for n in range(3)]
+
+    for n in range(3):
+        own[n].wait()
+        acc[:, ends[n] : ends[n + 1]] = dot(
+            h1[:, pl.ds(pl.multiple_of(f * rg, 128), rg)], bufs[n][f]
+        )
+
+    def add(g):
+        for n, got in enumerate(project(g)):
+            acc[:, ends[n] : ends[n + 1]] += got
+
+    def pass_x(n):
+        in_x(n).wait_recv()
+        out_y(n).start()
+        out_z(n).start()
+        to_sib(n, 1, far).start()
+
+    def pass_rest(n):
+        in_y(n).wait_recv()
+        to_sib(n, 2, far).start()
+        in_z(n).wait_recv()
+        to_sib(n, 3, far).start()
+
+    def from_sib(n, first_part, g):
+        for i in (0,) if first_part else (1, 2, 3):
+            to_sib(n, i, g).wait_recv()
+
+    for n in range(3):
+        from_sib(n, True, sib[0])
+    add(sib[0])
+    for n in (1, 2):
+        pass_x(n)
+    cotg.relay_step(1)
+    pass_x(0)
+    cotg.relay_step(2)
+    for n in (1, 2, 0):
+        pass_rest(n)
+    add(far)
+    other = (at.x + 1) % at.chips * 2 + 1 - at.c
+    for n in range(3):
+        from_sib(n, False, other)
+    add(other)
+    for n in (3, 4):
+        pass_x(n)
+
+    for j in range(16):
+        cols = slice(128 * j, 128 * (j + 1))
+        got = turn(acc[:, cols], cos, sin, first).astype(BF16)
+        if j < 12:
+            q[:, cols] = got
+        else:
+            k[:, 128 * (j - 12) : 128 * (j - 11)] = got
+    v[...] = acc[:, 2048:].astype(BF16)
+    ratio = QUERY_HEADS // KEY_VALUE_HEADS
+    mask = jnp.concatenate([allowed] * ratio, axis=0)
+
+    def head(ref, h):
+        return ref[:, h * HEAD_SIZE : (h + 1) * HEAD_SIZE]
+
+    for g in range(KEY_VALUE_HEADS):
+        heads = range(g * ratio, (g + 1) * ratio)
+        rows = jnp.concatenate([head(q, h) for h in heads], axis=0)
+        s = jnp.where(mask, dot(rows, head(k, g), 1, 1) * SCORE_SCALE, MASKED)
+        top = jnp.max(s, axis=1, keepdims=True)
+        e = jnp.exp(s - top)
+        total = jnp.sum(e, axis=1, keepdims=True)
+        o = dot((e / total).astype(BF16), head(v, g)).astype(BF16)
+        log_total = top + jnp.log(total)
+        for i, h in enumerate(heads):
+            mixed[:, h * HEAD_SIZE : (h + 1) * HEAD_SIZE] = o[i * tokens : (i + 1) * tokens]
+            lse[:, h : h + 1] = log_total[i * tokens : (i + 1) * tokens]
+
+    cotg.relay_step(3)
+    for n in (3, 4):
+        pass_rest(n)
+    own[3].wait()
+    own[4].wait()
+    for n in (3, 4):
+        from_sib(n, True, sib[0])
+        from_sib(n, False, other)
+    total = x
+    for g in range(shards):
+        total = total + dot(mixed[:, g * rg : (g + 1) * rg], bufs[3][g])
+    resid[...] = total
+    scale = lax.rsqrt(jnp.mean(total * total, axis=1, keepdims=True) + EPS)
+    h2 = (total * scale * gain_f[...]).astype(BF16)
+    sent[:, :MODEL_WIDTH] = h2
+    logits = dot(h2[:, :rg], bufs[4][0])
+    for g in range(1, shards):
+        logits = logits + dot(h2[:, g * rg : (g + 1) * rg], bufs[4][g])
+    lane = lax.broadcasted_iota(jnp.int32, (tokens, 128), 1)
+    live = lane < experts
+    logits = jnp.where(live, logits, MASKED)
+    e = jnp.where(live, jnp.exp(logits - jnp.max(logits, axis=1, keepdims=True)), 0.0)
+    probs = e / jnp.sum(e, axis=1, keepdims=True)
+    probs_out[...] = probs
+    ids = routes[...]
+    chosen = lane == ids[:, :1]
+    for i in range(1, TOP):
+        chosen = chosen | (lane == ids[:, i : i + 1])
+    row = lax.broadcasted_iota(jnp.int32, (tokens, tokens), 0)
+    col = lax.broadcasted_iota(jnp.int32, (tokens, tokens), 1)
+    below = jnp.where(row > col, 1.0, 0.0).astype(BF16)
+    hits = jnp.where(chosen, 1.0, 0.0)
+    rank = jnp.where(chosen, dot(below, hits.astype(BF16)), jnp.where(live, -1.0, 0.0))
+    gate = jnp.where(chosen, probs, 0.0)
+    high = gate.astype(BF16).astype(F32)
+    low = gate - high
+    meta = rank + pltpu.roll(high, experts, 1) + pltpu.roll(low, 2 * experts, 1)
+    sent[:, MODEL_WIDTH:] = meta.astype(BF16)
+
+    save = [pltpu.make_async_copy(bufs[n], fulls[n], lsem.at[n]) for n in range(count)]
+    for c in save:
+        c.start()
+    cotg.each(lambda k: None)
+    cotg.finish()
+    keep = pltpu.make_async_copy(cot_all, cot_out, lsem.at[count])
+    keep.start()
+    for n in range(count):
+        out_x(n).wait_send()
+        own_sib(n).wait_send()
+        out_y(n).wait_send()
+        out_z(n).wait_send()
+        for i in (1, 2, 3):
+            to_sib(n, i, far).wait_send()
+    for c in save:
+        c.wait()
+    keep.wait()
+
+
+def attend(sizes, hidden, doc, routes, gain_a, gain_f, shares, cot):
+    shards, owners, tokens, experts = sizes
+    rg = MODEL_WIDTH // shards
+    side = owners // 4
+    vm, dma = pltpu.VMEM, pltpu.SemaphoreType.DMA
+    vmem, any_ = pl.BlockSpec(memory_space=pltpu.VMEM), pl.BlockSpec(memory_space=pl.ANY)
+    widths = [s.shape[1] for s in shares]
+    n = len(shares)
+
+    def shape(*dims, dtype=BF16):
+        return jax.ShapeDtypeStruct(dims, dtype)
+
+    outs = pl.pallas_call(
+        functools.partial(attend_kernel, sizes),
+        name="attend",
+        out_shape=(
+            shape(tokens, MODEL_WIDTH),
+            shape(tokens, MODEL_WIDTH),
+            shape(tokens, KEY_VALUE_HEADS * HEAD_SIZE),
+            shape(tokens, KEY_VALUE_HEADS * HEAD_SIZE),
+            shape(tokens, MODEL_WIDTH),
+            shape(tokens, 128, dtype=F32),
+            shape(tokens, MODEL_WIDTH, dtype=F32),
+            shape(tokens, MODEL_WIDTH + 128),
+            shape(tokens, 128, dtype=F32),
+            *[shape(shards, rg, w) for w in widths],
+            shape(owners, tokens, MODEL_WIDTH),
+        ),
+        in_specs=[vmem] * 5 + [any_] * (n + 1),
+        out_specs=[vmem] * 9 + [any_] * (n + 1),
+        scratch_shapes=[
+            tuple(vm((shards, rg, w), BF16) for w in widths),
+            vm((owners, tokens, MODEL_WIDTH), BF16),
+            vm((tokens, 2560), F32),
+            dma((n + 1,)),
+            dma((n,)),
+            dma((n,)),
+            dma((n,)),
+            dma((n,)),
+            dma((n,)),
+            dma((n,)),
+            dma((n, 4)),
+            dma((n, 4)),
+            dma((side + 1, owners)),
+            dma((owners,)),
+        ],
+        compiler_params=pltpu.CompilerParams(
+            collective_id=0, has_side_effects=True, vmem_limit_bytes=60 * 2**20
+        ),
+    )(hidden, doc, routes, gain_a[None], gain_f[None], *shares, cot)
+    return outs[:9], outs[9 : 9 + n], outs[9 + n]
+
+
 def moe_kernel(sizes, sent, cot, wgu, wd, comb_out, back_out, sums, far, *scratch):
     shards, owners, tokens, experts, held, pairing = sizes
     (rows_all, cot_all, taken, cots, slot_gate, place, wg_buf, wd_buf, gg, gd, from_core, to_far,
      own_sum, z_acc, dx_acc, dg_acc, side1, line1, side2, line2, own2,
-     rs, rr, cs, cr, wsem, coresend, corerecv, farsend, farrecv, osem, free, s1, s2, s3, s4, t1, t2, t3, t4,
+     rs, rr, wsem, coresend, corerecv, farsend, farrecv, osem, free, s1, s2, s3, s4, t1, t2, t3, t4,
      ) = scratch
     at = Place(shards, owners)
     groups = held // pairing
@@ -551,16 +841,14 @@
         c.start()
     at.meet()
     rows = LineGather(at, rows_all, rs, rr)
-    cotg = LineGather(at, cot_all, cs, cr)
     c1 = pltpu.make_async_copy(sent, rows_all.at[at.e], osem.at[0, 0])
-    c2 = pltpu.make_async_copy(cot, cot_all.at[at.e], osem.at[0, 1])
+    c2 = pltpu.make_async_copy(cot, cot_all, osem.at[0, 1])
     c1.start()
     c2.start()
     c1.wait()
     rows.begin()
     rows.relay()
     c2.wait()
-    cotg.begin()
 
     lane = lax.broadcasted_iota(jnp.int32, (128, slots), 1)
     row = lax.broadcasted_iota(jnp.int32, (128, slots), 0)
@@ -594,8 +882,12 @@
             cots[g, to, :] = got[g * CAP : (g + 1) * CAP]
 
     rows.each(dispatch_rows)
-    cotg.relay()
-    cotg.each(dispatch_cot)
+
+    def dispatch_all(k, carry):
+        dispatch_cot(k)
+        return carry
+
+    lax.fori_loop(0, owners, dispatch_all, 0)
 
     def to_core(h, slot):
         out = []
@@ -730,7 +1022,6 @@
     add(held - 1, (held - 1) % 2)
 
     rows.finish()
-    cotg.finish()
 
     home = (col == e_row).astype(F32).astype(BF16)
     home_low = (col == e_row + experts).astype(F32).astype(BF16)
@@ -832,8 +1123,6 @@
             vm((tokens, MODEL_WIDTH), F32),
             dma((side + 1, owners)),
             dma((owners,)),
-            dma((side + 1, owners)),
-            dma((owners,)),
             dma((2, 2)),
             dma((2, 2, chips)),
             dma((2, 2, chips)),
@@ -848,6 +1137,263 @@
             collective_id=1, has_side_effects=True, vmem_limit_bytes=63 * 2**20
         ),
     )(sent, cot, wgu, wd)
+
+
+def grads_kernel(sizes, h1, mixed, right, aux, out, *scratch):
+    shards, owners, tokens = sizes
+    (left, rights, aux_in, turned, part, side_in, line_in, own, total,
+     lsem, rsem, asem, lsend, lrecv, rsend, rrecv, asend, arecv, s1, s2, s3, s4, gs, gr) = scratch
+    at = Place(shards, owners)
+    rg = MODEL_WIDTH // shards
+    piece = rg // owners
+    wide = right.shape[1]
+    split = wide - MODEL_WIDTH
+    f = at.f
+    sibling = (at.x * 2 + 1 - at.c, at.e)
+
+    def rows(i):
+        return pl.ds(pl.multiple_of(i * tokens, tokens), tokens)
+
+    def cols(i):
+        return pl.ds(pl.multiple_of(i * rg, rg), rg)
+
+    own_rights = pltpu.make_async_copy(right, rights.at[rows(f)], rsem)
+    own_rights.start()
+    local = [
+        pltpu.make_async_copy(h1.at[:, cols(f)], left.at[rows(f), pl.ds(0, rg)], lsem.at[0]),
+        pltpu.make_async_copy(mixed.at[:, cols(f)], left.at[rows(f), pl.ds(rg, rg)], lsem.at[1]),
+        pltpu.make_async_copy(aux.at[:, cols(f)], aux_in.at[0], asem),
+    ]
+    for c in local:
+        c.start()
+    at.meet(all_fsdp=True)
+
+    def block(g, send, dev):
+        return remote(rights.at[rows(g)], rights.at[rows(g)], rsend.at[send], rrecv.at[g], dev)
+
+    def lefts(i):
+        g = (f + i) % shards
+        dev = (g, at.e)
+        return (
+            remote(h1.at[:, cols(g)], left.at[rows(f), pl.ds(0, rg)],
+                   lsend.at[0, i - 1], lrecv.at[0, i - 1], dev),
+            remote(mixed.at[:, cols(g)], left.at[rows(f), pl.ds(rg, rg)],
+                   lsend.at[1, i - 1], lrecv.at[1, i - 1], dev),
+            remote(aux.at[:, cols(g)], aux_in.at[i], asend.at[i - 1], arecv.at[i - 1], dev),
+        )
+
+    own_rights.wait()
+    away = [(((at.x + i) % at.chips) * 2 + at.c) for i in range(1, at.chips)]
+    direct = [block(f, 0, sibling)]
+    direct += [block(f, 1 + n, (g, at.e)) for n, g in enumerate(away)]
+    for c in direct:
+        c.start()
+    sent = [c for i in range(1, shards) for c in lefts(i)]
+    for c in sent:
+        c.start()
+    passed = []
+    for n, g in enumerate(away):
+        block(g, 0, sibling).wait_recv()
+        c = block(g, at.chips + n, sibling)
+        c.start()
+        passed.append(c)
+    for c in local:
+        c.wait()
+    for c in sent:
+        c.wait_recv()
+    turned[...] = left[...].T
+    extra = aux_in[0]
+    for i in range(1, shards):
+        extra = extra + aux_in[i]
+    extra = extra.T.astype(BF16)
+    block(at.x * 2 + 1 - at.c, 0, sibling).wait_recv()
+    for n in range(1, at.chips):
+        block(((at.x + n) % at.chips) * 2 + 1 - at.c, 0, sibling).wait_recv()
+    step = 512
+    for n in range(wide // step):
+        lhs = turned[:rg] if n * step < split else turned[rg:]
+        got = dot(lhs, rights[:, n * step : (n + 1) * step]).astype(BF16)
+        for k in range(owners):
+            part[k, :, n * step : (n + 1) * step] = got[k * piece : (k + 1) * piece]
+    for k in range(owners):
+        part[k, :, wide : wide + aux.shape[0]] = extra[k * piece : (k + 1) * piece]
+    scatter = LineScatter(at, part, side_in, line_in, own, (s1, s2, s3, s4))
+    scatter.begin(lambda k: None)
+    scatter.sum()
+    gather = LineGather(at, total, gs, gr)
+    total[at.e] = own[...].astype(BF16)
+    gather.begin()
+    gather.relay()
+    gather.each(lambda k: None)
+    out[...] = total[...]
+    for c in direct + sent + passed:
+        c.wait_send()
+    scatter.finish()
+    gather.finish()
+
+
+def sum_grads(sizes, h1, mixed, right, aux):
+    shards, owners, tokens = sizes
+    rg = MODEL_WIDTH // shards
+    piece = rg // owners
+    chips = shards // 2
+    wide, extra = right.shape[1], aux.shape[0]
+    full = wide + 128
+    line = 4
+    side = owners // line
+    vm, dma = pltpu.VMEM, pltpu.SemaphoreType.DMA
+    vmem = pl.BlockSpec(memory_space=pltpu.VMEM)
+    return pl.pallas_call(
+        functools.partial(grads_kernel, sizes),
+        name="grads",
+        out_shape=jax.ShapeDtypeStruct((owners, piece, full), BF16),
+        in_specs=[vmem] * 4,
+        out_specs=vmem,
+        scratch_shapes=[
+            vm((shards * tokens, 2 * rg), BF16),
+            vm((shards * tokens, wide), BF16),
+            vm((shards, extra, rg), F32),
+            vm((2 * rg, shards * tokens), BF16),
+            vm((owners, piece, full), BF16),
+            vm((line, side - 1, piece, full), BF16),
+            vm((line + 1, piece, full), BF16),
+            vm((piece, full), F32),
+            vm((owners, piece, full), BF16),
+            dma((2,)),
+            dma,
+            dma,
+            dma((2, shards - 1)),
+            dma((2, shards - 1)),
+            dma((2 * chips,)),
+            dma((shards,)),
+            dma((shards - 1,)),
+            dma((shards - 1,)),
+            dma((line, side)),
+            dma((line, side)),
+            dma((line,)),
+            dma((line + 1,)),
+            dma((side + 1, owners)),
+            dma((owners,)),
+        ],
+        compiler_params=pltpu.CompilerParams(
+            collective_id=2, has_side_effects=True, vmem_limit_bytes=60 * 2**20
+        ),
+    )(h1, mixed, right, aux)
+
+
+def backward_rows(
+    state,
+    route_rows,
+    cot_rows,
+    grad_ffn_in,
+    grad_gates,
+    gain_attn,
+    w_query,
+    key_matrix,
+    value_matrix,
+    w_output,
+    gain_ffn,
+    w_router,
+):
+    (
+        normed_attn,
+        scale_attn,
+        attention_input,
+        cosine_table,
+        sine_table,
+        allowed,
+        query_rows,
+        key_rows,
+        value_rows,
+        attention_mixed,
+        log_total,
+        resid,
+        ffn_in,
+        normed_ffn,
+        scale_ffn,
+        probs,
+        gates,
+    ) = state
+    document_length = attention_input.shape[0]
+    query_group = QUERY_HEADS // KEY_VALUE_HEADS
+    grad_probs = jnp.where(route_rows, grad_gates, 0.0)
+    grad_logits = (
+        probs * (grad_probs - jnp.sum(probs * grad_probs, axis=-1, keepdims=True))
+    ).astype(jnp.bfloat16)
+    grad_router = jnp.dot(grad_logits.T, ffn_in, preferred_element_type=jnp.float32)
+    grad_ffn_in = grad_ffn_in + jnp.dot(grad_logits, w_router.T, preferred_element_type=jnp.float32)
+    grad_resid_part, grad_gain_ffn = norm_backward(grad_ffn_in, normed_ffn, scale_ffn, gain_ffn)
+    grad_resid = cot_rows.astype(jnp.float32) + grad_resid_part
+    grad_attn = grad_resid.astype(jnp.bfloat16)
+    mixed_gradient = jnp.dot(grad_attn, w_output.T, preferred_element_type=jnp.float32).astype(
+        jnp.bfloat16
+    )
+    scores = scores_of(query_rows, key_rows, allowed)
+    weights = jnp.exp(scores - log_total)
+    weights_low = weights.astype(jnp.bfloat16)
+    gradient_by_group = mixed_gradient.reshape(
+        document_length, KEY_VALUE_HEADS, query_group, HEAD_SIZE
+    )
+    mixed_by_group = attention_mixed.reshape(
+        document_length, KEY_VALUE_HEADS, query_group, HEAD_SIZE
+    )
+    value_gradients = jnp.einsum(
+        "grqk,qgrd->kgd", weights_low, gradient_by_group, preferred_element_type=jnp.float32
+    )
+    grad_weights = jnp.einsum(
+        "qgrd,kgd->grqk", gradient_by_group, value_rows, preferred_element_type=jnp.float32
+    )
+    delta = jnp.transpose(
+        jnp.sum(
+            gradient_by_group.astype(jnp.float32) * mixed_by_group.astype(jnp.float32), axis=-1
+        ),
+        (1, 2, 0),
+    )
+    grad_scores = (weights * (grad_weights - delta[..., None]) * SCORE_SCALE).astype(jnp.bfloat16)
+    query_by_group = query_rows.reshape(document_length, KEY_VALUE_HEADS, query_group, HEAD_SIZE)
+    grad_query_rows = jnp.einsum(
+        "grqk,kgd->qgrd", grad_scores, key_rows, preferred_element_type=jnp.float32
+    ).reshape(document_length, QUERY_HEADS, HEAD_SIZE)
+    key_row_gradient = jnp.einsum(
+        "grqk,qgrd->kgd", grad_scores, query_by_group, preferred_element_type=jnp.float32
+    )
+    grad_query_rows = (
+        inverse_rotation(grad_query_rows, cosine_table, sine_table)
+        .reshape(document_length, QUERY_HEADS * HEAD_SIZE)
+        .astype(jnp.bfloat16)
+    )
+    key_row_gradient = (
+        inverse_rotation(key_row_gradient, cosine_table, sine_table)
+        .reshape(document_length, KEY_VALUE_HEADS * HEAD_SIZE)
+        .astype(jnp.bfloat16)
+    )
+    value_row_gradient = value_gradients.reshape(
+        document_length, KEY_VALUE_HEADS * HEAD_SIZE
+    ).astype(jnp.bfloat16)
+    grad_attn_in = jnp.dot(grad_query_rows, w_query.T, preferred_element_type=jnp.float32)
+    grad_attn_in = grad_attn_in + jnp.dot(
+        key_row_gradient, key_matrix.T, preferred_element_type=jnp.float32
+    )
+    grad_attn_in = grad_attn_in + jnp.dot(
+        value_row_gradient, value_matrix.T, preferred_element_type=jnp.float32
+    )
+    grad_hidden_part, grad_gain_attn = norm_backward(
+        grad_attn_in, normed_attn, scale_attn, gain_attn
+    )
+    grad_in = grad_resid + grad_hidden_part
+    right = jnp.concatenate(
+        [grad_query_rows, key_row_gradient, value_row_gradient, grad_attn], axis=1
+    )
+    aux = jnp.concatenate(
+        [
+            grad_router,
+            grad_gain_attn[None],
+            grad_gain_ffn[None],
+            jnp.zeros((128 - 2 - grad_router.shape[0], MODEL_WIDTH), jnp.float32),
+        ],
+        axis=0,
+    )
+    return grad_in, right, aux
 
 
 def plain_local(
@@ -1019,33 +1565,50 @@
     pairing = 2 if held % 2 == 0 else 1
     f32, bf16 = jnp.float32, jnp.bfloat16
 
-    first = lax.all_gather(
-        jnp.concatenate([w_query, key_matrix, value_matrix, w_router], axis=1),
-        "fsdp",
-        axis=0,
-        tiled=True,
-    )
-    full_query, full_key, full_value, full_router = jnp.split(first, (1536, 2048, 2560), axis=1)
-    full_output = lax.all_gather(w_output, "fsdp", axis=0, tiled=True)
+    router = jnp.concatenate(
+        [w_router, jnp.zeros((w_router.shape[0], 128 - experts), bf16)], axis=1
+    )
+    shares = (w_query, key_matrix, value_matrix, w_output, router)
+    made, fulls, cot_all = attend(
+        (shards, owners, tokens, experts), hidden_in, doc_ids, routes, gain_attn, gain_ffn, shares,
+        cotangent,
+    )
+    h1, q, k, v, mixed, lse, resid, sent, probs = made
+    full_query, full_key, full_value, full_output, full_router = (
+        w.reshape(MODEL_WIDTH, -1) for w in fulls
+    )
+    full_router = full_router[:, :experts]
+    probs = probs[:, :experts]
     weights_attn = (gain_attn, full_query, full_key, full_value, full_output, gain_ffn, full_router)
-    state = forward_local(hidden_in, doc_ids[0], routes, *weights_attn)
-    resid, ffn_in, probs = state[11], state[12], state[15]
-
     chosen = jnp.any(
         routes[:, :, None] == jnp.arange(experts, dtype=jnp.int32)[None, None, :], axis=1
     )
-    below = jnp.tril(jnp.ones((tokens, tokens), bf16), -1)
-    rank = jnp.dot(below, chosen.astype(bf16), preferred_element_type=f32)
-    rank = jnp.where(chosen, rank, -1.0)
-    gate = jnp.where(chosen, probs, 0.0)
-    gate_high = gate.astype(bf16)
-    gate_low = (gate - gate_high.astype(f32)).astype(bf16)
-    meta = jnp.concatenate([rank.astype(bf16), gate_high, gate_low], axis=1)
-    sent = jnp.concatenate(
-        [ffn_in, meta, jnp.zeros((tokens, 128 - 3 * experts), bf16)], axis=1
+    ffn_in = sent[:, :MODEL_WIDTH]
+    _, normed_attn, scale_attn = norm_forward(hidden_in.astype(f32), gain_attn)
+    _, normed_ffn, scale_ffn = norm_forward(resid, gain_ffn)
+    cosine, sine, allowed = rope_tables(doc_ids[0])
+    ratio = QUERY_HEADS // KEY_VALUE_HEADS
+    state = (
+        normed_attn,
+        scale_attn,
+        h1,
+        cosine,
+        sine,
+        allowed,
+        q.reshape(tokens, QUERY_HEADS, HEAD_SIZE),
+        k.reshape(tokens, KEY_VALUE_HEADS, HEAD_SIZE),
+        v.reshape(tokens, KEY_VALUE_HEADS, HEAD_SIZE),
+        mixed,
+        lse[:, :QUERY_HEADS].T.reshape(KEY_VALUE_HEADS, ratio, tokens, 1),
+        resid,
+        ffn_in,
+        normed_ffn,
+        scale_ffn,
+        probs,
+        None,
     )
     sizes = (shards, owners, tokens, experts, held, pairing)
-    combined, back, sums, far = moe(sizes, sent, cotangent, w_gateup, w_down)
+    combined, back, sums, far = moe(sizes, sent, cot_all, w_gateup, w_down)
     block_out = (resid + combined).astype(bf16)
     grad_ffn = back[:, :MODEL_WIDTH]
     grad_gate_dense = (
@@ -1055,22 +1618,32 @@
     grad_gateup, grad_down = (
         s.astype(f32) + jnp.sum(r.astype(f32), axis=0) for s, r in zip(sums, far)
     )
-    grad_input, grads = backward_local(
+    grad_input, right, aux = backward_rows(
         state, chosen, cotangent, grad_ffn, grad_gate_dense, *weights_attn
     )
-    widths = [g.shape[1] if g.ndim == 2 else 1 for g in grads]
-    flat = jnp.concatenate([g if g.ndim == 2 else g[:, None] for g in grads], axis=1)
-    share = lax.psum_scatter(flat.astype(bf16), "fsdp", scatter_dimension=0, tiled=True)
-    total = lax.psum(share, "expert").astype(f32)
-    pieces = jnp.split(total, [sum(widths[: i + 1]) for i in range(len(widths) - 1)], axis=1)
-    pieces = [p if g.ndim == 2 else p[:, 0] for p, g in zip(pieces, grads)]
-    return (block_out, grad_input, *pieces, grad_gateup, grad_down)
+    total = sum_grads((shards, owners, tokens), state[2], state[9], right, aux)
+    total = total.reshape(MODEL_WIDTH // shards, -1).astype(f32)
+    ends = (1536, 2048, 2560, 4096, 4096 + experts)
+    grad_query, grad_key, grad_value, grad_output, grad_router, rest = jnp.split(total, ends, axis=1)
+    return (
+        block_out,
+        grad_input,
+        grad_query,
+        grad_key,
+        grad_value,
+        grad_output,
+        grad_router,
+        rest[:, 0],
+        rest[:, 1],
+        grad_gateup,
+        grad_down,
+    )
 
 
 def local(*args):
     owners, held = lax.axis_size("expert"), args[10].shape[0]
     groups = held // (2 if held % 2 == 0 else 1)
-    if owners * groups * CAP <= 2048 and owners % 4 == 0:
+    if lax.axis_size("fsdp") == 4 and owners == 8 and owners * groups * CAP <= 2048:
         return kernel_local(*args)
     return plain_local(*args)
 

time: 700 us -> 447 us (0.64)
  waiting for transfers between devices: 306 us -> 0 us
  Pallas kernels: 216 us -> 383 us
  local copies, waits for them, and re-layouts: 99.5 us -> 23.4 us
  matrix products: 39.2 us -> 15.5 us
  between operations: 14.6 us -> 1.2 us
    pallas_call x0 -> x2, Pallas kernels: none -> 194 us  [the longest x1 117 us: sum_grads(): pl.pallas_call(functools.partial(grads_kernel, sizes), name='grads', out_...]
    psum x1 -> x0, waiting for transfers between devices: 117 us -> none  [kernel_local(): total = lax.psum(share, 'expert').astype(f32)]
    unnamed x5 -> x0, waiting for transfers between devices: 102 us -> none
    all_gather x2 -> x0, waiting for transfers between devices: 86.9 us -> none  [the longest x1 58.6 us: kernel_local(): lax.all_gather(jnp.concatenate([w_query, key_matrix, value_matrix, w_rout...]
    concatenate x2, local copies, waits for them, and re-layouts: 54.1 us -> 0.74 us  [the longest x1 0.67 us: kernel_local(): jnp.concatenate([w_router, jnp.zeros((w_router.shape[0], 128 - experts),...]
    unnamed x93 -> x61, local copies, waits for them, and re-layouts: 36.9 us -> 7.14 us
    pallas_call x1, Pallas kernels: 216 us -> 189 us  [moe(): pl.pallas_call(functools.partial(moe_kernel, sizes), name='moe', out_shap...]
    dot_general x21 -> x10, matrix products: 38.7 us -> 14 us  [the longest x1 4.12 us: backward_rows(): jnp.dot(grad_query_rows, w_query.T, preferred_element_type=jnp.float32)]
  transfers between devices with their start and end apart: 4 -> 0, of which waited for: 4 -> 0; matrix products, arithmetic and copies ran while one was open for 3% -> 0% of each run, Pallas kernels for 0% -> 0%
where the time goes in v2:
time: 447 us; the launch traced here: 444 us
  Pallas kernels  383 us (86%)
  local copies, waits for them, and re-layouts  23.4 us (5%)
  other arithmetic  20.7 us (5%)
  matrix products  15.5 us (3%)
    pallas_call x1, Pallas kernels, moe(): pl.pallas_call(functools.partial(moe_kernel, sizes), name='moe', out_shap...  189 us
    pallas_call x1, Pallas kernels, sum_grads(): pl.pallas_call(functools.partial(grads_kernel, sizes), name='grads', out_...  117 us
    pallas_call x1, Pallas kernels, attend(): pl.pallas_call(functools.partial(attend_kernel, sizes), name='attend', ou...  76.9 us

profile of v2, /device:TPU:0, one launch (start us, length us, event | category | flops | bytes accessed | tf_op | source)
XLA Modules:
  0.0 443.9 jit_solution(5694929983411305076)
XLA Ops:
  0.6 0.9 copy.61
  1.5 0.7 concatenate.15.refs_4_
  2.2 1.4 copy.62.routes
  3.6 1.3 broadcast_in_dim.36.gain_a
  4.9 1.3 broadcast_in_dim.37.gain_f
  6.2 76.9 %attend.1 = (bf16[128,1536]{1,0:T(8,128)(2,1)}, bf16[128,1536]{1,0:T(8,128)(2,1)}, bf16[128,512]{1,0:T(8,128)(2,1)}, bf16[128,512]{1,0:T(8,128)(2,1)}, bf16[128,...) custom-call(bf16[128,1536]{1,0:T(8,128)(2,1)} %hidden.1, ...), custom_call_target="tpu_custom_call" | custom-call | tf_op jit(solution)/shard_map/attend/pallas_call | solution.py:780
  83.1 0.0 copy-start.27
  83.1 188.9 %moe.1 = (f32[128,1536]{1,0:T(8,128)}, f32[128,1664]{1,0:T(8,128)}, bf16[10,384,512]{2,1,0:T(8,128)(2,1)}, bf16[10,64,1536]{2,1,0:T(8,128)(2,1)}, bf16[1,10,384,...) custom-call(bf16[128,1664]{1,0:T(8,128)(2,1)} %get-tuple-element.33.sent, ...), custom_call_target="tpu_custom_call" | custom-call | tf_op jit(solution)/shard_map/moe/pallas_call | solution.py:1091
  272.0 0.1 copy.63
  272.2 1.1 multiply_reduce_fusion.4
  273.3 0.0 copy-start.8
  273.3 1.0 multiply_convert_fusion
  274.3 0.1 multiply_reduce_fusion.3
  274.5 1.2 fusion.14
  275.7 1.6 multiply_reduce_fusion
  277.3 0.3 fusion.21
  277.6 0.6 copy-done.5
  278.1 1.6 convolution_convert_fusion
  279.8 0.9 copy.68
  280.7 0.9 copy.65
  281.6 0.1 copy.64
  281.8 0.0 copy-start.19
  281.8 0.1 copy.66
  281.9 0.1 compare_and_fusion
  282.0 0.4 copy-done.19
  282.4 1.5 fusion.4
  283.9 0.0 copy-start.2
  283.9 0.5 fusion.5
  284.4 2.1 copy.69
  286.5 1.3 multiply_reduce_fusion.1
  287.8 1.0 copy.67
  288.9 0.0 copy-start.20
  288.9 2.0 fusion.2
  290.9 1.5 convolution_bitcast_fusion.1
  292.4 0.1 fusion.20
  292.5 0.1 multiply_cosine_fusion
  292.7 0.3 fusion.24
  293.0 0.1 multiply_add_fusion.1
  293.2 4.1 fusion.25
  297.3 0.0 copy-start.3
  297.3 0.0 copy-start.25
  297.3 0.7 convolution_add_fusion.1
  298.0 0.3 copy-done.3
  298.3 0.5 copy-done.16
  298.8 1.6 fusion.13
  300.5 0.2 fusion.17
  300.7 0.1 pad.4.clone
  300.8 1.0 maximum_maximum_fusion.aux
  301.8 0.8 copy.75
  302.6 0.1 copy.74
  302.7 0.2 copy.73
  302.9 2.0 pad_maximum_fusion.right
  304.9 117.5 %grads.1 = bf16[8,48,4224]{2,1,0:T(8,128)(2,1)} custom-call(bf16[128,1536]{1,0:T(8,128)(2,1)} %get-tuple-element.48.h1, bf16[128,1536]{1,0:T(8,128)(2,1)} %get-tuple-element.44.mixed, bf16[128,4096]{1,0:T(8,128)(2,1)} %pad_maximum_fusion.right, f32[128,1536]{1,0:T(8,128)} %maximum_maximum_fusion.aux), custom_call_target="tpu_custom_call" | custom-call | tf_op jit(solution)/shard_map/grads/pallas_call | solution.py:1246
  422.4 2.3 bitcast_convert_fusion
  424.7 3.3 fusion.22
  428.0 1.4 fusion.23
  429.3 0.1 copy-done
  429.4 0.7 copy.84
  430.2 1.9 slice_reduce_fusion
  432.1 2.6 fusion.12
  434.7 2.6 convert_add_fusion.1
  437.3 0.9 copy-done.6
  438.2 1.2 copy-done.7
  439.5 4.5 %convert_add_fusion = f32[10,384,512]{2,1,0:T(8,128)} fusion(bf16[10,384,512]{2,1,0:T(8,128)(2,1)S(1)} %copy-done.6, bf16[1,10,384,512]{3,2,1,0:T(8,128)(2,1)S(1)} %copy-done.7), kind=kLoop, calls=%fused_computation | loop fusion | flops 5898240 | bytes 15728640 | tf_op jit(solution)/shard_map/add | solution.py:1619
  (59 shorter events, 0.3 us)
Async XLA Ops:
  83.1 188.9 %copy-start.27 = (s32[128,8]{0,1:T(8,128)S(1)}, s32[128,8]{0,1:T(8,128)}, u32[]{:S(2)}) copy-start(s32[128,8]{0,1:T(8,128)} %param.15) | copy-start | bytes 12292
  83.1 189.1 %copy-start.22 = (f32[128,128]{1,0:T(8,128)S(1)}, f32[128,128]{1,0:T(8,128)}, u32[]{:S(2)}) copy-start(f32[128,128]{1,0:T(8,128)} %get-tuple-element.37) | copy-start | bytes 196612
  83.1 191.3 %copy-start.1 = (f32[128,1536]{1,0:T(8,128)S(1)}, f32[128,1536]{1,0:T(8,128)}, u32[]{:S(2)}) copy-start(f32[128,1536]{1,0:T(8,128)} %get-tuple-element.32) | copy-start | bytes 2359300
  83.1 192.6 %copy-start.23 = (f32[1536]{0:T(1024)S(1)}, f32[1536]{0:T(1024)}, u32[]{:S(2)}) copy-start(f32[1536]{0:T(1024)} %param.21) | copy-start | bytes 18436
  272.0 3.7 copy-start.18
  273.3 4.0 copy-start.8
  275.7 2.5 copy-start.5
  277.5 2.2 copy-start.10
  278.1 2.6 copy-start.21
  278.1 3.5 copy-start.24
  278.1 3.6 copy-start.26
  278.1 3.8 copy-start.28
  281.8 0.7 copy-start.19
  281.9 2.0 copy-start.4
  283.9 5.0 %copy-start.2 = (f32[8,3,128,128]{2,3,1,0:T(8,128)}, f32[8,3,128,128]{2,3,1,0:T(8,128)S(1)}, u32[]{:S(2)}) copy-start(f32[8,3,128,128]{2,3,1,0:T(8,128)S(1)} %fusion.4) | copy-start | bytes 4718596
  288.9 3.8 copy-start.20
  293.2 4.2 copy-start.17
  297.3 1.0 copy-start.3
  297.3 1.5 copy-start.16
  297.3 1.5 copy-start.25
  298.0 2.5 copy-start.15
  300.4 2.4 copy-start.11
  424.7 4.7 %copy-start = (f32[384,4224]{1,0:T(8,128)}, f32[384,4224]{1,0:T(8,128)S(1)}, u32[]{:S(2)}) copy-start(f32[384,4224]{1,0:T(8,128)S(1)} %bitcast_convert_fusion) | copy-start | bytes 19464196
  428.0 4.1 copy-start.9
  428.0 4.1 copy-start.12
  432.1 2.6 copy-start.13
  432.1 2.6 copy-start.14
  434.7 3.5 copy-start.6
  434.7 4.7 %copy-start.7 = (bf16[1,10,384,512]{3,2,1,0:T(8,128)(2,1)S(1)}, bf16[1,10,384,512]{3,2,1,0:T(8,128)(2,1)}, u32[]{:S(2)}) copy-start(bf16[1,10,384,512]{3,2,1,0:T(8,128)(2,1)} %get-tuple-element.50) | copy-start | bytes 11796484

commit v3 on v1

--- a/solution.py
+++ b/solution.py
@@ -283,19 +283,23 @@
         self.a, self.b = self.e // self.side, self.e % self.side
         self.x, self.c = self.f // 2, self.f % 2
 
-    def others(self):
+    def others(self, all_fsdp):
         out = [((self.f, self.e + self.side), self.a < self.line - 1)]
         out.append(((self.f, self.e - self.side), self.a > 0))
         for i in range(1, self.side):
             out.append(((self.f, self.a * self.side + (self.b + i) % self.side), None))
+        if all_fsdp:
+            out += [(((self.f + i) % self.shards, self.e), None) for i in range(1, self.shards)]
+            return out
         out.append(((self.x * 2 + 1 - self.c, self.e), None))
         for i in range(1, self.chips):
             out.append((((self.x + i) % self.chips * 2 + self.c, self.e), None))
         return out
 
-    def meet(self):
+    def meet(self, all_fsdp=False):
         bar = pltpu.get_barrier_semaphore()
-        for dev, cond in self.others():
+        others = self.others(all_fsdp)
+        for dev, cond in others:
 
             def signal(dev=dev):
                 pl.semaphore_signal(bar, inc=1, device_id=dev, device_id_type=MESH)
@@ -304,10 +308,10 @@
                 signal()
             else:
                 pl.when(cond)(signal)
-        count = self.side - 1 + 1 + self.chips - 1
         pl.semaphore_wait(
             bar,
-            count
+            len(others)
+            - 2
             + jnp.where(self.a < self.line - 1, 1, 0)
             + jnp.where(self.a > 0, 1, 0),
         )
@@ -322,98 +326,113 @@
 class LineGather:
     def __init__(self, at, buf, send, recv):
         self.at, self.buf, self.send, self.recv = at, buf, send, recv
-
-    def up(self, k):
+        width, count = buf.shape[2], recv.shape[0]
+        cut = [width * p // count // 128 * 128 for p in range(count)] + [width]
+        self.parts = [pl.ds(lo, hi - lo) for lo, hi in zip(cut, cut[1:])]
+
+    def copy(self, k, p, way, dev):
+        ref = self.buf.at[k, :, self.parts[p]]
+        return remote(ref, ref, self.send.at[p, way, k], self.recv.at[p, k], (self.at.f, dev))
+
+    def up(self, k, p):
+        return self.copy(k, p, 0, self.at.e + self.at.side)
+
+    def down(self, k, p):
+        return self.copy(k, p, 1, self.at.e - self.at.side)
+
+    def across(self, k, i, p):
         at = self.at
-        return remote(
-            self.buf.at[k], self.buf.at[k], self.send.at[0, k], self.recv.at[k], (at.f, at.e + at.side)
-        )
-
-    def down(self, k):
+        return self.copy(k, p, 1 + i, at.a * at.side + (at.b + i) % at.side)
+
+    def spread(self, k, p, up, down):
         at = self.at
-        return remote(
-            self.buf.at[k], self.buf.at[k], self.send.at[1, k], self.recv.at[k], (at.f, at.e - at.side)
-        )
-
-    def across(self, k, i):
+        if up:
+
+            @pl.when(at.a < at.line - 1)
+            def _():
+                self.up(k, p).start()
+
+        if down:
+
+            @pl.when(at.a > 0)
+            def _():
+                self.down(k, p).start()
+
+        for i in range(1, at.side):
+            self.across(k, i, p).start()
+
+    def begin(self):
+        for p in range(len(self.parts)):
+            self.spread(self.at.e, p, True, True)
+
+    def relay_step(self, s):
         at = self.at
-        dev = (at.f, at.a * at.side + (at.b + i) % at.side)
-        return remote(
-            self.buf.at[k], self.buf.at[k], self.send.at[1 + i, k], self.recv.at[k], dev
-        )
-
-    def begin(self):
-        at = self.at
-
-        @pl.when(at.a < at.line - 1)
-        def _():
-            self.up(at.e).start()
-
-        @pl.when(at.a > 0)
-        def _():
-            self.down(at.e).start()
-
-        for i in range(1, at.side):
-            self.across(at.e, i).start()
+        for p in range(len(self.parts)):
+
+            @pl.when(at.a - s >= 0)
+            def _(p=p):
+                k = at.e - s * at.side
+                self.down(k, p).wait_recv()
+                self.spread(k, p, True, False)
+
+            @pl.when(at.a + s < at.line)
+            def _(p=p):
+                k = at.e + s * at.side
+                self.up(k, p).wait_recv()
+                self.spread(k, p, False, True)
 
     def relay(self):
-        at = self.at
-        for s in range(1, at.line):
-
-            @pl.when(at.a - s >= 0)
-            def _(s=s):
-                k = at.e - s * at.side
-                self.down(k).wait_recv()
-
-                @pl.when(at.a < at.line - 1)
-                def _():
-                    self.up(k).start()
-
-                for i in range(1, at.side):
-                    self.across(k, i).start()
-
-            @pl.when(at.a + s < at.line)
-            def _(s=s):
-                k = at.e + s * at.side
-                self.up(k).wait_recv()
-
-                @pl.when(at.a > 0)
-                def _():
-                    self.down(k).start()
-
-                for i in range(1, at.side):
-                    self.across(k, i).start()
+        for s in range(1, self.at.line):
+            self.relay_step(s)
 
     def each(self, use):
         at = self.at
 
-        def step(i, carry):
-            k = (at.a + i) % at.line * at.side + (at.b + i // at.line) % at.side
-
-            @pl.when(i >= at.line)
+        def near(s, carry):
+            pl.when(s > 0)(lambda: self.relay_step(s))
+            pl.when(at.a - s >= 0)(lambda: use(at.e - s * at.side))
+            pl.when((s > 0) & (at.a + s < at.line))(lambda: use(at.e + s * at.side))
+            return carry
+
+        lax.fori_loop(0, at.line, near, 0)
+        self.rest(use)
+
+    def rest(self, use=None):
+        at = self.at
+
+        def take(n, carry):
+            s, sign = n // 2, 1 - n % 2 * 2
+            a = at.a + sign * s
+
+            @pl.when((a >= 0) & (a < at.line) & (n != 1))
             def _():
-                self.across(k, 1).wait_recv()
-
-            use(k)
+                for i in range(1, at.side):
+                    k = a * at.side + (at.b + i) % at.side
+                    for p in range(len(self.parts)):
+                        self.across(k, i, p).wait_recv()
+                    if use is not None:
+                        use(k)
+
             return carry
 
-        lax.fori_loop(0, at.owners, step, 0)
+        lax.fori_loop(0, 2 * at.line, take, 0)
 
     def finish(self):
         at = self.at
         for s in range(at.line):
             k = s * at.side + at.b
-
-            @pl.when((at.a < at.line - 1) & (at.a >= s))
-            def _():
-                self.up(k).wait_send()
-
-            @pl.when((at.a > 0) & (at.a <= s))
-            def _():
-                self.down(k).wait_send()
-
-            for i in range(1, at.side):
-                self.across(k, i).wait_send()
+            for p in range(len(self.parts)):
+
+                @pl.when((at.a < at.line - 1) & (at.a >= s))
+                def _(k=k, p=p):
+                    self.up(k, p).wait_send()
+
+                @pl.when((at.a > 0) & (at.a <= s))
+                def _(k=k, p=p):
+                    self.down(k, p).wait_send()
+
+                for i in range(1, at.side):
+                    self.across(k, i, p).wait_send()
 
 
 class LineScatter:
@@ -469,39 +488,35 @@
 
         lax.fori_loop(0, at.owners, step, 0)
 
-    def sum(self):
+    def sum_step(self, n):
         at = self.at
-
-        def step(n, carry):
-            s = self.place(n)
-            k = s * at.side + at.b
-            for i in range(1, at.side):
-                self.across(s, i).wait_recv()
-            total = self.part[k].astype(F32)
-            for j in range(at.side - 1):
-                total = total + self.side_in[s, j].astype(F32)
-            self.own[...] = total
-
-            @pl.when(((s > at.a) & (at.a > 0)) | ((s < at.a) & (at.a < at.line - 1)))
-            def _():
-                self.along(s, at.e, s).wait_recv()
-                self.own[...] += self.line_in[s].astype(F32)
-
-            self.part[k] = self.own[...].astype(BF16)
-
-            @pl.when(s > at.a)
-            def _():
-                self.up(s).start()
-
-            @pl.when(s < at.a)
-            def _():
-                self.down(s).start()
-
-            return carry
-
-        lax.fori_loop(0, at.line, step, 0)
-        total = self.part[at.e].astype(F32)
+        s = self.place(n)
+        k = s * at.side + at.b
+        for i in range(1, at.side):
+            self.across(s, i).wait_recv()
+        total = self.part[k].astype(F32)
+        for j in range(at.side - 1):
+            total = total + self.side_in[s, j].astype(F32)
         self.own[...] = total
+
+        @pl.when(((s > at.a) & (at.a > 0)) | ((s < at.a) & (at.a < at.line - 1)))
+        def _():
+            self.along(s, at.e, s).wait_recv()
+            self.own[...] += self.line_in[s].astype(F32)
+
+        self.part[k] = self.own[...].astype(BF16)
+
+        @pl.when(s > at.a)
+        def _():
+            self.up(s).start()
+
+        @pl.when(s < at.a)
+        def _():
+            self.down(s).start()
+
+    def sum_last(self):
+        at = self.at
+        self.own[...] = self.part[at.e].astype(F32)
 
         @pl.when(at.a > 0)
         def _():
@@ -528,39 +543,366 @@
                 self.down(s).wait_send()
 
 
-def moe_kernel(sizes, sent, cot, wgu, wd, comb_out, back_out, sums, far, *scratch):
+def rope_of(allowed, tokens):
+    lane = lax.broadcasted_iota(jnp.int32, (tokens, 128), 1)
+    position = jnp.sum(allowed.astype(F32), axis=1, keepdims=True) - 1.0
+    half = HEAD_SIZE // 2
+    inverse = jnp.exp(-math.log(BASE) * (2.0 * (lane % half).astype(F32) / HEAD_SIZE))
+    angle = position * inverse
+    return jnp.cos(angle), jnp.sin(angle), lane % HEAD_SIZE < half
+
+
+def turn(x, cos, sin, first):
+    half = HEAD_SIZE // 2
+    other = jnp.where(first, -pltpu.roll(x, 128 - half, 1), pltpu.roll(x, half, 1))
+    return x * cos + other * sin
+
+
+def visible(doc, tokens):
+    row = lax.broadcasted_iota(jnp.int32, (tokens, tokens), 0)
+    col = lax.broadcasted_iota(jnp.int32, (tokens, tokens), 1)
+    key_doc = jnp.broadcast_to(doc.astype(F32), (tokens, tokens))
+    own = jnp.sum(jnp.where(row == col, key_doc, 0.0), axis=1, keepdims=True)
+    return (own == key_doc) & (col <= row)
+
+
+def picked(routes, lane):
+    ids = routes[...].astype(F32).T
+    lane = lane.astype(F32)
+    chosen = lane == ids[:, :1]
+    for i in range(1, TOP):
+        chosen = chosen | (lane == ids[:, i : i + 1])
+    return chosen
+
+
+def attend_kernel(sizes, hidden, doc, routes, gain_a, gain_f, *refs):
+    shards, owners, tokens, experts = sizes
+    shares, cot = refs[:5], refs[5]
+    h1, q, k, v, mixed, lse, resid, sent, probs_out = refs[6:15]
+    fulls, cot_out, left = refs[15:20], refs[20], refs[21]
+    (bufs, cot_all, acc, lsem, xs, xr, ys, yr, ss, sr, cs, cr, ls, lr, own_left) = refs[22:]
+    at = Place(shards, owners)
+    rg = MODEL_WIDTH // shards
+    half, quarter = rg // 2, rg // 4
+    f = at.f
+    sib = (at.x * 2 + 1 - at.c, at.e)
+    over = ((at.x + 1) % at.chips * 2 + at.c, at.e)
+    far = over[0]
+    other = (at.x + 1) % at.chips * 2 + 1 - at.c
+    mine = (at.a + at.b) % 2
+    beside = (f, at.a * at.side + (at.b + 1) % at.side)
+    step = jnp.where(at.a % 2 == 0, at.side, -at.side)
+    along = (f, at.e + step)
+    count = len(shares)
+
+    own = [pltpu.make_async_copy(shares[n], bufs[n].at[f], lsem.at[n]) for n in range(count)]
+    own.append(pltpu.make_async_copy(cot, cot_all.at[at.e], lsem.at[count]))
+    for c in own:
+        c.start()
+
+    def piece(n, g, start, size, send, recv, dev):
+        ref = bufs[n].at[g, pl.ds(pl.multiple_of(start, quarter), size)]
+        return remote(ref, ref, send, recv, dev)
+
+    def begins(i):
+        return (mine * half, mine * half + quarter, (1 - mine) * half, (1 - mine) * half + quarter)[i]
+
+    def out_x(n, i):
+        start = pl.ds(pl.multiple_of(begins(i), quarter), quarter)
+        return remote(
+            shares[n].at[start], bufs[n].at[f, start], xs.at[n, i], xr.at[n, i], over
+        )
+
+    def in_x(n, i):
+        return piece(n, far, begins(i), quarter, xs.at[n, i], xr.at[n, i], over)
+
+    def out_yz(n, i):
+        return piece(n, far, begins(i), quarter, ys.at[n, i], yr.at[n, i], (beside, along)[i])
+
+    def in_yz(n, i):
+        return piece(n, far, begins(2 + i), quarter, ys.at[n, i], yr.at[n, i], (beside, along)[i])
+
+    def to_sib(n, i, g):
+        return piece(n, g, begins(i), quarter, ss.at[n, i], sr.at[n, i], sib)
+
+    def own_sib(n):
+        return remote(shares[n], bufs[n].at[f], ss.at[n, 4], sr.at[n, 4], sib)
+
+    def small_x():
+        return remote(shares[4], bufs[4].at[f], xs.at[4, 0], xr.at[4, 0], over)
+
+    def small_sib():
+        return remote(bufs[4].at[far], bufs[4].at[far], ss.at[4, 0], sr.at[4, 0], sib)
+
+    def pass_x(n, i):
+        in_x(n, i).wait_recv()
+        out_yz(n, i).start()
+        to_sib(n, i, far).start()
+
+    def pass_rest(n):
+        for i in range(2):
+            in_yz(n, i).wait_recv()
+            to_sib(n, 2 + i, far).start()
+
+    def from_sib(n):
+        for i in range(4):
+            to_sib(n, i, other).wait_recv()
+
+    def lefts(n, i):
+        g = (f + i) % shards
+        return remote(
+            (h1, mixed)[n].at[:, pl.ds(pl.multiple_of(g * rg, 128), rg)],
+            left.at[pl.ds(f * tokens, tokens), pl.ds(n * rg, rg)],
+            ls.at[n, i - 1], lr.at[n, i - 1], (g, at.e),
+        )
+
+    def left_own(n):
+        return pltpu.make_async_copy(
+            (h1, mixed)[n].at[:, pl.ds(pl.multiple_of(f * rg, 128), rg)],
+            left.at[pl.ds(f * tokens, tokens), pl.ds(n * rg, rg)],
+            own_left.at[n],
+        )
+
+    def send_left(n):
+        left_own(n).start()
+        for i in range(1, shards):
+            lefts(n, i).start()
+
+    at.meet(all_fsdp=True)
+    order = (1, 2, 0, 3)
+    for n in order[:3]:
+        for i in range(2):
+            out_x(n, i).start()
+        own_sib(n).start()
+    small_x().start()
+    own_sib(4).start()
+    for i in range(2):
+        out_x(3, i).start()
+    own_sib(3).start()
+    cotg = LineGather(at, cot_all, cs, cr)
+    own[count].wait()
+    cotg.begin()
+
+    x = hidden[...].astype(F32)
+    scale = lax.rsqrt(jnp.mean(x * x, axis=1, keepdims=True) + EPS)
+    h1[...] = (x * scale * gain_a[...].reshape(1, -1)).astype(BF16)
+    allowed = visible(doc[...], tokens)
+    cos, sin, first = rope_of(allowed, tokens)
+
+    ends = (0, 1536, 2048, 2560)
+
+    def project(g):
+        part = h1[:, pl.ds(pl.multiple_of(g * rg, 128), rg)]
+        return [dot(part, bufs[n][g]) for n in range(3)]
+
+    for n in range(3):
+        own[n].wait()
+        acc[:, ends[n] : ends[n + 1]] = dot(
+            h1[:, pl.ds(pl.multiple_of(f * rg, 128), rg)], bufs[n][f]
+        )
+
+    def add(g):
+        for n, got in enumerate(project(g)):
+            acc[:, ends[n] : ends[n + 1]] += got
+
+    for n in range(3):
+        own_sib(n).wait_recv()
+    add(sib[0])
+    for n in (1, 2):
+        for i in range(2):
+            pass_x(n, i)
+    cotg.relay_step(1)
+    pass_x(0, 0)
+    cotg.relay_step(2)
+    pass_x(0, 1)
+    for n in (1, 2, 0):
+        pass_rest(n)
+    cotg.relay_step(3)
+    pass_x(3, 0)
+    add(far)
+    for n in range(3):
+        from_sib(n)
+    add(other)
+    small_x().wait_recv()
+    small_sib().start()
+    pass_x(3, 1)
+
+    for j in range(16):
+        cols = slice(128 * j, 128 * (j + 1))
+        got = turn(acc[:, cols], cos, sin, first).astype(BF16)
+        if j < 12:
+            q[:, cols] = got
+        else:
+            k[:, 128 * (j - 12) : 128 * (j - 11)] = got
+    v[...] = acc[:, 2048:].astype(BF16)
+    ratio = QUERY_HEADS // KEY_VALUE_HEADS
+    mask = jnp.concatenate([allowed] * ratio, axis=0)
+
+    def head(ref, h):
+        return ref[:, h * HEAD_SIZE : (h + 1) * HEAD_SIZE]
+
+    for g in range(KEY_VALUE_HEADS):
+        heads = range(g * ratio, (g + 1) * ratio)
+        rows = jnp.concatenate([head(q, h) for h in heads], axis=0)
+        s = jnp.where(mask, dot(rows, head(k, g), 1, 1) * SCORE_SCALE, MASKED)
+        top = jnp.max(s, axis=1, keepdims=True)
+        e = jnp.exp(s - top)
+        total = jnp.sum(e, axis=1, keepdims=True)
+        o = dot((e / total).astype(BF16), head(v, g)).astype(BF16)
+        log_total = top + jnp.log(total)
+        for i, h in enumerate(heads):
+            mixed[:, h * HEAD_SIZE : (h + 1) * HEAD_SIZE] = o[i * tokens : (i + 1) * tokens]
+            lse[:, h : h + 1] = log_total[i * tokens : (i + 1) * tokens]
+
+    send_left(0)
+    send_left(1)
+    pass_rest(3)
+    for n in (3, 4):
+        own[n].wait()
+        own_sib(n).wait_recv()
+    small_sib().wait_recv()
+    from_sib(3)
+    total = x
+    for g in range(shards):
+        total = total + dot(mixed[:, g * rg : (g + 1) * rg], bufs[3][g])
+    resid[...] = total
+    scale = lax.rsqrt(jnp.mean(total * total, axis=1, keepdims=True) + EPS)
+    h2 = (total * scale * gain_f[...].reshape(1, -1)).astype(BF16)
+    sent[:, :MODEL_WIDTH] = h2
+    logits = dot(h2[:, :rg], bufs[4][0], 1, 1)
+    for g in range(1, shards):
+        logits = logits + dot(h2[:, g * rg : (g + 1) * rg], bufs[4][g], 1, 1)
+    logits = jnp.concatenate([logits, jnp.zeros((tokens, 128 - experts), F32)], axis=1)
+    lane = lax.broadcasted_iota(jnp.int32, (tokens, 128), 1)
+    live = lane < experts
+    logits = jnp.where(live, logits, MASKED)
+    e = jnp.where(live, jnp.exp(logits - jnp.max(logits, axis=1, keepdims=True)), 0.0)
+    probs = e / jnp.sum(e, axis=1, keepdims=True)
+    probs_out[...] = probs
+    chosen = picked(routes, lane)
+    row = lax.broadcasted_iota(jnp.int32, (tokens, tokens), 0)
+    col = lax.broadcasted_iota(jnp.int32, (tokens, tokens), 1)
+    below = jnp.where(row > col, 1.0, 0.0).astype(BF16)
+    hits = jnp.where(chosen, 1.0, 0.0)
+    rank = jnp.where(chosen, dot(below, hits.astype(BF16)), jnp.where(live, -1.0, 0.0))
+    gate = jnp.where(chosen, probs, 0.0)
+    high = gate.astype(BF16).astype(F32)
+    low = gate - high
+    meta = rank + pltpu.roll(high, experts, 1) + pltpu.roll(low, 2 * experts, 1)
+    sent[:, MODEL_WIDTH:] = meta.astype(BF16)
+
+    save = [pltpu.make_async_copy(bufs[n], fulls[n], lsem.at[n]) for n in range(count)]
+    for c in save:
+        c.start()
+    cotg.rest()
+    cotg.finish()
+    keep = pltpu.make_async_copy(cot_all, cot_out, lsem.at[count])
+    keep.start()
+    for n in range(count):
+        own_sib(n).wait_send()
+    small_x().wait_send()
+    small_sib().wait_send()
+    for n in order:
+        for i in range(2):
+            out_x(n, i).wait_send()
+            out_yz(n, i).wait_send()
+        for i in range(4):
+            to_sib(n, i, far).wait_send()
+    for n in range(2):
+        left_own(n).wait()
+        for i in range(1, shards):
+            lefts(n, i).wait()
+    for c in save:
+        c.wait()
+    keep.wait()
+
+
+def attend(sizes, hidden, doc, routes, gain_a, gain_f, shares, cot):
+    shards, owners, tokens, experts = sizes
+    rg = MODEL_WIDTH // shards
+    side = owners // 4
+    vm, dma = pltpu.VMEM, pltpu.SemaphoreType.DMA
+    vmem, any_ = pl.BlockSpec(memory_space=pltpu.VMEM), pl.BlockSpec(memory_space=pl.ANY)
+    n = len(shares)
+
+    def shape(*dims, dtype=BF16):
+        return jax.ShapeDtypeStruct(dims, dtype)
+
+    outs = pl.pallas_call(
+        functools.partial(attend_kernel, sizes),
+        name="attend",
+        out_shape=(
+            shape(tokens, MODEL_WIDTH),
+            shape(tokens, MODEL_WIDTH),
+            shape(tokens, KEY_VALUE_HEADS * HEAD_SIZE),
+            shape(tokens, KEY_VALUE_HEADS * HEAD_SIZE),
+            shape(tokens, MODEL_WIDTH),
+            shape(tokens, 128, dtype=F32),
+            shape(tokens, MODEL_WIDTH, dtype=F32),
+            shape(tokens, MODEL_WIDTH + 128),
+            shape(tokens, 128, dtype=F32),
+            *[shape(shards, *s.shape) for s in shares],
+            shape(owners, tokens, MODEL_WIDTH),
+            shape(shards * tokens, 2 * rg),
+        ),
+        in_specs=[vmem] * 5 + [any_] * (n + 1),
+        out_specs=[vmem] * 9 + [any_] * (n + 2),
+        scratch_shapes=[
+            tuple(vm((shards, *s.shape), BF16) for s in shares),
+            vm((owners, tokens, MODEL_WIDTH), BF16),
+            vm((tokens, 2560), F32),
+            dma((n + 1,)),
+            dma((n, 2)),
+            dma((n, 2)),
+            dma((n, 2)),
+            dma((n, 2)),
+            dma((n, 5)),
+            dma((n, 5)),
+            dma((2, side + 1, owners)),
+            dma((2, owners)),
+            dma((2, shards - 1)),
+            dma((2, shards - 1)),
+            dma((2,)),
+        ],
+        compiler_params=pltpu.CompilerParams(
+            collective_id=0, has_side_effects=True, vmem_limit_bytes=60 * 2**20
+        ),
+    )(hidden, doc, routes, gain_a, gain_f, *shares, cot)
+    return outs[:9], outs[9 : 9 + n], outs[9 + n], outs[10 + n]
+
+
+EARLY = 4
+
+
+def moe_kernel(sizes, sent, cot, wgu, wd, back_out, comb_out, sums, far, away, *scratch):
     shards, owners, tokens, experts, held, pairing = sizes
-    (rows_all, cot_all, taken, cots, slot_gate, place, wg_buf, wd_buf, gg, gd, from_core, to_far,
-     own_sum, z_acc, dx_acc, dg_acc, side1, line1, side2, line2, own2,
-     rs, rr, cs, cr, wsem, coresend, corerecv, farsend, farrecv, osem, free, s1, s2, s3, s4, t1, t2, t3, t4,
+    (rows_all, cot_buf, taken, cots, made, grads, slot_gate, slot_grad, place, wg_buf, wd_buf,
+     acts, dus, gg, gd, from_core, stage, side1, line1,
+     rs, rr, wsem, csem, coresend, corerecv, farsend, farrecv, osem, free, s1, s2, s3, s4,
      ) = scratch
     at = Place(shards, owners)
     groups = held // pairing
     slots = groups * CAP
     half = wd.shape[1]
     rg, rd = MODEL_WIDTH // shards, half // shards
-    width = MODEL_WIDTH + 128
-
-    def weights(h, slot):
-        return (
-            pltpu.make_async_copy(wgu.at[h], wg_buf.at[slot], wsem.at[0, slot]),
-            pltpu.make_async_copy(wd.at[h], wd_buf.at[slot], wsem.at[1, slot]),
-        )
-
-    for c in weights(0, 0):
+    sibling = (at.x * 2 + 1 - at.c, at.e)
+
+    def weights(g):
+        out = []
+        for m in range(pairing):
+            h, slot = g * pairing + m, g % 2 * pairing + m
+            out.append(pltpu.make_async_copy(wgu.at[h], wg_buf.at[slot], wsem.at[0, slot]))
+            out.append(pltpu.make_async_copy(wd.at[h], wd_buf.at[slot], wsem.at[1, slot]))
+        return out
+
+    mine = pltpu.make_async_copy(sent, rows_all.at[at.e], osem.at[0, 0])
+    mine.start()
+    for c in weights(0):
         c.start()
     at.meet()
     rows = LineGather(at, rows_all, rs, rr)
-    cotg = LineGather(at, cot_all, cs, cr)
-    c1 = pltpu.make_async_copy(sent, rows_all.at[at.e], osem.at[0, 0])
-    c2 = pltpu.make_async_copy(cot, cot_all.at[at.e], osem.at[0, 1])
-    c1.start()
-    c2.start()
-    c1.wait()
+    mine.wait()
     rows.begin()
-    rows.relay()
-    c2.wait()
-    cotg.begin()
 
     lane = lax.broadcasted_iota(jnp.int32, (128, slots), 1)
     row = lax.broadcasted_iota(jnp.int32, (128, slots), 0)
@@ -575,7 +917,7 @@
     col = lax.broadcasted_iota(jnp.int32, (slots, 128), 1)
     pick_gate = (col == e_row + experts) | (col == e_row + 2 * experts)
 
-    def dispatch_rows(k):
+    def dispatch(k):
         rank_at = dot(rows_all[k, :, MODEL_WIDTH:], find_rank)
         pt = jnp.where(rank_at == slot_rank, 1.0, 0.0).astype(BF16)
         place[k] = pt
@@ -587,189 +929,232 @@
             taken[g, to, :] = got[g * CAP : (g + 1) * CAP, :MODEL_WIDTH].astype(BF16)
             slot_gate[g, to, :] = gate[g * CAP : (g + 1) * CAP]
 
-    def dispatch_cot(k):
-        got = dot(place[k], cot_all[k], 0, 0).astype(BF16)
+    def dispatch_both(k):
+        pull = pltpu.make_async_copy(cot.at[k], cot_buf.at[0], csem.at[0])
+        pull.start()
+        dispatch(k)
+        pull.wait()
+        got = dot(place[k], cot_buf[0], 0, 0).astype(BF16)
         to = pl.ds(k * CAP, CAP)
         for g in range(groups):
             cots[g, to, :] = got[g * CAP : (g + 1) * CAP]
 
-    rows.each(dispatch_rows)
-    cotg.relay()
-    cotg.each(dispatch_cot)
-
-    def to_core(h, slot):
+    rows.each(dispatch_both)
+    rows.finish()
+
+    def through(g):
+        for c in weights(g):
+            c.wait()
+
+        @pl.when(g + 1 < groups)
+        def _():
+            for c in weights(g + 1):
+                c.start()
+
+        gate = slot_gate[g][:, :1]
+        total = jnp.zeros((owners * CAP, 1), F32)
+        for m in range(pairing):
+            h, slot = g * pairing + m, g % 2 * pairing + m
+            gu = dot(taken[g], wg_buf[slot])
+            a, b = gu[:, :half], gu[:, half:]
+            sig = 1.0 / (1.0 + jnp.exp(-a))
+            s = a * sig
+            act = s * b
+            acts[h] = (act * gate).astype(BF16)
+            dp = dot(cots[g], wd_buf[slot], 1, 1)
+            total = total + jnp.sum(act * dp, axis=1, keepdims=True)
+            dact = dp * gate
+            dus[h, :, :half] = (dact * b * sig * (1.0 + a * (1.0 - sig))).astype(BF16)
+            dus[h, :, half:] = (dact * s).astype(BF16)
+        slot_grad[g] = jnp.broadcast_to(total, (owners * CAP, 128))
+        n = MODEL_WIDTH // 3
+        for i in range(3):
+            cols = slice(i * n, (i + 1) * n)
+            y = 0.0
+            dx = 0.0
+            for m in range(pairing):
+                h, slot = g * pairing + m, g % 2 * pairing + m
+                y = y + dot(acts[h], wd_buf[slot, :, cols])
+                dx = dx + dot(dus[h], wg_buf[slot, cols, :], 1, 1)
+            made[g, :, cols] = y.astype(BF16)
+            grads[g, :, cols] = dx.astype(BF16)
+
+    def to_core(h):
+        slot = h % 2
         out = []
         for i in range(at.chips):
             f = 2 * i + 1 - at.c
-            for n, (buf, r, o) in enumerate(((gg, rg, 0), (gd, rd, 1))):
+            for n, (buf, r) in enumerate(((gg, rg), (gd, rd))):
                 out.append(
                     remote(
                         buf.at[slot, pl.ds(pl.multiple_of(f * r, r), r)],
-                        from_core[o].at[slot, i],
+                        from_core[n].at[slot, i],
                         coresend.at[slot, n, i],
                         corerecv.at[slot, n, i],
-                        (at.x * 2 + 1 - at.c, at.e),
+                        sibling,
                     )
                 )
         return out
 
     def to_chips(h):
+        return chip_copies(at, h, away, h, far, farsend, farrecv)
+
+    def keep(h):
+        slot = h % 2
         out = []
-        for i in range(1, at.chips):
-            j = at.chips - 1 - i
-            dev = ((at.x + i) % at.chips * 2 + at.c, at.e)
-            for n in range(2):
+        for n in range(2):
+            out.append(pltpu.make_async_copy(stage[n].at[slot, 0], sums[n].at[h], osem.at[n, slot]))
+            for i in range(1, at.chips):
                 out.append(
-                    remote(
-                        to_far[n].at[h, i - 1],
-                        far[n].at[j, h],
-                        farsend.at[n, i - 1, h],
-                        farrecv.at[n, j, h],
-                        dev,
+                    pltpu.make_async_copy(
+                        stage[n].at[slot, i], away[n].at[h, i - 1], osem.at[2 * i + n, slot]
                     )
                 )
         return out
 
-    def own_copy(h, slot):
-        return [
-            pltpu.make_async_copy(own_sum[n].at[slot], sums[n].at[h], osem.at[n, slot])
-            for n in range(2)
-        ]
-
-    def add(h, slot):
-        for c in to_core(h, slot):
+    def add(h):
+        slot = h % 2
+        for c in to_core(h):
             c.wait()
 
         @pl.when(h >= 2)
         def _():
-            for c in own_copy(h, slot):
-                c.wait()
+            leave(h - 2)
 
         for i in range(at.chips):
             x = (at.x + i) % at.chips
             f = 2 * x + at.c
             for n, (buf, r) in enumerate(((gg, rg), (gd, rd))):
-                mine = buf[slot, pl.ds(pl.multiple_of(f * r, r), r)].astype(F32)
-                total = (mine + from_core[n][slot, x].astype(F32)).astype(BF16)
-                if i == 0:
-                    own_sum[n][slot] = total
-                else:
-                    to_far[n][h, i - 1] = total
-        for c in to_chips(h):
-            c.start()
-        for c in own_copy(h, slot):
+                own = buf[slot, pl.ds(pl.multiple_of(f * r, r), r)].astype(F32)
+                stage[n][slot, i] = (own + from_core[n][slot, x].astype(F32)).astype(BF16)
+        for c in keep(h):
             c.start()
 
         @pl.when(h < held - 2)
         def _():
-            pl.semaphore_signal(
-                free, inc=1, device_id=(at.x * 2 + 1 - at.c, at.e), device_id_type=MESH
-            )
-
-    def step(h, carry):
-        slot = h % 2
-        g, m = h // pairing, h % pairing
-        for c in weights(h, slot):
+            pl.semaphore_signal(free, inc=1, device_id=sibling, device_id_type=MESH)
+
+    def leave(h):
+        for c in keep(h):
             c.wait()
 
-        @pl.when(h + 1 < held)
+        @pl.when(h < EARLY)
         def _():
-            for c in weights(h + 1, 1 - slot):
+            for c in to_chips(h):
                 c.start()
 
-        @pl.when(m == 0)
-        def _():
-            z_acc[...] = jnp.zeros_like(z_acc)
-            dx_acc[...] = jnp.zeros_like(dx_acc)
-            dg_acc[...] = jnp.zeros_like(dg_acc)
-
-        gu = dot(taken[g], wg_buf[slot])
-        a, b = gu[:, :half], gu[:, half:]
-        gate = slot_gate[g][:, :1]
-        sig = 1.0 / (1.0 + jnp.exp(-a))
-        s = a * sig
-        act = s * b
-        actg = (act * gate).astype(BF16)
-        dp = dot(cots[g], wd_buf[slot], 1, 1)
-        dg_acc[...] += jnp.broadcast_to(
-            jnp.sum(act * dp, axis=1, keepdims=True), dg_acc.shape
-        )
-        dact = dp * gate
-        da = dact * b * sig * (1.0 + a * (1.0 - sig))
-        db = dact * s
-        du = jnp.concatenate([da, db], axis=1).astype(BF16)
-        z_acc[...] += dot(actg, wd_buf[slot])
-        dx_acc[...] += dot(du, wg_buf[slot], 1, 1)
+    def weigh(h):
+        g, slot = h // pairing, h % 2
+        n = MODEL_WIDTH // 3
         for i in range(3):
-            n = MODEL_WIDTH // 3
             gg[slot, i * n : (i + 1) * n, :] = dot(
-                taken[g, :, i * n : (i + 1) * n], du, 0, 0
+                taken[g, :, i * n : (i + 1) * n], dus[h], 0, 0
             ).astype(BF16)
-        gd[slot] = dot(actg, cots[g], 0, 0).astype(BF16)
+        gd[slot] = dot(acts[h], cots[g], 0, 0).astype(BF16)
 
         @pl.when(h >= 2)
         def _():
             pl.semaphore_wait(free, 1)
 
-        for c in to_core(h, slot):
+        for c in to_core(h):
             c.start()
 
         @pl.when(h > 0)
         def _():
-            add(h - 1, 1 - slot)
-
-        @pl.when(m == pairing - 1)
-        def _():
-            taken[g] = z_acc[...].astype(BF16)
-            cots[g] = dx_acc[...].astype(BF16)
-            slot_gate[g] = dg_acc[...]
-
-        return carry
-
-    lax.fori_loop(0, held, step, 0)
-    add(held - 1, (held - 1) % 2)
-
-    rows.finish()
-    cotg.finish()
+            add(h - 1)
 
     home = (col == e_row).astype(F32).astype(BF16)
     home_low = (col == e_row + experts).astype(F32).astype(BF16)
+    parts = ((0, 512), (512, 1024), (1024, 1536))
 
     def make_back(k):
         to = pl.ds(k * CAP, CAP)
-        dx = jnp.concatenate([cots[g, to, :] for g in range(groups)], axis=0)
-        dg = jnp.concatenate([slot_gate[g, to, :] for g in range(groups)], axis=0)
+        dg = jnp.concatenate([slot_grad[g, to, :] for g in range(groups)], axis=0)
         high = dg.astype(BF16)
         low = (dg - high.astype(F32)).astype(BF16)
-        dgm = high * home + low * home_low
         pt = place[k]
-        rows_all[k, :, :MODEL_WIDTH] = dot(pt, dx).astype(BF16)
-        rows_all[k, :, MODEL_WIDTH:] = dot(pt, dgm).astype(BF16)
-
-    def make_comb(k):
+        for lo, hi in parts:
+            dx = jnp.concatenate([grads[g, to, lo:hi] for g in range(groups)], axis=0)
+            rows_all[k, :, lo:hi] = dot(pt, dx).astype(BF16)
+        rows_all[k, :, MODEL_WIDTH:] = dot(pt, high * home + low * home_low).astype(BF16)
+
+    back = LineScatter(at, rows_all, side1, line1, back_out, (s1, s2, s3, s4))
+
+    def step(i, carry):
+        @pl.when(i < groups)
+        def _():
+            through(i)
+
+        @pl.when(i == groups)
+        def _():
+            back.begin(make_back)
+
+        @pl.when(i >= 1)
+        def _():
+            weigh(i - 1)
+
+        @pl.when(i == held - 1)
+        def _():
+            back.sum_step(0)
+
+        return carry
+
+    lax.fori_loop(0, held + 1, step, 0)
+    add(held - 1)
+    back.sum_step(1)
+
+    def combine(k, carry):
         to = pl.ds(k * CAP, CAP)
-        y = jnp.concatenate([taken[g, to, :] for g in range(groups)], axis=0)
-        cot_all[k] = dot(place[k], y).astype(BF16)
-
-    back = LineScatter(at, rows_all, side1, line1, back_out, (s1, s2, s3, s4))
-    comb = LineScatter(at, cot_all, side2, line2, own2, (t1, t2, t3, t4))
-    back.begin(make_back)
-    comb.begin(make_comb)
-    back.sum()
-    comb.sum()
-    comb_out[...] = own2[...]
+        slot = k % 2
+
+        def put(j):
+            return pltpu.make_async_copy(cot_buf.at[j % 2], comb_out.at[j], csem.at[j % 2])
+
+        @pl.when(k >= 2)
+        def _():
+            put(k - 2).wait()
+
+        for lo, hi in parts:
+            y = jnp.concatenate([made[g, to, lo:hi] for g in range(groups)], axis=0)
+            cot_buf[slot, :, lo:hi] = dot(place[k], y).astype(BF16)
+        put(k).start()
+
+        @pl.when(k == owners - 1)
+        def _():
+            put(k - 1).wait()
+            put(k).wait()
+
+        return carry
+
+    lax.fori_loop(0, owners, combine, 0)
+    for h in range(held - 2, held):
+        leave(h)
+    back.sum_step(2)
+    back.sum_step(3)
+    back.sum_last()
     back.finish()
-    comb.finish()
-    for h in range(held - 2, held):
-        for c in own_copy(h, h % 2):
-            c.wait()
 
     def drain(h, carry):
         for c in to_chips(h):
             c.wait()
         return carry
 
-    lax.fori_loop(0, held, drain, 0)
+    lax.fori_loop(0, EARLY, drain, 0)
+
+
+def chip_copies(at, h, away, j, far, send, recv):
+    out = []
+    for i in range(1, at.chips):
+        back = at.chips - 1 - i
+        dev = ((at.x + i) % at.chips * 2 + at.c, at.e)
+        for n in range(2):
+            out.append(
+                remote(
+                    away[n].at[h, i - 1], far[n].at[back, j], send.at[n, i - 1, j],
+                    recv.at[n, back, j], dev,
+                )
+            )
+    return out
 
 
 def moe(sizes, sent, cot, wgu, wd):
@@ -779,14 +1164,14 @@
     hidden, half = wgu.shape[2], wd.shape[1]
     rg, rd = MODEL_WIDTH // shards, half // shards
     chips = shards // 2
-    line = 4 if owners % 4 == 0 else 1
+    line = 4
     side = owners // line
     width = MODEL_WIDTH + 128
     vm, dma = pltpu.VMEM, pltpu.SemaphoreType.DMA
     any_, vmem = pl.BlockSpec(memory_space=pl.ANY), pl.BlockSpec(memory_space=pltpu.VMEM)
 
-    def pair(lead, dtype=BF16):
-        return (vm((*lead, rg, hidden), dtype), vm((*lead, rd, MODEL_WIDTH), dtype))
+    def pair(lead):
+        return (vm((*lead, rg, hidden), BF16), vm((*lead, rd, MODEL_WIDTH), BF16))
 
     def outs(lead):
         return (
@@ -794,60 +1179,335 @@
             jax.ShapeDtypeStruct((*lead, rd, MODEL_WIDTH), BF16),
         )
 
-    def scatter_sems():
-        return [dma((line, side)), dma((line, side)), dma((line,)), dma((line + 1,))]
-
     return pl.pallas_call(
         functools.partial(moe_kernel, sizes),
         name="moe",
         out_shape=(
-            jax.ShapeDtypeStruct((tokens, MODEL_WIDTH), F32),
             jax.ShapeDtypeStruct((tokens, width), F32),
+            jax.ShapeDtypeStruct((owners, tokens, MODEL_WIDTH), BF16),
             outs((held,)),
-            outs((chips - 1, held)),
+            outs((chips - 1, EARLY)),
+            outs((held, chips - 1)),
         ),
         in_specs=[any_] * 4,
-        out_specs=(vmem, vmem, (any_, any_), (any_, any_)),
+        out_specs=(vmem, any_, (any_, any_), (any_, any_), (any_, any_)),
         scratch_shapes=[
             vm((owners, tokens, width), BF16),
-            vm((owners, tokens, MODEL_WIDTH), BF16),
+            vm((2, tokens, MODEL_WIDTH), BF16),
+            vm((groups, rows, MODEL_WIDTH), BF16),
+            vm((groups, rows, MODEL_WIDTH), BF16),
             vm((groups, rows, MODEL_WIDTH), BF16),
             vm((groups, rows, MODEL_WIDTH), BF16),
             vm((groups, rows, 128), F32),
+            vm((groups, rows, 128), F32),
             vm((owners, tokens, slots), BF16),
-            vm((2, MODEL_WIDTH, hidden), BF16),
-            vm((2, half, MODEL_WIDTH), BF16),
+            vm((2 * pairing, MODEL_WIDTH, hidden), BF16),
+            vm((2 * pairing, half, MODEL_WIDTH), BF16),
+            vm((held, rows, half), BF16),
+            vm((held, rows, hidden), BF16),
             vm((2, MODEL_WIDTH, hidden), BF16),
             vm((2, half, MODEL_WIDTH), BF16),
             pair((2, chips)),
-            pair((held, chips - 1)),
-            pair((2,)),
-            vm((rows, MODEL_WIDTH), F32),
-            vm((rows, MODEL_WIDTH), F32),
-            vm((rows, 128), F32),
+            pair((2, chips)),
             vm((line, side - 1, tokens, width), BF16),
             vm((line + 1, tokens, width), BF16),
-            vm((line, side - 1, tokens, MODEL_WIDTH), BF16),
-            vm((line + 1, tokens, MODEL_WIDTH), BF16),
-            vm((tokens, MODEL_WIDTH), F32),
-            dma((side + 1, owners)),
-            dma((owners,)),
-            dma((side + 1, owners)),
-            dma((owners,)),
-            dma((2, 2)),
+            dma((2, side + 1, owners)),
+            dma((2, owners)),
+            dma((2, 2 * pairing)),
+            dma((2,)),
             dma((2, 2, chips)),
             dma((2, 2, chips)),
-            dma((2, chips - 1, held)),
-            dma((2, chips - 1, held)),
-            dma((2, 2)),
+            dma((2, chips - 1, EARLY)),
+            dma((2, chips - 1, EARLY)),
+            dma((2 * chips, 2)),
             pltpu.SemaphoreType.REGULAR,
-            *scatter_sems(),
-            *scatter_sems(),
+            dma((line, side)),
+            dma((line, side)),
+            dma((line,)),
+            dma((line + 1,)),
         ],
         compiler_params=pltpu.CompilerParams(
             collective_id=1, has_side_effects=True, vmem_limit_bytes=63 * 2**20
         ),
     )(sent, cot, wgu, wd)
+
+
+def reverse_kernel(sizes, hidden, doc, routes, gain_a, gain_f, cot, q, k, v, mixed, lse, resid, sent,
+                   probs, back, wo, wr, wq, wk, wv, comb, left_in, away0, away1, *refs):
+    shards, owners, tokens, experts, held = sizes
+    block_out, grad_in, total_o, total_q, far = refs[:5]
+    (w_bufs, left, turned, rights, dgrad, dattn_f, dqkv, aux, aux_in, comb_part, comb_side, comb_line,
+     comb_own, part_o, side_o, line_o, own_o, part_q, side_q, line_q, own_q,
+     wsem, rsend, rrecv, asend, arecv, farsend, farrecv, *sems) = refs[5:]
+    at = Place(shards, owners)
+    away = (away0, away1)
+    rg = MODEL_WIDTH // shards
+    piece = rg // owners
+    split = dqkv.shape[1]
+    f = at.f
+    sibling = (at.x * 2 + 1 - at.c, at.e)
+    over = ((at.x + 1) % at.chips * 2 + at.c, at.e)
+    ratio = QUERY_HEADS // KEY_VALUE_HEADS
+
+    fulls = (wo, wr, wq, wk, wv)
+    loads = [pltpu.make_async_copy(comb, comb_part, wsem.at[0])]
+    loads += [pltpu.make_async_copy(w, b, wsem.at[1 + i]) for i, (w, b) in enumerate(zip(fulls, w_bufs))]
+    loads.append(pltpu.make_async_copy(left_in, left, wsem.at[6]))
+    for c in loads:
+        c.start()
+    at.meet(all_fsdp=True)
+
+    combine = LineScatter(at, comb_part, comb_side, comb_line, comb_own, sems[:4])
+    outer = LineScatter(at, part_o, side_o, line_o, own_o, sems[4:8])
+    inner = LineScatter(at, part_q, side_q, line_q, own_q, sems[8:12])
+    outer_all = LineGather(at, total_o, sems[12], sems[13])
+    inner_all = LineGather(at, total_q, sems[14], sems[15])
+    loads[0].wait()
+    combine.begin(lambda k: None)
+
+    def rows(i):
+        return pl.ds(pl.multiple_of(i * tokens, tokens), tokens)
+
+    def block(chunk, g, send, dev):
+        cols = (pl.ds(split, MODEL_WIDTH), pl.ds(0, split))[chunk]
+        ref = rights.at[rows(g), cols]
+        return remote(ref, ref, rsend.at[chunk, send], rrecv.at[chunk, g], dev)
+
+    def send_rights(chunk):
+        block(chunk, f, 0, sibling).start()
+        block(chunk, f, 1, over).start()
+
+    def pass_rights(chunk):
+        block(chunk, over[0], 0, sibling).wait_recv()
+        block(chunk, over[0], 2, sibling).start()
+
+    def take_rights(chunk):
+        block(chunk, sibling[0], 0, sibling).wait_recv()
+        block(chunk, (at.x + 1) % at.chips * 2 + 1 - at.c, 0, sibling).wait_recv()
+
+    def late(h):
+        return chip_copies(at, h, away, h - EARLY, far, farsend, farrecv)
+
+    h2 = sent[:, :MODEL_WIDTH]
+    lane = lax.broadcasted_iota(jnp.int32, (tokens, 128), 1)
+    chosen = picked(routes, lane)
+    meta = back[:, MODEL_WIDTH:]
+    dprobs = jnp.where(chosen, meta + pltpu.roll(meta, 128 - experts, 1), 0.0)
+    p = probs[...]
+    dlogits = (p * (dprobs - jnp.sum(p * dprobs, axis=1, keepdims=True))).astype(BF16)
+    loads[1].wait()
+    loads[2].wait()
+    aux[...] = dot(dlogits, h2, 0, 0)[: aux.shape[0]]
+
+    def full(i):
+        return w_bufs[i][...].reshape(MODEL_WIDTH, -1)
+
+    dh = back[:, :MODEL_WIDTH] + jnp.concatenate(
+        [dot(dlogits[:, :experts], w_bufs[1][g]) for g in range(shards)], axis=1
+    )
+    x = resid[...]
+    scale = lax.rsqrt(jnp.mean(x * x, axis=1, keepdims=True) + EPS)
+    n = x * scale
+    aux[experts + 1 : experts + 2, :] = jnp.sum(dh * n, axis=0, keepdims=True)
+    dn = dh * gain_f[...].reshape(1, -1)
+    dres = cot[...].astype(F32) + scale * (dn - n * jnp.mean(dn * n, axis=1, keepdims=True))
+    dgrad[...] = dres
+    dattn = dres.astype(BF16)
+    rights[rows(f), split:] = dattn
+    send_rights(0)
+    for c in late(EARLY):
+        c.start()
+    dattn_f[...] = dot(dattn, full(0), 1, 1).astype(BF16)
+
+    allowed = visible(doc[...], tokens)
+    cos, sin, first = rope_of(allowed, tokens)
+    mask = jnp.concatenate([allowed] * ratio, axis=0)
+
+    def stack(ref, heads):
+        return jnp.concatenate(
+            [ref[:, h * HEAD_SIZE : (h + 1) * HEAD_SIZE] for h in heads], axis=0
+        )
+
+    kept = QUERY_HEADS * HEAD_SIZE
+    span = KEY_VALUE_HEADS * HEAD_SIZE
+    for g in range(KEY_VALUE_HEADS):
+        heads = range(g * ratio, (g + 1) * ratio)
+        one = slice(g * HEAD_SIZE, (g + 1) * HEAD_SIZE)
+        qs, ks, vs = stack(q, heads), k[:, one], v[:, one]
+        dos, os = stack(dattn_f, heads), stack(mixed, heads)
+        logs = jnp.concatenate([lse[:, h : h + 1] for h in heads], axis=0)
+        s = jnp.where(mask, dot(qs, ks, 1, 1) * SCORE_SCALE, MASKED)
+        w = jnp.exp(s - logs)
+        low = w.astype(BF16)
+        delta = jnp.sum(dos.astype(F32) * os.astype(F32), axis=1, keepdims=True)
+        ds = (w * (dot(dos, vs, 1, 1) - delta) * SCORE_SCALE).astype(BF16)
+        dq = dot(ds, ks)
+        for i, h in enumerate(heads):
+            dqkv[:, h * HEAD_SIZE : (h + 1) * HEAD_SIZE] = dq[i * tokens : (i + 1) * tokens]
+        dqkv[:, kept + g * HEAD_SIZE : kept + (g + 1) * HEAD_SIZE] = dot(ds, qs, 0, 0)
+        at_v = kept + span + g * HEAD_SIZE
+        dqkv[:, at_v : at_v + HEAD_SIZE] = dot(low, dos, 0, 0)
+        if g == 2:
+            combine.sum_step(0)
+        if g == 5:
+            pass_rights(0)
+
+    for j in range((kept + span) // 128):
+        cols = slice(128 * j, 128 * (j + 1))
+        rights[rows(f), cols] = turn(dqkv[:, cols], cos, -sin, first).astype(BF16)
+    rights[rows(f), kept + span : split] = dqkv[:, kept + span :].astype(BF16)
+    send_rights(1)
+    combine.sum_step(1)
+    for i in range(3, 6):
+        loads[i].wait()
+    mine = rights[rows(f), :split]
+    dh = dot(mine[:, :kept], full(2), 1, 1)
+    dh = dh + dot(mine[:, kept : kept + span], full(3), 1, 1)
+    dh = dh + dot(mine[:, kept + span :], full(4), 1, 1)
+    x = hidden[...].astype(F32)
+    scale = lax.rsqrt(jnp.mean(x * x, axis=1, keepdims=True) + EPS)
+    n = x * scale
+    aux[experts : experts + 1, :] = jnp.sum(dh * n, axis=0, keepdims=True)
+    dn = dh * gain_a[...].reshape(1, -1)
+    grad_in[...] = dgrad[...] + scale * (dn - n * jnp.mean(dn * n, axis=1, keepdims=True))
+
+    def cols(g):
+        return pl.ds(pl.multiple_of(g * rg, 128), rg)
+
+    def auxes(i):
+        g = (f + i) % shards
+        return remote(
+            aux.at[:, cols(g)], aux_in.at[i], asend.at[i - 1], arecv.at[i - 1], (g, at.e)
+        )
+
+    for i in range(1, shards):
+        auxes(i).start()
+    for h in range(EARLY + 1, held):
+        for c in late(h):
+            c.start()
+    aux_in[0] = aux[:, cols(f)]
+
+    loads[6].wait()
+    turned[...] = left[...].T
+    take_rights(0)
+    step = 512
+
+    def product(part, half, lo, hi):
+        for a in range(lo, hi, step):
+            got = dot(turned[half * rg : (half + 1) * rg], rights[:, a : a + step]).astype(BF16)
+            for i in range(owners):
+                part[i, :, a - lo : a - lo + step] = got[i * piece : (i + 1) * piece]
+
+    product(part_o, 1, split, split + MODEL_WIDTH)
+    outer.begin(lambda k: None)
+    combine.sum_step(2)
+    pass_rights(1)
+    combine.sum_step(3)
+    outer.sum_step(0)
+    combine.sum_last()
+    block_out[...] = (resid[...] + comb_own[...]).astype(BF16)
+    take_rights(1)
+    extra = aux_in[0]
+    for i in range(1, shards):
+        auxes(i).wait_recv()
+        extra = extra + aux_in[i]
+    extra = jnp.concatenate([extra, jnp.zeros((128 - extra.shape[0], rg), F32)], axis=0)
+    extra = extra.T.astype(BF16)
+    product(part_q, 0, 0, split)
+    for i in range(owners):
+        part_q[i, :, split:] = extra[i * piece : (i + 1) * piece]
+    inner.begin(lambda k: None)
+    for i in range(1, 4):
+        outer.sum_step(i)
+    outer.sum_last()
+    total_o[at.e] = own_o[...].astype(BF16)
+    outer_all.begin()
+    inner.sum_step(0)
+    inner.sum_step(1)
+    outer_all.relay_step(1)
+    inner.sum_step(2)
+    outer_all.relay_step(2)
+    inner.sum_step(3)
+    outer_all.relay_step(3)
+    inner.sum_last()
+    total_q[at.e] = own_q[...].astype(BF16)
+    inner_all.begin()
+    inner_all.relay()
+    outer_all.rest()
+    inner_all.rest()
+    for chunk in range(2):
+        for i in range(3):
+            block(chunk, f, i, sibling).wait_send()
+    for i in range(1, shards):
+        auxes(i).wait_send()
+    for t in (combine, outer, inner, outer_all, inner_all):
+        t.finish()
+    for h in range(EARLY, held):
+        for c in late(h):
+            c.wait()
+
+
+def reverse(sizes, vmem_args, fulls, comb, left, away):
+    shards, owners, tokens, experts, held = sizes
+    rg = MODEL_WIDTH // shards
+    piece = rg // owners
+    chips = shards // 2
+    line = 4
+    side = owners // line
+    split = MODEL_WIDTH + 2 * KEY_VALUE_HEADS * HEAD_SIZE
+    wide = split + 128
+    extra = 48
+    vm, dma = pltpu.VMEM, pltpu.SemaphoreType.DMA
+    vmem, any_ = pl.BlockSpec(memory_space=pltpu.VMEM), pl.BlockSpec(memory_space=pl.ANY)
+
+    def scatter(rows, width):
+        return [
+            vm((owners, rows, width), BF16),
+            vm((line, side - 1, rows, width), BF16),
+            vm((line + 1, rows, width), BF16),
+            vm((rows, width), F32),
+        ]
+
+    shape = jax.ShapeDtypeStruct
+    return pl.pallas_call(
+        functools.partial(reverse_kernel, sizes),
+        name="reverse",
+        out_shape=(
+            shape((tokens, MODEL_WIDTH), BF16),
+            shape((tokens, MODEL_WIDTH), F32),
+            shape((owners, piece, MODEL_WIDTH), BF16),
+            shape((owners, piece, wide), BF16),
+            tuple(shape((chips - 1, held - EARLY, *a.shape[2:]), BF16) for a in away),
+        ),
+        in_specs=[vmem] * len(vmem_args) + [any_] * 9,
+        out_specs=(vmem, vmem, vmem, vmem, (any_, any_)),
+        scratch_shapes=[
+            tuple(vm(w.shape, BF16) for w in fulls),
+            vm((shards * tokens, 2 * rg), BF16),
+            vm((2 * rg, shards * tokens), BF16),
+            vm((shards * tokens, split + MODEL_WIDTH), BF16),
+            vm((tokens, MODEL_WIDTH), F32),
+            vm((tokens, MODEL_WIDTH), BF16),
+            vm((tokens, split), F32),
+            vm((extra, MODEL_WIDTH), F32),
+            vm((shards, extra, rg), F32),
+            *scatter(tokens, MODEL_WIDTH),
+            *scatter(piece, MODEL_WIDTH),
+            *scatter(piece, wide),
+            dma((7,)),
+            dma((2, 3)),
+            dma((2, shards)),
+            dma((shards - 1,)),
+            dma((shards - 1,)),
+            dma((2, chips - 1, held - EARLY)),
+            dma((2, chips - 1, held - EARLY)),
+            *([dma((line, side)), dma((line, side)), dma((line,)), dma((line + 1,))] * 3),
+            *([dma((1, side + 1, owners)), dma((1, owners))] * 2),
+        ],
+        compiler_params=pltpu.CompilerParams(
+            collective_id=2, has_side_effects=True, vmem_limit_bytes=63 * 2**20
+        ),
+    )(*vmem_args, *fulls, comb, left, *away)
 
 
 def plain_local(
@@ -1019,58 +1679,50 @@
     pairing = 2 if held % 2 == 0 else 1
     f32, bf16 = jnp.float32, jnp.bfloat16
 
-    first = lax.all_gather(
-        jnp.concatenate([w_query, key_matrix, value_matrix, w_router], axis=1),
-        "fsdp",
-        axis=0,
-        tiled=True,
-    )
-    full_query, full_key, full_value, full_router = jnp.split(first, (1536, 2048, 2560), axis=1)
-    full_output = lax.all_gather(w_output, "fsdp", axis=0, tiled=True)
-    weights_attn = (gain_attn, full_query, full_key, full_value, full_output, gain_ffn, full_router)
-    state = forward_local(hidden_in, doc_ids[0], routes, *weights_attn)
-    resid, ffn_in, probs = state[11], state[12], state[15]
-
-    chosen = jnp.any(
-        routes[:, :, None] == jnp.arange(experts, dtype=jnp.int32)[None, None, :], axis=1
-    )
-    below = jnp.tril(jnp.ones((tokens, tokens), bf16), -1)
-    rank = jnp.dot(below, chosen.astype(bf16), preferred_element_type=f32)
-    rank = jnp.where(chosen, rank, -1.0)
-    gate = jnp.where(chosen, probs, 0.0)
-    gate_high = gate.astype(bf16)
-    gate_low = (gate - gate_high.astype(f32)).astype(bf16)
-    meta = jnp.concatenate([rank.astype(bf16), gate_high, gate_low], axis=1)
-    sent = jnp.concatenate(
-        [ffn_in, meta, jnp.zeros((tokens, 128 - 3 * experts), bf16)], axis=1
-    )
+    shares = (w_query, key_matrix, value_matrix, w_output, w_router.T)
+    made, fulls, cot_all, left = attend(
+        (shards, owners, tokens, experts), hidden_in, doc_ids, routes.T, gain_attn, gain_ffn, shares,
+        cotangent,
+    )
+    h1, q, k, v, mixed, lse, resid, sent, probs = made
     sizes = (shards, owners, tokens, experts, held, pairing)
-    combined, back, sums, far = moe(sizes, sent, cotangent, w_gateup, w_down)
-    block_out = (resid + combined).astype(bf16)
-    grad_ffn = back[:, :MODEL_WIDTH]
-    grad_gate_dense = (
-        back[:, MODEL_WIDTH : MODEL_WIDTH + experts]
-        + back[:, MODEL_WIDTH + experts : MODEL_WIDTH + 2 * experts]
+    back, comb, sums, far, away = moe(sizes, sent, cot_all, w_gateup, w_down)
+    wq, wk, wv, wo, wr = fulls
+    block_out, grad_input, total_o, total_q, far_late = reverse(
+        (shards, owners, tokens, experts, held),
+        (hidden_in, doc_ids, routes.T, gain_attn, gain_ffn, cotangent, q, k, v, mixed,
+         lse, resid, sent, probs, back),
+        (wo, wr, wq, wk, wv),
+        comb,
+        left,
+        away,
     )
     grad_gateup, grad_down = (
-        s.astype(f32) + jnp.sum(r.astype(f32), axis=0) for s, r in zip(sums, far)
-    )
-    grad_input, grads = backward_local(
-        state, chosen, cotangent, grad_ffn, grad_gate_dense, *weights_attn
-    )
-    widths = [g.shape[1] if g.ndim == 2 else 1 for g in grads]
-    flat = jnp.concatenate([g if g.ndim == 2 else g[:, None] for g in grads], axis=1)
-    share = lax.psum_scatter(flat.astype(bf16), "fsdp", scatter_dimension=0, tiled=True)
-    total = lax.psum(share, "expert").astype(f32)
-    pieces = jnp.split(total, [sum(widths[: i + 1]) for i in range(len(widths) - 1)], axis=1)
-    pieces = [p if g.ndim == 2 else p[:, 0] for p, g in zip(pieces, grads)]
-    return (block_out, grad_input, *pieces, grad_gateup, grad_down)
+        s.astype(f32)
+        + jnp.sum(jnp.concatenate([r, t], axis=1).astype(f32), axis=0)
+        for s, r, t in zip(sums, far, far_late)
+    )
+    grad_output = total_o.reshape(-1, MODEL_WIDTH).astype(f32)
+    rest = total_q.reshape(-1, total_q.shape[2]).astype(f32)
+    return (
+        block_out,
+        grad_input,
+        rest[:, :1536],
+        rest[:, 1536:2048],
+        rest[:, 2048:2560],
+        grad_output,
+        rest[:, 2560 : 2560 + experts],
+        rest[:, 2560 + experts],
+        rest[:, 2561 + experts],
+        grad_gateup,
+        grad_down,
+    )
 
 
 def local(*args):
     owners, held = lax.axis_size("expert"), args[10].shape[0]
     groups = held // (2 if held % 2 == 0 else 1)
-    if owners * groups * CAP <= 2048 and owners % 4 == 0:
+    if lax.axis_size("fsdp") == 4 and owners == 8 and owners * groups * CAP <= 2048:
         return kernel_local(*args)
     return plain_local(*args)
 

time: 700 us -> 334 us (0.48)
  waiting for transfers between devices: 306 us -> 0 us
  Pallas kernels: 216 us -> 310 us
  local copies, waits for them, and re-layouts: 99.5 us -> 11 us
  matrix products: 39.2 us -> 0 us
  between operations: 14.6 us -> 0.73 us
  other arithmetic: 21.4 us -> 11.2 us
    pallas_call x0 -> x2, Pallas kernels: none -> 186 us  [the longest x1 119 us: reverse(): pl.pallas_call(functools.partial(reverse_kernel, sizes), name='reverse',...]
    psum x1 -> x0, waiting for transfers between devices: 117 us -> none  [kernel_local(): total = lax.psum(share, 'expert').astype(f32)]
    unnamed x5 -> x0, waiting for transfers between devices: 102 us -> none
    pallas_call x1, Pallas kernels: 216 us -> 125 us  [moe(): pl.pallas_call(functools.partial(moe_kernel, sizes), name='moe', out_shap...]
    all_gather x2 -> x0, waiting for transfers between devices: 86.9 us -> none  [the longest x1 58.6 us: kernel_local(): lax.all_gather(jnp.concatenate([w_query, key_matrix, value_matrix, w_rout...]
    concatenate x2 -> x0, local copies, waits for them, and re-layouts: 54.1 us -> none  [the longest x1 53.2 us: kernel_local(): jnp.concatenate([g if g.ndim == 2 else g[:, None] for g in grads], axis=1)]
    dot_general x22 -> x0, matrix products: 39.2 us -> none  [the longest x1 4.84 us: backward_local(): jnp.dot(grad_attn, w_output.T, preferred_element_type=jnp.float32)]
    unnamed x93 -> x21, local copies, waits for them, and re-layouts: 36.9 us -> 3.87 us
  transfers between devices with their start and end apart: 4 -> 0, of which waited for: 4 -> 0; matrix products, arithmetic and copies ran while one was open for 3% -> 0% of each run, Pallas kernels for 0% -> 0%
where the time goes in v3:
time: 334 us; the launch traced here: 333 us
  Pallas kernels  310 us (93%)
  other arithmetic  11.2 us (3%)
  local copies, waits for them, and re-layouts  11 us (3%)
    pallas_call x1, Pallas kernels, moe(): pl.pallas_call(functools.partial(moe_kernel, sizes), name='moe', out_shap...  125 us
    pallas_call x1, Pallas kernels, reverse(): pl.pallas_call(functools.partial(reverse_kernel, sizes), name='reverse',...  119 us
    pallas_call x1, Pallas kernels, attend(): pl.pallas_call(functools.partial(attend_kernel, sizes), name='attend', ou...  67 us
    add x2, other arithmetic, kernel_local(): s.astype(f32) + jnp.sum(jnp.concatenate([r, t], axis=1).astype(f32), axis=0)  9 us

profile of v3, /device:TPU:0, one launch (start us, length us, event | category | flops | bytes accessed | tf_op | source)
XLA Modules:
  0.0 333.3 jit_solution(341580571808103779)
XLA Ops:
  0.6 67.0 %attend.1 = (bf16[128,1536]{1,0:T(8,128)(2,1)}, bf16[128,1536]{1,0:T(8,128)(2,1)}, bf16[128,512]{1,0:T(8,128)(2,1)}, bf16[128,512]{1,0:T(8,128)(2,1)}, bf16[128,...) custom-call(bf16[128,1536]{1,0:T(8,128)(2,1)} %hidden.3, ...), custom_call_target="tpu_custom_call" | custom-call | tf_op jit(solution)/shard_map/attend/pallas_call | solution.py:831
  67.6 124.8 %moe.1 = (f32[128,1664]{1,0:T(8,128)}, bf16[8,128,1536]{2,1,0:T(8,128)(2,1)}, bf16[10,384,512]{2,1,0:T(8,128)(2,1)}, bf16[10,64,1536]{2,1,0:T(8,128)(2,1)}, bf16...) custom-call(bf16[128,1664]{1,0:T(8,128)(2,1)} %get-tuple-element.46., ...), custom_call_target="tpu_custom_call" | custom-call | tf_op jit(solution)/shard_map/moe/pallas_call | solution.py:1182
  192.5 0.0 copy-start.7
  192.5 118.6 %reverse.1 = (bf16[128,1536]{1,0:T(8,128)(2,1)}, f32[128,1536]{1,0:T(8,128)}, bf16[8,48,1536]{2,1,0:T(8,128)(2,1)}, bf16[8,48,2688]{2,1,0:T(8,128)(2,1)}, bf16[1...) custom-call(bf16[128,1536]{1,0:T(8,128)(2,1)} %hidden.3, s32[1,128]{1,0:T(1,128)} %doc.3, s32[8,128]{1,0:T(8,128)} %bitcast.18, ...), custom_call_target="tpu_custom_call" | custom-call | tf_op jit(solution)/shard_map/reverse/pallas_call | solution.py:1472
  311.1 0.0 copy-done.7
  311.1 0.0 copy-start.5
  311.1 0.0 copy-start.1
  311.2 0.0 copy-start.4
  311.2 4.5 %convert_add_fusion.1 = f32[10,64,1536]{2,1,0:T(8,128)} fusion(bf16[10,64,1536]{2,1,0:T(8,128)(2,1)} %get-tuple-element.66, bf16[6,64,1536]{2,1,0:T(8,128)(2,1)} %bitcast.14, bf16[4,64,1536]{2,1,0:T(8,128)(2,1)S(1)} %bitcast.15), kind=kLoop, calls=%fused_computation.1 | loop fusion | flops 3932160 | bytes 7864320 | tf_op jit(solution)/shard_map/add | solution.py:1701
  315.7 0.0 copy-done.5
  315.7 0.0 copy-start.2
  315.7 1.8 bitcast_convert_fusion.1
  317.5 0.0 copy-done.1
  317.5 0.0 copy-done.4
  317.5 0.7 copy-done.2
  318.2 0.0 copy-start.3
  318.2 4.5 %convert_add_fusion = f32[10,384,512]{2,1,0:T(8,128)} fusion(bf16[10,384,512]{2,1,0:T(8,128)(2,1)S(1)} %copy-done.1, bf16[6,384,512]{2,1,0:T(8,128)(2,1)S(1)} %bitcast.12, bf16[4,384,512]{2,1,0:T(8,128)(2,1)S(1)} %bitcast.13), kind=kLoop, calls=%fused_computation | loop fusion | flops 7864320 | bytes 15728640 | tf_op jit(solution)/shard_map/add | solution.py:1701
  322.6 0.0 copy-done.3
  322.6 0.4 bitcast_convert_fusion
  323.1 0.0 copy-start
  323.1 1.1 slice_reduce_fusion
  324.2 0.8 copy-done
  325.0 0.7 copy.26
  325.7 2.6 fusion
  328.4 0.0 copy-start.8
  328.4 0.0 copy-start.6
  328.4 3.3 slice.24
  331.7 0.0 copy-done.8
  331.7 0.7 copy.29
  332.4 0.0 copy-done.6
  332.4 0.9 copy.30
  (1 shorter events, 0.0 us)
Async XLA Ops:
  192.5 118.6 %copy-start.7 = (bf16[1,4,64,1536]{3,2,1,0:T(8,128)(2,1)S(1)}, bf16[1,4,64,1536]{3,2,1,0:T(8,128)(2,1)}, u32[]{:S(2)}) copy-start(bf16[1,4,64,1536]{3,2,1,0:T(8,128)(2,1)} %get-tuple-element.67) | copy-start | bytes 2359300
  311.1 4.6 %copy-start.5 = (bf16[8,48,1536]{2,1,0:T(8,128)(2,1)S(1)}, bf16[8,48,1536]{2,1,0:T(8,128)(2,1)}, u32[]{:S(2)}) copy-start(bf16[8,48,1536]{2,1,0:T(8,128)(2,1)} %get-tuple-element.62) | copy-start | bytes 3538948
  311.1 6.3 %copy-start.1 = (bf16[10,384,512]{2,1,0:T(8,128)(2,1)S(1)}, bf16[10,384,512]{2,1,0:T(8,128)(2,1)}, u32[]{:S(2)}) copy-start(bf16[10,384,512]{2,1,0:T(8,128)(2,1)} %get-tuple-element.63) | copy-start | bytes 11796484
  311.2 6.3 %copy-start.4 = (bf16[1,4,384,512]{3,2,1,0:T(8,128)(2,1)S(1)}, bf16[1,4,384,512]{3,2,1,0:T(8,128)(2,1)}, u32[]{:S(2)}) copy-start(bf16[1,4,384,512]{3,2,1,0:T(8,128)(2,1)} %get-tuple-element.64) | copy-start | bytes 4718596
  315.7 2.5 copy-start.2
  318.2 4.5 %copy-start.3 = (bf16[8,48,2688]{2,1,0:T(8,128)(2,1)S(1)}, bf16[8,48,2688]{2,1,0:T(8,128)(2,1)}, u32[]{:S(2)}) copy-start(bf16[8,48,2688]{2,1,0:T(8,128)(2,1)} %get-tuple-element.61) | copy-start | bytes 6193156
  323.1 1.9 copy-start
  328.4 3.3 copy-start.8
  328.4 4.1 %copy-start.6 = (f32[128,1536]{1,0:T(8,128)S(1)}, f32[128,1536]{1,0:T(8,128)}, u32[]{:S(2)}) copy-start(f32[128,1536]{1,0:T(8,128)} %get-tuple-element.85) | copy-start | bytes 2359300

commit v4 on v3

--- a/solution.py
+++ b/solution.py
@@ -283,6 +283,11 @@
         self.a, self.b = self.e // self.side, self.e % self.side
         self.x, self.c = self.f // 2, self.f % 2
 
+    def detour(self):
+        end = self.line - 1
+        got = jnp.where(self.a % 2 == 0, end, 0)
+        return got, end - got, self.e + jnp.where(self.a % 2 == 0, self.side, -self.side)
+
     def others(self, all_fsdp):
         out = [((self.f, self.e + self.side), self.a < self.line - 1)]
         out.append(((self.f, self.e - self.side), self.a > 0))
@@ -324,8 +329,9 @@
 
 
 class LineGather:
-    def __init__(self, at, buf, send, recv):
+    def __init__(self, at, buf, send, recv, balance=False):
         self.at, self.buf, self.send, self.recv = at, buf, send, recv
+        self.balance = balance
         width, count = buf.shape[2], recv.shape[0]
         cut = [width * p // count // 128 * 128 for p in range(count)] + [width]
         self.parts = [pl.ds(lo, hi - lo) for lo, hi in zip(cut, cut[1:])]
@@ -344,7 +350,7 @@
         at = self.at
         return self.copy(k, p, 1 + i, at.a * at.side + (at.b + i) % at.side)
 
-    def spread(self, k, p, up, down):
+    def spread(self, k, p, up, down, across=True):
         at = self.at
         if up:
 
@@ -358,14 +364,21 @@
             def _():
                 self.down(k, p).start()
 
-        for i in range(1, at.side):
-            self.across(k, i, p).start()
+        if across and (p < len(self.parts) - 1 or not self.balance):
+            self.across(k, 1, p).start()
+        elif across:
+            pl.when(k // at.side != at.detour()[0])(lambda: self.across(k, 1, p).start())
+
+    def detour(self):
+        at = self.at
+        k = at.detour()[1] * at.side + 1 - at.b
+        return self.copy(k, len(self.parts) - 1, 3, at.detour()[2])
 
     def begin(self):
         for p in range(len(self.parts)):
             self.spread(self.at.e, p, True, True)
 
-    def relay_step(self, s):
+    def relay_step(self, s, across=True):
         at = self.at
         for p in range(len(self.parts)):
 
@@ -373,13 +386,23 @@
             def _(p=p):
                 k = at.e - s * at.side
                 self.down(k, p).wait_recv()
-                self.spread(k, p, True, False)
+                self.spread(k, p, True, False, across)
 
             @pl.when(at.a + s < at.line)
             def _(p=p):
                 k = at.e + s * at.side
                 self.up(k, p).wait_recv()
-                self.spread(k, p, False, True)
+                self.spread(k, p, False, True, across)
+
+    def cross(self, n):
+        at = self.at
+        a = (
+            jnp.where(at.a > 0, at.a - 1, at.a + 1),
+            jnp.where(at.a == 0, 2, jnp.where(at.a == at.line - 1, at.a - 2, at.a + 1)),
+            jnp.where(at.a < at.line // 2, at.line - 1, 0),
+        )[n - 1]
+        for p in range(len(self.parts)):
+            self.spread(a * at.side + at.b, p, False, False)
 
     def relay(self):
         for s in range(1, self.at.line):
@@ -406,12 +429,13 @@
 
             @pl.when((a >= 0) & (a < at.line) & (n != 1))
             def _():
-                for i in range(1, at.side):
-                    k = a * at.side + (at.b + i) % at.side
-                    for p in range(len(self.parts)):
-                        self.across(k, i, p).wait_recv()
-                    if use is not None:
-                        use(k)
+                k = a * at.side + 1 - at.b
+                for p in range(len(self.parts)):
+                    self.across(k, 1, p).wait_recv()
+                if self.balance:
+                    pl.when(a == at.detour()[1])(lambda: self.detour().start())
+                if use is not None:
+                    use(k)
 
             return carry
 
@@ -431,26 +455,52 @@
                 def _(k=k, p=p):
                     self.down(k, p).wait_send()
 
-                for i in range(1, at.side):
-                    self.across(k, i, p).wait_send()
+                if p < len(self.parts) - 1 or not self.balance:
+                    self.across(k, 1, p).wait_send()
+                else:
+                    pl.when(s != at.detour()[0])(
+                        lambda k=k, p=p: self.across(k, 1, p).wait_send()
+                    )
+        if self.balance:
+            self.detour().wait_send()
 
 
 class LineScatter:
-    def __init__(self, at, part, side_in, line_in, own, sems):
+    def __init__(self, at, part, side_in, line_in, own, extra, sems, balance=False):
+        self.balance = balance
         self.at, self.part, self.side_in, self.line_in, self.own = at, part, side_in, line_in, own
-        self.ssend, self.srecv, self.lsend, self.lrecv = sems
-
-    def across(self, s, i):
+        self.extra = extra
+        self.ssend, self.srecv, self.lsend, self.lrecv, self.esem = sems
+        width = part.shape[2]
+        self.cut = width // 256 * 128
+        self.parts = (pl.ds(0, self.cut), pl.ds(self.cut, width - self.cut))
+
+    def across(self, s, p):
         at = self.at
-        b = (at.b + i) % at.side
-        j = at.side - 1 - i
         return remote(
-            self.part.at[s * at.side + b],
-            self.side_in.at[s, j],
-            self.ssend.at[s, i - 1],
-            self.srecv.at[s, j],
-            (at.f, at.a * at.side + b),
+            self.part.at[s * at.side + 1 - at.b, :, self.parts[p]],
+            self.side_in.at[s, :, self.parts[p]],
+            self.ssend.at[s, p],
+            self.srecv.at[s, p],
+            (at.f, at.a * at.side + 1 - at.b),
         )
+
+    def detour(self):
+        at = self.at
+        k = at.detour()[0] * at.side + 1 - at.b
+        return remote(
+            self.part.at[k, :, self.parts[1]], self.extra, self.esem.at[0], self.esem.at[1],
+            (at.f, at.detour()[2]),
+        )
+
+    def join(self):
+        at = self.at
+        s = at.detour()[1]
+        k = s * at.side + 1 - at.b
+        self.detour().wait_recv()
+        mine = self.part[k, :, self.cut :].astype(F32)
+        self.part[k, :, self.cut :] = (mine + self.extra[...].astype(F32)).astype(BF16)
+        self.across(s, 1).start()
 
     def along(self, s, dev, slot):
         at = self.at
@@ -473,31 +523,57 @@
         at = self.at
         return jnp.where(at.a < at.line // 2, at.line - 1 - i, i)
 
+    def middle(self):
+        at = self.at
+        return (at.a > 0) & (at.a < at.line - 1)
+
+    def launch(self, make, lo, hi):
+        at = self.at
+        got, passed, _ = at.detour()
+
+        def step(n, carry):
+            s = self.place(n)
+            make(s * at.side + 1 - at.b)
+            self.across(s, 0).start()
+            if self.balance:
+                pl.when(s == got)(lambda: self.detour().start())
+                pl.when((s != got) & (s != passed))(lambda: self.across(s, 1).start())
+            else:
+                self.across(s, 1).start()
+            return carry
+
+        lax.fori_loop(lo, hi, step, 0)
+
     def begin(self, make):
+        self.launch(make, 0, 2)
+
+    def more(self, make):
         at = self.at
+        if self.balance:
+            pl.when(self.middle())(self.join)
+        self.launch(make, 2, at.line)
 
         def step(n, carry):
-            s, i = self.place(n % at.line), n // at.line + 1
-            make(s * at.side + (at.b + i) % at.side)
-
-            @pl.when(i < at.side)
-            def _():
-                self.across(s, i).start()
-
+            make(n * at.side + at.b)
             return carry
 
-        lax.fori_loop(0, at.owners, step, 0)
+        lax.fori_loop(0, at.line, step, 0)
 
     def sum_step(self, n):
         at = self.at
+        if n == 1 and self.balance:
+            pl.when(jnp.logical_not(self.middle()))(self.join)
         s = self.place(n)
         k = s * at.side + at.b
-        for i in range(1, at.side):
-            self.across(s, i).wait_recv()
-        total = self.part[k].astype(F32)
-        for j in range(at.side - 1):
-            total = total + self.side_in[s, j].astype(F32)
-        self.own[...] = total
+        got = at.detour()[0]
+        self.own[...] = self.part[k].astype(F32)
+        self.across(s, 0).wait_recv()
+        self.own[:, : self.cut] += self.side_in[s, :, : self.cut].astype(F32)
+
+        @pl.when((s != got) | (not self.balance))
+        def _():
+            self.across(s, 1).wait_recv()
+            self.own[:, self.cut :] += self.side_in[s, :, self.cut :].astype(F32)
 
         @pl.when(((s > at.a) & (at.a > 0)) | ((s < at.a) & (at.a < at.line - 1)))
         def _():
@@ -530,9 +606,13 @@
 
     def finish(self):
         at = self.at
+        if self.balance:
+            self.detour().wait_send()
         for s in range(at.line):
-            for i in range(1, at.side):
-                self.across(s, i).wait_send()
+            self.across(s, 0).wait_send()
+            pl.when((s != at.detour()[0]) | (not self.balance))(
+                lambda s=s: self.across(s, 1).wait_send()
+            )
 
             @pl.when(at.a < s)
             def _(s=s):
@@ -711,14 +791,17 @@
     for n in (1, 2):
         for i in range(2):
             pass_x(n, i)
-    cotg.relay_step(1)
+    cotg.relay_step(1, False)
+    cotg.cross(1)
     pass_x(0, 0)
-    cotg.relay_step(2)
+    cotg.relay_step(2, False)
     pass_x(0, 1)
+    cotg.cross(2)
     for n in (1, 2, 0):
         pass_rest(n)
-    cotg.relay_step(3)
     pass_x(3, 0)
+    cotg.relay_step(3, False)
+    cotg.cross(3)
     add(far)
     for n in range(3):
         from_sib(n)
@@ -726,6 +809,9 @@
     small_x().wait_recv()
     small_sib().start()
     pass_x(3, 1)
+    save = [pltpu.make_async_copy(bufs[n], fulls[n], lsem.at[n]) for n in range(count)]
+    for c in save[:3]:
+        c.start()
 
     for j in range(16):
         cols = slice(128 * j, 128 * (j + 1))
@@ -791,8 +877,7 @@
     meta = rank + pltpu.roll(high, experts, 1) + pltpu.roll(low, 2 * experts, 1)
     sent[:, MODEL_WIDTH:] = meta.astype(BF16)
 
-    save = [pltpu.make_async_copy(bufs[n], fulls[n], lsem.at[n]) for n in range(count)]
-    for c in save:
+    for c in save[3:]:
         c.start()
     cotg.rest()
     cotg.finish()
@@ -858,7 +943,7 @@
             dma((n, 2)),
             dma((n, 5)),
             dma((n, 5)),
-            dma((2, side + 1, owners)),
+            dma((2, side + 2, owners)),
             dma((2, owners)),
             dma((2, shards - 1)),
             dma((2, shards - 1)),
@@ -872,13 +957,14 @@
 
 
 EARLY = 4
+AHEAD = 2
 
 
 def moe_kernel(sizes, sent, cot, wgu, wd, back_out, comb_out, sums, far, away, *scratch):
     shards, owners, tokens, experts, held, pairing = sizes
     (rows_all, cot_buf, taken, cots, made, grads, slot_gate, slot_grad, place, wg_buf, wd_buf,
-     acts, dus, gg, gd, from_core, stage, side1, line1,
-     rs, rr, wsem, csem, coresend, corerecv, farsend, farrecv, osem, free, s1, s2, s3, s4,
+     acts, dus, gg, gd, from_core, stage, side1, line1, extra1,
+     rs, rr, wsem, csem, coresend, corerecv, farsend, farrecv, osem, free, s1, s2, s3, s4, s5,
      ) = scratch
     at = Place(shards, owners)
     groups = held // pairing
@@ -1017,10 +1103,6 @@
         for c in to_core(h):
             c.wait()
 
-        @pl.when(h >= 2)
-        def _():
-            leave(h - 2)
-
         for i in range(at.chips):
             x = (at.x + i) % at.chips
             f = 2 * x + at.c
@@ -1058,10 +1140,6 @@
 
         for c in to_core(h):
             c.start()
-
-        @pl.when(h > 0)
-        def _():
-            add(h - 1)
 
     home = (col == e_row).astype(F32).astype(BF16)
     home_low = (col == e_row + experts).astype(F32).astype(BF16)
@@ -1078,7 +1156,7 @@
             rows_all[k, :, lo:hi] = dot(pt, dx).astype(BF16)
         rows_all[k, :, MODEL_WIDTH:] = dot(pt, high * home + low * home_low).astype(BF16)
 
-    back = LineScatter(at, rows_all, side1, line1, back_out, (s1, s2, s3, s4))
+    back = LineScatter(at, rows_all, side1, line1, back_out, extra1, (s1, s2, s3, s4, s5), True)
 
     def step(i, carry):
         @pl.when(i < groups)
@@ -1088,20 +1166,30 @@
         @pl.when(i == groups)
         def _():
             back.begin(make_back)
-
-        @pl.when(i >= 1)
-        def _():
-            weigh(i - 1)
-
-        @pl.when(i == held - 1)
-        def _():
-            back.sum_step(0)
+            back.more(make_back)
+
+        def staged(back, act):
+            h = jnp.where(i < groups, i, i - gap) - back
+            early = (i >= back) & (i < AHEAD + back)
+            pl.when(early | (i >= groups + back))(lambda: act(h))
+
+        staged(2, leave)
+        staged(0, weigh)
+        staged(1, add)
+
+        for n in range(2):
+
+            @pl.when(i == groups + 3 + 4 * n)
+            def _(n=n):
+                back.sum_step(n)
 
         return carry
 
-    lax.fori_loop(0, held + 1, step, 0)
+    gap = groups - AHEAD
+    lax.fori_loop(0, held + gap, step, 0)
+    leave(held - 2)
     add(held - 1)
-    back.sum_step(1)
+    back.sum_step(2)
 
     def combine(k, carry):
         to = pl.ds(k * CAP, CAP)
@@ -1127,9 +1215,7 @@
         return carry
 
     lax.fori_loop(0, owners, combine, 0)
-    for h in range(held - 2, held):
-        leave(h)
-    back.sum_step(2)
+    leave(held - 1)
     back.sum_step(3)
     back.sum_last()
     back.finish()
@@ -1150,7 +1236,7 @@
         for n in range(2):
             out.append(
                 remote(
-                    away[n].at[h, i - 1], far[n].at[back, j], send.at[n, i - 1, j],
+                    away[n].at[h, i - 1], far[n].at[back, h], send.at[n, i - 1, j],
                     recv.at[n, back, j], dev,
                 )
             )
@@ -1186,7 +1272,7 @@
             jax.ShapeDtypeStruct((tokens, width), F32),
             jax.ShapeDtypeStruct((owners, tokens, MODEL_WIDTH), BF16),
             outs((held,)),
-            outs((chips - 1, EARLY)),
+            outs((chips - 1, held)),
             outs((held, chips - 1)),
         ),
         in_specs=[any_] * 4,
@@ -1209,9 +1295,10 @@
             vm((2, half, MODEL_WIDTH), BF16),
             pair((2, chips)),
             pair((2, chips)),
-            vm((line, side - 1, tokens, width), BF16),
+            vm((line, tokens, width), BF16),
             vm((line + 1, tokens, width), BF16),
-            dma((2, side + 1, owners)),
+            vm((tokens, width - width // 256 * 128), BF16),
+            dma((2, side + 2, owners)),
             dma((2, owners)),
             dma((2, 2 * pairing)),
             dma((2,)),
@@ -1221,10 +1308,11 @@
             dma((2, chips - 1, EARLY)),
             dma((2 * chips, 2)),
             pltpu.SemaphoreType.REGULAR,
-            dma((line, side)),
-            dma((line, side)),
+            dma((line, 2)),
+            dma((line, 2)),
             dma((line,)),
             dma((line + 1,)),
+            dma((2,)),
         ],
         compiler_params=pltpu.CompilerParams(
             collective_id=1, has_side_effects=True, vmem_limit_bytes=63 * 2**20
@@ -1233,12 +1321,12 @@
 
 
 def reverse_kernel(sizes, hidden, doc, routes, gain_a, gain_f, cot, q, k, v, mixed, lse, resid, sent,
-                   probs, back, wo, wr, wq, wk, wv, comb, left_in, away0, away1, *refs):
+                   probs, back, wo, wr, wq, wk, wv, comb, left_in, away0, away1, far0, far1, *refs):
     shards, owners, tokens, experts, held = sizes
-    block_out, grad_in, total_o, total_q, far = refs[:5]
+    block_out, grad_in, out_o, out_q, out_k, out_v, out_r, far = refs[:8]
     (w_bufs, left, turned, rights, dgrad, dattn_f, dqkv, aux, aux_in, comb_part, comb_side, comb_line,
-     comb_own, part_o, side_o, line_o, own_o, part_q, side_q, line_q, own_q,
-     wsem, rsend, rrecv, asend, arecv, farsend, farrecv, *sems) = refs[5:]
+     comb_own, comb_x, part_o, side_o, line_o, own_o, extra_o, part_q, side_q, line_q, own_q, extra_q,
+     total_o, total_q, wsem, rsend, rrecv, asend, arecv, farsend, farrecv, *sems) = refs[8:]
     at = Place(shards, owners)
     away = (away0, away1)
     rg = MODEL_WIDTH // shards
@@ -1257,13 +1345,14 @@
         c.start()
     at.meet(all_fsdp=True)
 
-    combine = LineScatter(at, comb_part, comb_side, comb_line, comb_own, sems[:4])
-    outer = LineScatter(at, part_o, side_o, line_o, own_o, sems[4:8])
-    inner = LineScatter(at, part_q, side_q, line_q, own_q, sems[8:12])
-    outer_all = LineGather(at, total_o, sems[12], sems[13])
-    inner_all = LineGather(at, total_q, sems[14], sems[15])
+    combine = LineScatter(at, comb_part, comb_side, comb_line, comb_own, comb_x, sems[:5], True)
+    outer = LineScatter(at, part_o, side_o, line_o, own_o, extra_o, sems[5:10], True)
+    inner = LineScatter(at, part_q, side_q, line_q, own_q, extra_q, sems[10:15], True)
+    outer_all = LineGather(at, total_o, sems[15], sems[16])
+    inner_all = LineGather(at, total_q, sems[17], sems[18])
     loads[0].wait()
-    combine.begin(lambda k: None)
+    nothing = lambda k: None
+    combine.begin(nothing)
 
     def rows(i):
         return pl.ds(pl.multiple_of(i * tokens, tokens), tokens)
@@ -1318,6 +1407,7 @@
     for c in late(EARLY):
         c.start()
     dattn_f[...] = dot(dattn, full(0), 1, 1).astype(BF16)
+    combine.more(nothing)
 
     allowed = visible(doc[...], tokens)
     cos, sin, first = rope_of(allowed, tokens)
@@ -1347,16 +1437,28 @@
         dqkv[:, kept + g * HEAD_SIZE : kept + (g + 1) * HEAD_SIZE] = dot(ds, qs, 0, 0)
         at_v = kept + span + g * HEAD_SIZE
         dqkv[:, at_v : at_v + HEAD_SIZE] = dot(low, dos, 0, 0)
-        if g == 2:
+        if g == 3:
             combine.sum_step(0)
-        if g == 5:
-            pass_rights(0)
 
     for j in range((kept + span) // 128):
         cols = slice(128 * j, 128 * (j + 1))
         rights[rows(f), cols] = turn(dqkv[:, cols], cos, -sin, first).astype(BF16)
     rights[rows(f), kept + span : split] = dqkv[:, kept + span :].astype(BF16)
     send_rights(1)
+    pass_rights(0)
+    loads[6].wait()
+    turned[...] = left[...].T
+    take_rights(0)
+    step = 512
+
+    def product(part, half, lo, hi):
+        for a in range(lo, hi, step):
+            got = dot(turned[half * rg : (half + 1) * rg], rights[:, a : a + step]).astype(BF16)
+            for i in range(owners):
+                part[i, :, a - lo : a - lo + step] = got[i * piece : (i + 1) * piece]
+
+    product(part_o, 1, split, split + MODEL_WIDTH)
+    outer.begin(nothing)
     combine.sum_step(1)
     for i in range(3, 6):
         loads[i].wait()
@@ -1387,22 +1489,10 @@
             c.start()
     aux_in[0] = aux[:, cols(f)]
 
-    loads[6].wait()
-    turned[...] = left[...].T
-    take_rights(0)
-    step = 512
-
-    def product(part, half, lo, hi):
-        for a in range(lo, hi, step):
-            got = dot(turned[half * rg : (half + 1) * rg], rights[:, a : a + step]).astype(BF16)
-            for i in range(owners):
-                part[i, :, a - lo : a - lo + step] = got[i * piece : (i + 1) * piece]
-
-    product(part_o, 1, split, split + MODEL_WIDTH)
-    outer.begin(lambda k: None)
+    outer.more(nothing)
     combine.sum_step(2)
+    combine.sum_step(3)
     pass_rights(1)
-    combine.sum_step(3)
     outer.sum_step(0)
     combine.sum_last()
     block_out[...] = (resid[...] + comb_own[...]).astype(BF16)
@@ -1416,25 +1506,43 @@
     product(part_q, 0, 0, split)
     for i in range(owners):
         part_q[i, :, split:] = extra[i * piece : (i + 1) * piece]
-    inner.begin(lambda k: None)
+    inner.begin(nothing)
     for i in range(1, 4):
         outer.sum_step(i)
     outer.sum_last()
+    inner.more(nothing)
     total_o[at.e] = own_o[...].astype(BF16)
     outer_all.begin()
     inner.sum_step(0)
+    outer_all.relay_step(1)
     inner.sum_step(1)
-    outer_all.relay_step(1)
     inner.sum_step(2)
     outer_all.relay_step(2)
     inner.sum_step(3)
-    outer_all.relay_step(3)
     inner.sum_last()
     total_q[at.e] = own_q[...].astype(BF16)
     inner_all.begin()
+    outer_all.relay_step(3)
     inner_all.relay()
     outer_all.rest()
+
+    def shown(k, carry):
+        to = pl.ds(pl.multiple_of(k * piece, piece), piece)
+        out_o[to, :] = total_o[k]
+        return carry
+
+    lax.fori_loop(0, owners, shown, 0)
     inner_all.rest()
+
+    def shown_too(k, carry):
+        to = pl.ds(pl.multiple_of(k * piece, piece), piece)
+        out_q[to, :] = total_q[k, :, :kept]
+        out_k[to, :] = total_q[k, :, kept : kept + span]
+        out_v[to, :] = total_q[k, :, kept + span : split]
+        out_r[to, :] = total_q[k, :, split:]
+        return carry
+
+    lax.fori_loop(0, owners, shown_too, 0)
     for chunk in range(2):
         for i in range(3):
             block(chunk, f, i, sibling).wait_send()
@@ -1447,7 +1555,7 @@
             c.wait()
 
 
-def reverse(sizes, vmem_args, fulls, comb, left, away):
+def reverse(sizes, vmem_args, fulls, comb, left, away, far):
     shards, owners, tokens, experts, held = sizes
     rg = MODEL_WIDTH // shards
     piece = rg // owners
@@ -1463,9 +1571,10 @@
     def scatter(rows, width):
         return [
             vm((owners, rows, width), BF16),
-            vm((line, side - 1, rows, width), BF16),
+            vm((line, rows, width), BF16),
             vm((line + 1, rows, width), BF16),
             vm((rows, width), F32),
+            vm((rows, width - width // 256 * 128), BF16),
         ]
 
     shape = jax.ShapeDtypeStruct
@@ -1475,12 +1584,16 @@
         out_shape=(
             shape((tokens, MODEL_WIDTH), BF16),
             shape((tokens, MODEL_WIDTH), F32),
-            shape((owners, piece, MODEL_WIDTH), BF16),
-            shape((owners, piece, wide), BF16),
-            tuple(shape((chips - 1, held - EARLY, *a.shape[2:]), BF16) for a in away),
+            shape((rg, MODEL_WIDTH), BF16),
+            shape((rg, MODEL_WIDTH), BF16),
+            shape((rg, KEY_VALUE_HEADS * HEAD_SIZE), BF16),
+            shape((rg, KEY_VALUE_HEADS * HEAD_SIZE), BF16),
+            shape((rg, 128), BF16),
+            tuple(shape(r.shape, BF16) for r in far),
         ),
-        in_specs=[vmem] * len(vmem_args) + [any_] * 9,
-        out_specs=(vmem, vmem, vmem, vmem, (any_, any_)),
+        in_specs=[vmem] * len(vmem_args) + [any_] * 11,
+        out_specs=(*[vmem] * 7, (any_, any_)),
+        input_output_aliases={len(vmem_args) + 9: 7, len(vmem_args) + 10: 8},
         scratch_shapes=[
             tuple(vm(w.shape, BF16) for w in fulls),
             vm((shards * tokens, 2 * rg), BF16),
@@ -1494,6 +1607,8 @@
             *scatter(tokens, MODEL_WIDTH),
             *scatter(piece, MODEL_WIDTH),
             *scatter(piece, wide),
+            vm((owners, piece, MODEL_WIDTH), BF16),
+            vm((owners, piece, wide), BF16),
             dma((7,)),
             dma((2, 3)),
             dma((2, shards)),
@@ -1501,13 +1616,74 @@
             dma((shards - 1,)),
             dma((2, chips - 1, held - EARLY)),
             dma((2, chips - 1, held - EARLY)),
-            *([dma((line, side)), dma((line, side)), dma((line,)), dma((line + 1,))] * 3),
-            *([dma((1, side + 1, owners)), dma((1, owners))] * 2),
+            *([dma((line, 2)), dma((line, 2)), dma((line,)), dma((line + 1,)), dma((2,))] * 3),
+            *([dma((2, side + 2, owners)), dma((2, owners))] * 2),
         ],
         compiler_params=pltpu.CompilerParams(
             collective_id=2, has_side_effects=True, vmem_limit_bytes=63 * 2**20
         ),
-    )(*vmem_args, *fulls, comb, left, *away)
+    )(*vmem_args, *fulls, comb, left, *away, *far)
+
+
+def finish_kernel(experts, *refs):
+    (s0, r0, s1, r1, q, k, v, o, extra, rows, gradient), outs = refs[:11], refs[11:]
+    o0, o1, oq, ok, ov, oo, orouter, oga, ogf, orows, ograd = outs
+    for a, b, c in ((s0, r0, o0), (s1, r1, o1)):
+        total = a[...].astype(F32)
+        for i in range(b.shape[0]):
+            total = total + b[i].astype(F32)
+        c[...] = total
+    for a, b in ((q, oq), (k, ok), (v, ov), (o, oo)):
+        b[...] = a[...].astype(F32)
+    orows[...] = rows[...]
+    ograd[...] = gradient[...]
+
+    @pl.when(pl.program_id(0) == 0)
+    def _():
+        turned = extra[...].astype(F32).T
+        orouter[...] = turned[:experts]
+        oga[...] = turned[experts]
+        ogf[...] = turned[experts + 1]
+
+
+def finish(experts, sums, far, grads, extra, rows, gradient):
+    steps = 8
+    rg = sums[0].shape[1]
+    two = [s.reshape(-1, s.shape[2]) for s in sums]
+    away = [r.reshape(r.shape[0], -1, r.shape[3]) for r in far]
+
+    def rows_of(a):
+        return pl.BlockSpec((a.shape[0] // steps, a.shape[1]), lambda i: (i, 0))
+
+    def deep(a):
+        return pl.BlockSpec((a.shape[0], a.shape[1] // steps, a.shape[2]), lambda i: (0, i, 0))
+
+    def whole(shape):
+        return pl.BlockSpec(shape, lambda i: (0,) * len(shape))
+
+    shape = jax.ShapeDtypeStruct
+    small = [(experts, rg), (rg,), (rg,)]
+    out = pl.pallas_call(
+        functools.partial(finish_kernel, experts),
+        name="finish",
+        grid=(steps,),
+        out_shape=(
+            *[shape(a.shape, F32) for a in two],
+            *[shape(a.shape, F32) for a in grads],
+            *[shape(a, F32) for a in small],
+            shape(rows.shape, rows.dtype),
+            shape(gradient.shape, F32),
+        ),
+        in_specs=[
+            rows_of(two[0]), deep(away[0]), rows_of(two[1]), deep(away[1]),
+            *[rows_of(a) for a in grads], whole(extra.shape), rows_of(rows), rows_of(gradient),
+        ],
+        out_specs=(
+            *[rows_of(a) for a in two], *[rows_of(a) for a in grads], *[whole(a) for a in small],
+            rows_of(rows), rows_of(gradient),
+        ),
+    )(two[0], away[0], two[1], away[1], *grads, extra, rows, gradient)
+    return out[0].reshape(sums[0].shape), out[1].reshape(sums[1].shape), *out[2:]
 
 
 def plain_local(
@@ -1688,7 +1864,7 @@
     sizes = (shards, owners, tokens, experts, held, pairing)
     back, comb, sums, far, away = moe(sizes, sent, cot_all, w_gateup, w_down)
     wq, wk, wv, wo, wr = fulls
-    block_out, grad_input, total_o, total_q, far_late = reverse(
+    block_out, grad_input, total_o, total_q, total_k, total_v, total_r, far = reverse(
         (shards, owners, tokens, experts, held),
         (hidden_in, doc_ids, routes.T, gain_attn, gain_ffn, cotangent, q, k, v, mixed,
          lse, resid, sent, probs, back),
@@ -1696,24 +1872,22 @@
         comb,
         left,
         away,
-    )
-    grad_gateup, grad_down = (
-        s.astype(f32)
-        + jnp.sum(jnp.concatenate([r, t], axis=1).astype(f32), axis=0)
-        for s, r, t in zip(sums, far, far_late)
-    )
-    grad_output = total_o.reshape(-1, MODEL_WIDTH).astype(f32)
-    rest = total_q.reshape(-1, total_q.shape[2]).astype(f32)
+        far,
+    )
+    out = finish(
+        experts, sums, far, (total_q, total_k, total_v, total_o), total_r, block_out, grad_input
+    )
+    grad_gateup, grad_down, grad_q, grad_k, grad_v, grad_o, grad_r, ga, gf, block, gradient = out
     return (
-        block_out,
-        grad_input,
-        rest[:, :1536],
-        rest[:, 1536:2048],
-        rest[:, 2048:2560],
-        grad_output,
-        rest[:, 2560 : 2560 + experts],
-        rest[:, 2560 + experts],
-        rest[:, 2561 + experts],
+        block,
+        gradient,
+        grad_q,
+        grad_k,
+        grad_v,
+        grad_o,
+        grad_r.T,
+        ga,
+        gf,
         grad_gateup,
         grad_down,
     )

time: 334 us -> 321 us (0.961); the launches traced: 333 us -> 316 us
  other arithmetic: 11.2 us -> 0 us
  local copies, waits for them, and re-layouts: 11 us -> 0 us
  Pallas kernels: 310 us -> 315 us
    pallas_call x0 -> x1, Pallas kernels: none -> 14.6 us  [finish(): pl.pallas_call(functools.partial(finish_kernel, experts), name='finish',...]
    add x2 -> x0, other arithmetic: 9 us -> none  [kernel_local(): s.astype(f32) + jnp.sum(jnp.concatenate([r, t], axis=1).astype(f32), axis=0)]
    slice x4 -> x0, local copies, waits for them, and re-layouts: 7.08 us -> none  [the longest x1 3.32 us: kernel_local(): rest[:, :1536]]
    pallas_call x1, Pallas kernels: 125 us -> 121 us  [moe(): pl.pallas_call(functools.partial(moe_kernel, sizes), name='moe', out_shap...]
    unnamed x21 -> x0, local copies, waits for them, and re-layouts: 3.87 us -> none
    pallas_call x1, Pallas kernels: 67 us -> 63.2 us  [attend(): pl.pallas_call(functools.partial(attend_kernel, sizes), name='attend', ou...]
where the time goes in v4:
time: 321 us; the launch traced here: 316 us
  Pallas kernels  315 us (98%)
    pallas_call x1, Pallas kernels, moe(): pl.pallas_call(functools.partial(moe_kernel, sizes), name='moe', out_shap...  121 us
    pallas_call x1, Pallas kernels, reverse(): pl.pallas_call(functools.partial(reverse_kernel, sizes), name='reverse',...  117 us
    pallas_call x1, Pallas kernels, attend(): pl.pallas_call(functools.partial(attend_kernel, sizes), name='attend', ou...  63.2 us
    pallas_call x1, Pallas kernels, finish(): pl.pallas_call(functools.partial(finish_kernel, experts), name='finish',...  14.6 us

profile of v4, /device:TPU:0, one launch (start us, length us, event | category | flops | bytes accessed | tf_op | source)
XLA Modules:
  0.0 316.0 jit_solution(316779216030705208)
XLA Ops:
  0.6 63.2 %attend.1 = (bf16[128,1536]{1,0:T(8,128)(2,1)}, bf16[128,1536]{1,0:T(8,128)(2,1)}, bf16[128,512]{1,0:T(8,128)(2,1)}, bf16[128,512]{1,0:T(8,128)(2,1)}, bf16[128,...) custom-call(bf16[128,1536]{1,0:T(8,128)(2,1)} %hidden.3, ...), custom_call_target="tpu_custom_call" | custom-call | tf_op jit(solution)/shard_map/attend/pallas_call | solution.py:916
  63.9 120.8 %moe.1 = (f32[128,1664]{1,0:T(8,128)}, bf16[8,128,1536]{2,1,0:T(8,128)(2,1)}, bf16[10,384,512]{2,1,0:T(8,128)(2,1)}, bf16[10,64,1536]{2,1,0:T(8,128)(2,1)}, bf16...) custom-call(bf16[128,1664]{1,0:T(8,128)(2,1)} %get-tuple-element.54., ...), custom_call_target="tpu_custom_call" | custom-call | tf_op jit(solution)/shard_map/moe/pallas_call | solution.py:1268
  184.7 116.5 %reverse.1 = (bf16[128,1536]{1,0:T(8,128)(2,1)}, f32[128,1536]{1,0:T(8,128)}, bf16[384,1536]{1,0:T(8,128)(2,1)}, bf16[384,1536]{1,0:T(8,128)(2,1)}, bf16[384,512...) custom-call(bf16[128,1536]{1,0:T(8,128)(2,1)} %hidden.3, ...), custom_call_target="tpu_custom_call", output_to_operand_aliasing={{7}: (24, {}), {8}: (25, {})} | custom-call | tf_op jit(solution)/shard_map/reverse/pallas_call | solution.py:1581
  301.2 14.6 %finish.1 = (f32[3840,512]{1,0:T(8,128)}, f32[640,1536]{1,0:T(8,128)}, f32[384,1536]{1,0:T(8,128)}, f32[384,512]{1,0:T(8,128)}, f32[384,512]{1,0:T(8,128)}, /*in...) custom-call(bf16[3840,512]{1,0:T(8,128)(2,1)} %bitcast.11, ...), custom_call_target="tpu_custom_call" | custom-call | tf_op jit(solution)/shard_map/finish/pallas_call | solution.py:1666

commit v5 on v4

--- a/solution.py
+++ b/solution.py
@@ -749,7 +749,7 @@
             lefts(n, i).start()
 
     at.meet(all_fsdp=True)
-    order = (1, 2, 0, 3)
+    order = (0, 1, 2, 3)
     for n in order[:3]:
         for i in range(2):
             out_x(n, i).start()
@@ -788,16 +788,16 @@
     for n in range(3):
         own_sib(n).wait_recv()
     add(sib[0])
+    pass_x(0, 0)
+    cotg.relay_step(1, False)
+    cotg.cross(1)
+    pass_x(0, 1)
+    cotg.relay_step(2, False)
     for n in (1, 2):
         for i in range(2):
             pass_x(n, i)
-    cotg.relay_step(1, False)
-    cotg.cross(1)
-    pass_x(0, 0)
-    cotg.relay_step(2, False)
-    pass_x(0, 1)
     cotg.cross(2)
-    for n in (1, 2, 0):
+    for n in range(3):
         pass_rest(n)
     pass_x(3, 0)
     cotg.relay_step(3, False)
@@ -842,15 +842,19 @@
 
     send_left(0)
     send_left(1)
-    pass_rest(3)
+
+    def output(g):
+        return dot(mixed[:, pl.ds(pl.multiple_of(g * rg, 128), rg)], bufs[3][g])
+
     for n in (3, 4):
         own[n].wait()
         own_sib(n).wait_recv()
+    resid[...] = x + output(f) + output(sib[0])
+    pass_rest(3)
+    resid[...] += output(far)
     small_sib().wait_recv()
     from_sib(3)
-    total = x
-    for g in range(shards):
-        total = total + dot(mixed[:, g * rg : (g + 1) * rg], bufs[3][g])
+    total = resid[...] + output(other)
     resid[...] = total
     scale = lax.rsqrt(jnp.mean(total * total, axis=1, keepdims=True) + EPS)
     h2 = (total * scale * gain_f[...].reshape(1, -1)).astype(BF16)
@@ -963,7 +967,7 @@
 def moe_kernel(sizes, sent, cot, wgu, wd, back_out, comb_out, sums, far, away, *scratch):
     shards, owners, tokens, experts, held, pairing = sizes
     (rows_all, cot_buf, taken, cots, made, grads, slot_gate, slot_grad, place, wg_buf, wd_buf,
-     acts, dus, gg, gd, from_core, stage, side1, line1, extra1,
+     acts, dus, gg, gd, turned, from_core, stage, side1, line1, extra1,
      rs, rr, wsem, csem, coresend, corerecv, farsend, farrecv, osem, free, s1, s2, s3, s4, s5,
      ) = scratch
     at = Place(shards, owners)
@@ -1107,8 +1111,8 @@
             x = (at.x + i) % at.chips
             f = 2 * x + at.c
             for n, (buf, r) in enumerate(((gg, rg), (gd, rd))):
-                own = buf[slot, pl.ds(pl.multiple_of(f * r, r), r)].astype(F32)
-                stage[n][slot, i] = (own + from_core[n][slot, x].astype(F32)).astype(BF16)
+                own = buf[slot, pl.ds(pl.multiple_of(f * r, r), r)]
+                stage[n][slot, i] = own + from_core[n][slot, x]
         for c in keep(h):
             c.start()
 
@@ -1128,9 +1132,14 @@
     def weigh(h):
         g, slot = h // pairing, h % 2
         n = MODEL_WIDTH // 3
+
+        @pl.when(h % pairing == 0)
+        def _():
+            turned[...] = taken[g].T
+
         for i in range(3):
             gg[slot, i * n : (i + 1) * n, :] = dot(
-                taken[g, :, i * n : (i + 1) * n], dus[h], 0, 0
+                turned[i * n : (i + 1) * n], dus[h]
             ).astype(BF16)
         gd[slot] = dot(acts[h], cots[g], 0, 0).astype(BF16)
 
@@ -1179,7 +1188,7 @@
 
         for n in range(2):
 
-            @pl.when(i == groups + 3 + 4 * n)
+            @pl.when(i == groups + 3 + 3 * n)
             def _(n=n):
                 back.sum_step(n)
 
@@ -1187,8 +1196,6 @@
 
     gap = groups - AHEAD
     lax.fori_loop(0, held + gap, step, 0)
-    leave(held - 2)
-    add(held - 1)
     back.sum_step(2)
 
     def combine(k, carry):
@@ -1214,9 +1221,11 @@
 
         return carry
 
+    back.sum_step(3)
+    leave(held - 2)
+    add(held - 1)
     lax.fori_loop(0, owners, combine, 0)
     leave(held - 1)
-    back.sum_step(3)
     back.sum_last()
     back.finish()
 
@@ -1293,6 +1302,7 @@
             vm((held, rows, hidden), BF16),
             vm((2, MODEL_WIDTH, hidden), BF16),
             vm((2, half, MODEL_WIDTH), BF16),
+            vm((MODEL_WIDTH, rows), BF16),
             pair((2, chips)),
             pair((2, chips)),
             vm((line, tokens, width), BF16),
@@ -1647,7 +1657,7 @@
 
 
 def finish(experts, sums, far, grads, extra, rows, gradient):
-    steps = 8
+    steps = 2
     rg = sums[0].shape[1]
     two = [s.reshape(-1, s.shape[2]) for s in sums]
     away = [r.reshape(r.shape[0], -1, r.shape[3]) for r in far]

time: 321 us -> 315 us (0.981); the launches traced: 316 us -> 314 us
    pallas_call x1, Pallas kernels: 117 us -> 123 us  [reverse(): pl.pallas_call(functools.partial(reverse_kernel, sizes), name='reverse',...]
    pallas_call x1, Pallas kernels: 121 us -> 115 us  [moe(): pl.pallas_call(functools.partial(moe_kernel, sizes), name='moe', out_shap...]
where the time goes in v5:
time: 315 us; the launch traced here: 314 us
  Pallas kernels  313 us (99%)
    pallas_call x1, Pallas kernels, reverse(): pl.pallas_call(functools.partial(reverse_kernel, sizes), name='reverse',...  123 us
    pallas_call x1, Pallas kernels, moe(): pl.pallas_call(functools.partial(moe_kernel, sizes), name='moe', out_shap...  115 us
    pallas_call x1, Pallas kernels, attend(): pl.pallas_call(functools.partial(attend_kernel, sizes), name='attend', ou...  63.2 us
    pallas_call x1, Pallas kernels, finish(): pl.pallas_call(functools.partial(finish_kernel, experts), name='finish',...  12.5 us

profile of v5, /device:TPU:0, one launch (start us, length us, event | category | flops | bytes accessed | tf_op | source)
XLA Modules:
  0.0 314.1 jit_solution(2876569421318070529)
XLA Ops:
  0.6 63.2 %attend.1 = (bf16[128,1536]{1,0:T(8,128)(2,1)}, bf16[128,1536]{1,0:T(8,128)(2,1)}, bf16[128,512]{1,0:T(8,128)(2,1)}, bf16[128,512]{1,0:T(8,128)(2,1)}, bf16[128,...) custom-call(bf16[128,1536]{1,0:T(8,128)(2,1)} %hidden.3, ...), custom_call_target="tpu_custom_call" | custom-call | tf_op jit(solution)/shard_map/attend/pallas_call | solution.py:920
  63.9 114.7 %moe.1 = (f32[128,1664]{1,0:T(8,128)}, bf16[8,128,1536]{2,1,0:T(8,128)(2,1)}, bf16[10,384,512]{2,1,0:T(8,128)(2,1)}, bf16[10,64,1536]{2,1,0:T(8,128)(2,1)}, bf16...) custom-call(bf16[128,1664]{1,0:T(8,128)(2,1)} %get-tuple-element.54., ...), custom_call_target="tpu_custom_call" | custom-call | tf_op jit(solution)/shard_map/moe/pallas_call | solution.py:1277
  178.6 122.8 %reverse.1 = (bf16[128,1536]{1,0:T(8,128)(2,1)}, f32[128,1536]{1,0:T(8,128)}, bf16[384,1536]{1,0:T(8,128)(2,1)}, bf16[384,1536]{1,0:T(8,128)(2,1)}, bf16[384,512...) custom-call(bf16[128,1536]{1,0:T(8,128)(2,1)} %hidden.3, ...), custom_call_target="tpu_custom_call", output_to_operand_aliasing={{7}: (24, {}), {8}: (25, {})} | custom-call | tf_op jit(solution)/shard_map/reverse/pallas_call | solution.py:1591
  301.4 12.5 %finish.1 = (f32[3840,512]{1,0:T(8,128)}, f32[640,1536]{1,0:T(8,128)}, f32[384,1536]{1,0:T(8,128)}, f32[384,512]{1,0:T(8,128)}, f32[384,512]{1,0:T(8,128)}, /*in...) custom-call(bf16[3840,512]{1,0:T(8,128)(2,1)} %bitcast.11, ...), custom_call_target="tpu_custom_call" | custom-call | tf_op jit(solution)/shard_map/finish/pallas_call | solution.py:1676

commit v6 on v5

--- a/solution.py
+++ b/solution.py
@@ -1129,6 +1129,11 @@
             for c in to_chips(h):
                 c.start()
 
+        @pl.when(h == EARLY)
+        def _():
+            for c in to_chips(h)[0::2]:
+                c.start()
+
     def weigh(h):
         g, slot = h // pairing, h % 2
         n = MODEL_WIDTH // 3
@@ -1168,6 +1173,10 @@
     back = LineScatter(at, rows_all, side1, line1, back_out, extra1, (s1, s2, s3, s4, s5), True)
 
     def step(i, carry):
+        @pl.when((i >= 2) & (i < AHEAD + 2))
+        def _():
+            leave(i - 2)
+
         @pl.when(i < groups)
         def _():
             through(i)
@@ -1179,7 +1188,7 @@
 
         def staged(back, act):
             h = jnp.where(i < groups, i, i - gap) - back
-            early = (i >= back) & (i < AHEAD + back)
+            early = (i >= back) & (i < AHEAD + back) & (back < 2)
             pl.when(early | (i >= groups + back))(lambda: act(h))
 
         staged(2, leave)
@@ -1235,6 +1244,8 @@
         return carry
 
     lax.fori_loop(0, EARLY, drain, 0)
+    for c in to_chips(EARLY)[0::2]:
+        c.wait()
 
 
 def chip_copies(at, h, away, j, far, send, recv):
@@ -1314,8 +1325,8 @@
             dma((2,)),
             dma((2, 2, chips)),
             dma((2, 2, chips)),
-            dma((2, chips - 1, EARLY)),
-            dma((2, chips - 1, EARLY)),
+            dma((2, chips - 1, EARLY + 1)),
+            dma((2, chips - 1, EARLY + 1)),
             dma((2 * chips, 2)),
             pltpu.SemaphoreType.REGULAR,
             dma((line, 2)),
@@ -1414,7 +1425,7 @@
     dattn = dres.astype(BF16)
     rights[rows(f), split:] = dattn
     send_rights(0)
-    for c in late(EARLY):
+    for c in late(EARLY)[1::2]:
         c.start()
     dattn_f[...] = dot(dattn, full(0), 1, 1).astype(BF16)
     combine.more(nothing)
@@ -1561,7 +1572,7 @@
     for t in (combine, outer, inner, outer_all, inner_all):
         t.finish()
     for h in range(EARLY, held):
-        for c in late(h):
+        for c in late(h)[1::2] if h == EARLY else late(h):
             c.wait()
 
 

time: 315 us -> 312 us (level)
    pallas_call x1, Pallas kernels: 123 us -> 118 us  [reverse(): pl.pallas_call(functools.partial(reverse_kernel, sizes), name='reverse',...]
where the time goes in v6:
time: 312 us; the launch traced here: 311 us
  Pallas kernels  311 us (100%)
    pallas_call x1, Pallas kernels, reverse(): pl.pallas_call(functools.partial(reverse_kernel, sizes), name='reverse',...  118 us
    pallas_call x1, Pallas kernels, moe(): pl.pallas_call(functools.partial(moe_kernel, sizes), name='moe', out_shap...  117 us
    pallas_call x1, Pallas kernels, attend(): pl.pallas_call(functools.partial(attend_kernel, sizes), name='attend', ou...  63.2 us
    pallas_call x1, Pallas kernels, finish(): pl.pallas_call(functools.partial(finish_kernel, experts), name='finish',...  12.5 us

profile of v6, /device:TPU:0, one launch (start us, length us, event | category | flops | bytes accessed | tf_op | source)
XLA Modules:
  0.0 311.4 jit_solution(3211787015081190597)
XLA Ops:
  0.6 63.2 %attend.1 = (bf16[128,1536]{1,0:T(8,128)(2,1)}, bf16[128,1536]{1,0:T(8,128)(2,1)}, bf16[128,512]{1,0:T(8,128)(2,1)}, bf16[128,512]{1,0:T(8,128)(2,1)}, bf16[128,...) custom-call(bf16[128,1536]{1,0:T(8,128)(2,1)} %hidden.3, ...), custom_call_target="tpu_custom_call" | custom-call | tf_op jit(solution)/shard_map/attend/pallas_call | solution.py:920
  63.9 117.2 %moe.1 = (f32[128,1664]{1,0:T(8,128)}, bf16[8,128,1536]{2,1,0:T(8,128)(2,1)}, bf16[10,384,512]{2,1,0:T(8,128)(2,1)}, bf16[10,64,1536]{2,1,0:T(8,128)(2,1)}, bf16...) custom-call(bf16[128,1664]{1,0:T(8,128)(2,1)} %get-tuple-element.54., ...), custom_call_target="tpu_custom_call" | custom-call | tf_op jit(solution)/shard_map/moe/pallas_call | solution.py:1288
  181.1 117.6 %reverse.1 = (bf16[128,1536]{1,0:T(8,128)(2,1)}, f32[128,1536]{1,0:T(8,128)}, bf16[384,1536]{1,0:T(8,128)(2,1)}, bf16[384,1536]{1,0:T(8,128)(2,1)}, bf16[384,512...) custom-call(bf16[128,1536]{1,0:T(8,128)(2,1)} %hidden.3, ...), custom_call_target="tpu_custom_call", output_to_operand_aliasing={{7}: (24, {}), {8}: (25, {})} | custom-call | tf_op jit(solution)/shard_map/reverse/pallas_call | solution.py:1602
  298.8 12.5 %finish.1 = (f32[3840,512]{1,0:T(8,128)}, f32[640,1536]{1,0:T(8,128)}, f32[384,1536]{1,0:T(8,128)}, f32[384,512]{1,0:T(8,128)}, f32[384,512]{1,0:T(8,128)}, /*in...) custom-call(bf16[3840,512]{1,0:T(8,128)(2,1)} %bitcast.11, ...), custom_call_target="tpu_custom_call" | custom-call | tf_op jit(solution)/shard_map/finish/pallas_call | solution.py:1687

commit v7 on v6

--- a/solution.py
+++ b/solution.py
@@ -961,7 +961,7 @@
 
 
 EARLY = 4
-AHEAD = 2
+AHEAD = 3
 
 
 def moe_kernel(sizes, sent, cot, wgu, wd, back_out, comb_out, sums, far, away, *scratch):

time: 312 us -> 314 us (level)
  no operation moved by 1% of the time
where the time goes in v7:
time: 314 us
  Pallas kernels  313 us (100%)
    pallas_call x1, Pallas kernels, moe(): pl.pallas_call(functools.partial(moe_kernel, sizes), name='moe', out_shap...  119 us
    pallas_call x1, Pallas kernels, reverse(): pl.pallas_call(functools.partial(reverse_kernel, sizes), name='reverse',...  118 us
    pallas_call x1, Pallas kernels, attend(): pl.pallas_call(functools.partial(attend_kernel, sizes), name='attend', ou...  63.2 us
    pallas_call x1, Pallas kernels, finish(): pl.pallas_call(functools.partial(finish_kernel, experts), name='finish',...  12.5 us

profile of v7, /device:TPU:0, one launch (start us, length us, event | category | flops | bytes accessed | tf_op | source)
XLA Modules:
  0.0 313.6 jit_solution(18374401358044748287)
XLA Ops:
  0.6 63.2 %attend.1 = (bf16[128,1536]{1,0:T(8,128)(2,1)}, bf16[128,1536]{1,0:T(8,128)(2,1)}, bf16[128,512]{1,0:T(8,128)(2,1)}, bf16[128,512]{1,0:T(8,128)(2,1)}, bf16[128,...) custom-call(bf16[128,1536]{1,0:T(8,128)(2,1)} %hidden.3, ...), custom_call_target="tpu_custom_call" | custom-call | tf_op jit(solution)/shard_map/attend/pallas_call | solution.py:920
  63.9 119.1 %moe.1 = (f32[128,1664]{1,0:T(8,128)}, bf16[8,128,1536]{2,1,0:T(8,128)(2,1)}, bf16[10,384,512]{2,1,0:T(8,128)(2,1)}, bf16[10,64,1536]{2,1,0:T(8,128)(2,1)}, bf16...) custom-call(bf16[128,1664]{1,0:T(8,128)(2,1)} %get-tuple-element.54., ...), custom_call_target="tpu_custom_call" | custom-call | tf_op jit(solution)/shard_map/moe/pallas_call | solution.py:1288
  183.0 117.9 %reverse.1 = (bf16[128,1536]{1,0:T(8,128)(2,1)}, f32[128,1536]{1,0:T(8,128)}, bf16[384,1536]{1,0:T(8,128)(2,1)}, bf16[384,1536]{1,0:T(8,128)(2,1)}, bf16[384,512...) custom-call(bf16[128,1536]{1,0:T(8,128)(2,1)} %hidden.3, ...), custom_call_target="tpu_custom_call", output_to_operand_aliasing={{7}: (24, {}), {8}: (25, {})} | custom-call | tf_op jit(solution)/shard_map/reverse/pallas_call | solution.py:1602
  301.0 12.5 %finish.1 = (f32[3840,512]{1,0:T(8,128)}, f32[640,1536]{1,0:T(8,128)}, f32[384,1536]{1,0:T(8,128)}, f32[384,512]{1,0:T(8,128)}, f32[384,512]{1,0:T(8,128)}, /*in...) custom-call(bf16[3840,512]{1,0:T(8,128)(2,1)} %bitcast.11, ...), custom_call_target="tpu_custom_call" | custom-call | tf_op jit(solution)/shard_map/finish/pallas_call | solution.py:1687
